TPU v7x, 128 devices: a whole 4x4x4 slice. The times are simulated.
128 devices in a mesh: rx: 16 (over x, y), ry: 8 (over z, core).
Axes of the slice: x: 4, y: 4, z: 4, core: 2. Of those that a mesh axis runs over, the one named last changes fastest.
Arguments:
- rhs: float32 [16384, 128], P(('rx', 'ry')), may hold values from -6 to 6
- a_diag: bfloat16 [16384, 128, 128], P(('rx', 'ry'))
- a_pair: bfloat16 [16384, 128, 128], P(('rx', 'ry')), may hold values from -0.25 to 0.25
- a_far: bfloat16 [16384, 2, 128, 128], P(('rx', 'ry')), may hold values from -0.25 to 0.25
- approx_inv: bfloat16 [16384, 128, 128], P(('rx', 'ry'))
- prolong: bfloat16 [16384, 128, 128], P(('rx', 'ry'))
- col_index: int32 [16384, 2], P(('rx', 'ry')), may hold values from 0 to 16383, as said below
- partner: int32 [8192], P(('rx', 'ry')), may hold values from 1 to 16383, as said below
- odd_owner: int32 [8192], P(('rx', 'ry')), may hold values from 0 to 8191, as said below
Outputs:
- fine: float32 [16384, 128], P(('rx', 'ry'))
- coarse_blocks: bfloat16 [8192, 128, 128], P(('rx', 'ry'))
- coarse_residual: float32 [8192, 128], P(('rx', 'ry'))
Inputs may be any that keep to these rules, and one draw needn't show every extreme that they name: partner[c] is an odd fine row on another device with the same ry index as coarse row c's device (coarse row c stands on device c // 64, fine row i on device i // 128); every odd fine row is named once; the odd rows of each device go to exactly 8 devices, 8 rows to each. odd_owner[o] is the coarse row c with partner[c] = 2o + 1. col_index[i,0] is a block row of a device with the same ry index as row i's device; col_index[i,1] a block row of the device with the same rx index whose ry index is one more or one less, wrapping.
All inputs are finite; a program needn't handle non-finite values.
Results may differ from a plain program's by a relative error of at most 0.0065.
Values may be sent and summed in bfloat16 or wider, within the bound.
No kernel may reach another device: no remote copies, remote signals or barrier semaphores. Data moves between devices by JAX's collectives and lax.ppermute only.
A program may use at most 128 MiB of HBM per device.

v0:
```python
import functools

import jax
import jax.numpy as jnp
from jax import lax
from jax.experimental import pallas as pl
from jax.experimental.pallas import tpu as pltpu
from jax.sharding import PartitionSpec as P

OMEGA = 0.7
THETA = 0.08
B = 128
VMEM_LIMIT = 48 * 1024 * 1024
BF = jnp.bfloat16
F32 = jnp.float32

NT = (((1,), (1,)), ((), ()))
NN = (((1,), (0,)), ((), ()))
TN = (((0,), (0,)), ((), ()))


def dot(left, right, dims):
    return lax.dot_general(left, right, dims, preferred_element_type=F32)


def split(row):
    rows = lax.broadcasted_iota(jnp.int32, (8, B), 0)
    full = jnp.broadcast_to(row, (8, B))
    high = full.astype(BF).astype(F32)
    return jnp.where(rows == 0, high, jnp.where(rows == 1, full - high, 0.0)).astype(BF)


def single(row):
    rows = lax.broadcasted_iota(jnp.int32, (8, B), 0)
    return jnp.where(rows == 0, jnp.broadcast_to(row, (8, B)), 0.0).astype(BF)


def joined(product):
    return product[0:1] + product[1:2]


def params():
    return pltpu.CompilerParams(
        dimension_semantics=("arbitrary",), vmem_limit_bytes=VMEM_LIMIT
    )


def whole(shape):
    return pl.BlockSpec(shape, lambda i, *_: (0,) * len(shape))


def start_kernel(rhs, inv, out, out_low):
    for j in range(rhs.shape[0]):
        row = OMEGA * joined(dot(split(rhs[j : j + 1]), inv[j], NT))
        out[j : j + 1] = row
    out_low[...] = out[...].astype(BF)


def first_sweep(rhs, inv, group=32):
    rows = rhs.shape[0]
    return pl.pallas_call(
        start_kernel,
        out_shape=(
            jax.ShapeDtypeStruct((rows, B), F32),
            jax.ShapeDtypeStruct((rows, B), BF),
        ),
        grid=(rows // group,),
        in_specs=[
            pl.BlockSpec((group, B), lambda i: (i, 0)),
            pl.BlockSpec((group, B, B), lambda i: (i, 0, 0)),
        ],
        out_specs=(
            pl.BlockSpec((group, B), lambda i: (i, 0)),
            pl.BlockSpec((group, B), lambda i: (i, 0)),
        ),
        compiler_params=params(),
        name="first_sweep",
    )(rhs, inv)


def defect_rows(i, group, slots, rows, rhs, x, x_group, tables, low, high, diag, pair, far, tab, side, held):
    @pl.when(i == 0)
    def _():
        quarter = tables[0].shape[0]
        for k, t in enumerate(tables):
            tab[k * quarter : (k + 1) * quarter] = t[...].astype(F32)
        side[0:rows] = low[...].astype(F32)
        side[rows : 2 * rows] = high[...].astype(F32)

    for j in range(group):
        r = i * group + j
        mate = tab[pl.ds(slots[r], 1)]
        first = tab[pl.ds(slots[rows + r], 1)]
        second = side[pl.ds(slots[2 * rows + r], 1)]
        total = dot(split(x_group[j : j + 1]), diag[j], NT)
        total += dot(single(mate), pair[j], NT)
        total += dot(single(first), far[j, 0], NT)
        total += dot(single(second), far[j, 1], NT)
        held[j : j + 1] = rhs[j : j + 1] - joined(total)


def sweep_kernel(group, rows, slots, rhs, x_group, t0, t1, t2, t3, low, high, diag, pair, far, inv, out, out_low, tab, side, held):
    i = pl.program_id(0)
    defect_rows(i, group, slots, rows, rhs, None, x_group, (t0, t1, t2, t3), low, high, diag, pair, far, tab, side, held)
    for j in range(group):
        step = joined(dot(split(held[j : j + 1]), inv[j], NT))
        out[j : j + 1] = x_group[j : j + 1] + OMEGA * step
    out_low[...] = out[...].astype(BF)


def residual_kernel(group, rows, slots, sends, rhs, x_group, t0, t1, t2, t3, low, high, diag, pair, far, prol, even, packed, tab, side, held, mail):
    i = pl.program_id(0)
    defect_rows(i, group, slots, rows, rhs, None, x_group, (t0, t1, t2, t3), low, high, diag, pair, far, tab, side, held)

    @pl.when(i == 0)
    def _():
        mail[...] = jnp.zeros_like(mail)

    for j in range(group):
        value = joined(dot(split(held[j : j + 1]), prol[j], NN))
        if j % 2 == 0:
            even[j // 2 : j // 2 + 1] = value
        else:
            mail[pl.ds(sends[i * (group // 2) + j // 2], 1)] = value

    @pl.when(i == pl.num_programs(0) - 1)
    def _():
        packed[...] = mail[...].astype(BF)


def apply_specs(rows, group):
    row = pl.BlockSpec((group, B), lambda i, *_: (i, 0))
    block = pl.BlockSpec((group, B, B), lambda i, *_: (i, 0, 0))
    return [
        row,
        row,
        *[whole((4 * rows, B))] * 4,
        whole((rows, B)),
        whole((rows, B)),
        block,
        block,
        pl.BlockSpec((group, 2, B, B), lambda i, *_: (i, 0, 0, 0)),
        block,
    ]


def apply_scratch(rows, group):
    return [
        pltpu.VMEM((16 * rows, B), F32),
        pltpu.VMEM((2 * rows, B), F32),
        pltpu.VMEM((group, B), F32),
    ]


def second_sweep(slots, rhs, x, tables, low, high, diag, pair, far, inv, group=16):
    rows = rhs.shape[0]
    row = pl.BlockSpec((group, B), lambda i, *_: (i, 0))
    return pl.pallas_call(
        functools.partial(sweep_kernel, group, rows),
        out_shape=(
            jax.ShapeDtypeStruct((rows, B), F32),
            jax.ShapeDtypeStruct((rows, B), BF),
        ),
        grid_spec=pltpu.PrefetchScalarGridSpec(
            num_scalar_prefetch=1,
            grid=(rows // group,),
            in_specs=apply_specs(rows, group),
            out_specs=(row, row),
            scratch_shapes=apply_scratch(rows, group),
        ),
        compiler_params=params(),
        name="second_sweep",
    )(slots, rhs, x, *tables, low, high, diag, pair, far, inv)


def residual_pieces(slots, sends, rhs, x, tables, low, high, diag, pair, far, prol, group=16):
    rows = rhs.shape[0]
    return pl.pallas_call(
        functools.partial(residual_kernel, group, rows),
        out_shape=(
            jax.ShapeDtypeStruct((rows // 2, B), F32),
            jax.ShapeDtypeStruct((rows, B), BF),
        ),
        grid_spec=pltpu.PrefetchScalarGridSpec(
            num_scalar_prefetch=2,
            grid=(rows // group,),
            in_specs=apply_specs(rows, group),
            out_specs=(
                pl.BlockSpec((group // 2, B), lambda i, *_: (i, 0)),
                whole((rows, B)),
            ),
            scratch_shapes=apply_scratch(rows, group) + [pltpu.VMEM((rows, B), F32)],
        ),
        compiler_params=params(),
        name="residual_pieces",
    )(slots, sends, rhs, x, *tables, low, high, diag, pair, far, prol)


def odd_kernel(group, half, sends, prol, diag, pair, out, buf, sem):
    i = pl.program_id(0)

    def copy(item):
        return pltpu.make_async_copy(buf.at[item], out.at[sends[item]], sem.at[item])

    for j in range(group):
        item = i * group + j
        p = prol[j, 0]
        lower = dot(p, diag[j, 0], TN).astype(BF)
        buf[item, 0] = p
        buf[item, 1] = dot(p, pair[j, 0], TN).astype(BF)
        buf[item, 2] = dot(lower, p, NN).astype(BF)
        copy(item).start()

    @pl.when(i == pl.num_programs(0) - 1)
    def _():
        def wait(item, carry):
            copy(item).wait()
            return carry

        lax.fori_loop(0, half, wait, 0)


def odd_blocks(sends, prol, diag, pair, group=8):
    half = prol.shape[0] // 2
    odd = pl.BlockSpec((group, 1, B, B), lambda i, *_: (i, 1, 0, 0))
    return pl.pallas_call(
        functools.partial(odd_kernel, group, half),
        out_shape=jax.ShapeDtypeStruct((2 * half, 3, B, B), BF),
        grid_spec=pltpu.PrefetchScalarGridSpec(
            num_scalar_prefetch=1,
            grid=(half // group,),
            in_specs=[odd, odd, odd],
            out_specs=pl.BlockSpec(memory_space=pl.ANY),
            scratch_shapes=[
                pltpu.VMEM((half, 3, B, B), BF),
                pltpu.SemaphoreType.DMA((half,)),
            ],
        ),
        compiler_params=params(),
        name="odd_blocks",
    )(sends, *[a.reshape(half, 2, B, B) for a in (prol, diag, pair)])


def even_kernel(prol, diag, pair, out):
    for j in range(prol.shape[0]):
        p = prol[j, 0]
        out[j, 0] = dot(p, diag[j, 0], TN).astype(BF)
        out[j, 1] = dot(p, pair[j, 0], TN).astype(BF)


def even_blocks(prol, diag, pair, group=16):
    half = prol.shape[0] // 2
    even = pl.BlockSpec((group, 1, B, B), lambda i, *_: (i, 0, 0, 0))
    return pl.pallas_call(
        even_kernel,
        out_shape=jax.ShapeDtypeStruct((half, 2, B, B), BF),
        grid=(half // group,),
        in_specs=[even, even, even],
        out_specs=pl.BlockSpec((group, 2, B, B), lambda i: (i, 0, 0, 0)),
        compiler_params=params(),
        name="even_blocks",
    )(*[a.reshape(half, 2, B, B) for a in (prol, diag, pair)])


def coarse_kernel(group, half, recvs, got, mail, even, own, prol, blocks, restricted, packed, lift, buf, sem, letters, reply):
    i = pl.program_id(0)

    def copy(item):
        return pltpu.make_async_copy(got.at[recvs[item]], buf.at[item], sem.at[item])

    @pl.when(i == 0)
    def _():
        def start(item, carry):
            copy(item).start()
            return carry

        lax.fori_loop(0, half, start, 0)
        letters[...] = mail[...].astype(F32)
        reply[...] = jnp.zeros_like(reply)

    for j in range(group):
        item = i * group + j
        copy(item).wait()
    for j in range(group):
        item = i * group + j
        p = prol[j, 0]
        total = dot(own[j, 0], p, NN) + dot(own[j, 1], buf[item, 0], NN)
        total = total + dot(buf[item, 1], p, NN) + buf[item, 2].astype(F32)
        blocks[j] = total.astype(BF)
    for j in range(group):
        item = i * group + j
        slot = recvs[item]
        r = even[j : j + 1] + letters[pl.ds(slot, 1)]
        restricted[j : j + 1] = r
        c = THETA * r
        c = c + THETA * (r - joined(dot(split(c), blocks[j], NT)))
        reply[pl.ds(slot, 1)] = c
        lift[j : j + 1] = joined(dot(split(c), prol[j, 0], NT))

    @pl.when(i == pl.num_programs(0) - 1)
    def _():
        packed[...] = reply[...].astype(BF)


def coarse(recvs, got, mail, even, own, prol, group=16):
    half = even.shape[0]
    row = pl.BlockSpec((group, B), lambda i, *_: (i, 0))
    return pl.pallas_call(
        functools.partial(coarse_kernel, group, half),
        out_shape=(
            jax.ShapeDtypeStruct((half, B, B), BF),
            jax.ShapeDtypeStruct((half, B), F32),
            jax.ShapeDtypeStruct((2 * half, B), BF),
            jax.ShapeDtypeStruct((half, B), F32),
        ),
        grid_spec=pltpu.PrefetchScalarGridSpec(
            num_scalar_prefetch=1,
            grid=(half // group,),
            in_specs=[
                pl.BlockSpec(memory_space=pl.ANY),
                whole((2 * half, B)),
                row,
                pl.BlockSpec((group, 2, B, B), lambda i, *_: (i, 0, 0, 0)),
                pl.BlockSpec((group, 1, B, B), lambda i, *_: (i, 0, 0, 0)),
            ],
            out_specs=(
                pl.BlockSpec((group, B, B), lambda i, *_: (i, 0, 0)),
                row,
                whole((2 * half, B)),
                row,
            ),
            scratch_shapes=[
                pltpu.VMEM((half, 3, B, B), BF),
                pltpu.SemaphoreType.DMA((half,)),
                pltpu.VMEM((2 * half, B), F32),
                pltpu.VMEM((2 * half, B), F32),
            ],
        ),
        compiler_params=params(),
        name="coarse",
    )(recvs, got, mail, even, own, prol.reshape(half, 2, B, B))


def finish_kernel(group, sends, mail, lift, x, prol, out, letters):
    i = pl.program_id(0)

    @pl.when(i == 0)
    def _():
        letters[...] = mail[...].astype(F32)

    for j in range(group):
        e = 2 * j
        out[e : e + 1] = x[e : e + 1] + lift[j : j + 1]
        c = letters[pl.ds(sends[i * group + j], 1)]
        out[e + 1 : e + 2] = x[e + 1 : e + 2] + joined(dot(single(c), prol[j, 0], NT))


def finish(sends, mail, lift, x, prol, group=32):
    half = lift.shape[0]
    return pl.pallas_call(
        functools.partial(finish_kernel, group),
        out_shape=jax.ShapeDtypeStruct((2 * half, B), F32),
        grid_spec=pltpu.PrefetchScalarGridSpec(
            num_scalar_prefetch=1,
            grid=(half // group,),
            in_specs=[
                whole((2 * half, B)),
                pl.BlockSpec((group, B), lambda i, *_: (i, 0)),
                pl.BlockSpec((2 * group, B), lambda i, *_: (i, 0)),
                pl.BlockSpec((group, 1, B, B), lambda i, *_: (i, 1, 0, 0)),
            ],
            out_specs=pl.BlockSpec((2 * group, B), lambda i, *_: (i, 0)),
            scratch_shapes=[pltpu.VMEM((2 * half, B), F32)],
        ),
        compiler_params=params(),
        name="finish",
    )(sends, mail, lift, x, prol.reshape(half, 2, B, B))


def gather_line(block, side):
    def along_x(d):
        return [
            (x * side + y, (x + d) % side * side + y)
            for x in range(side)
            for y in range(side)
        ]

    def along_y(d):
        return [
            (x * side + y, x * side + (y + d) % side)
            for x in range(side)
            for y in range(side)
        ]

    row = [block] + [lax.ppermute(block, "rx", along_x(d)) for d in range(1, side)]
    row = jnp.concatenate(row, axis=0)
    return [row] + [lax.ppermute(row, "rx", along_y(d)) for d in range(1, side)]


def neighbours(block):
    count = lax.axis_size("ry")
    forward = [(i, (i + 1) % count) for i in range(count)]
    backward = [(target, source) for source, target in forward]
    return lax.ppermute(block, "ry", forward), lax.ppermute(block, "ry", backward)


def exchange(packed):
    line = lax.axis_size("rx")
    shape = packed.shape
    out = lax.all_to_all(
        packed.reshape((line, -1) + shape[1:]), "rx", split_axis=0, concat_axis=0, tiled=True
    )
    return out.reshape(shape)


def body(rhs, a_diag, a_pair, a_far, approx_inv, prolong, col_index, partner, odd_owner):
    rows = rhs.shape[0]
    half = rows // 2
    line_size = lax.axis_size("rx")
    side_size = lax.axis_size("ry")
    line_pos = lax.axis_index("rx")
    side_pos = lax.axis_index("ry")
    grid_side = 4
    capacity = half // (line_size // 2)
    mate = jnp.stack([partner, 2 * odd_owner], axis=1).reshape(rows)

    def line_slot(global_row):
        line = global_row // rows // side_size
        back_x = (line_pos // grid_side - line // grid_side) % grid_side
        back_y = (line_pos - line) % grid_side
        return (back_y * grid_side + back_x) * rows + global_row % rows

    side_dev = col_index[:, 1] // rows
    below = side_dev % side_size == (side_pos - 1) % side_size
    side_slot = jnp.where(below, 0, rows) + col_index[:, 1] % rows
    slots = jnp.concatenate([line_slot(mate), line_slot(col_index[:, 0]), side_slot])

    target_line = odd_owner // half // side_size
    same_target = target_line[:, None] == target_line[None, :]
    earlier = odd_owner[None, :] < odd_owner[:, None]
    sends = target_line * capacity + jnp.sum(same_target & earlier, axis=1, dtype=jnp.int32)
    source_line = partner // rows // side_size
    same_source = source_line[:, None] == source_line[None, :]
    position = jnp.arange(half, dtype=jnp.int32)
    before = position[None, :] < position[:, None]
    recvs = source_line * capacity + jnp.sum(same_source & before, axis=1, dtype=jnp.int32)

    x, x_low = first_sweep(rhs, approx_inv)
    low, high = neighbours(x_low)
    tables = gather_line(x_low, grid_side)
    leaving = odd_blocks(sends, prolong, a_diag, a_pair)
    x, x_low = second_sweep(
        slots, rhs, x, tables, low, high, a_diag, a_pair, a_far, approx_inv
    )
    low, high = neighbours(x_low)
    tables = gather_line(x_low, grid_side)
    own = even_blocks(prolong, a_diag, a_pair)
    even, mail = residual_pieces(
        slots, sends, rhs, x, tables, low, high, a_diag, a_pair, a_far, prolong
    )
    leaving, own, mail = lax.optimization_barrier((leaving, own, mail))
    got = exchange(leaving)
    mail = exchange(mail)
    blocks, restricted, reply, lift = coarse(recvs, got, mail, even, own, prolong)
    fine = finish(sends, exchange(reply), lift, x, prolong)
    return fine, blocks, restricted


def solution(mesh):
    rows = P(("rx", "ry"))
    return jax.shard_map(
        body,
        mesh=mesh,
        in_specs=(rows,) * 9,
        out_specs=(rows,) * 3,
        check_vma=False,
    )
```

profile of v0, /device:TPU:0, one launch (start us, length us, event | category | flops | bytes accessed | tf_op | source)
XLA Modules:
  0.0 331.8 jit_solution(8541367894357142791)
XLA Ops:
  0.6 2.2 copy-done.4
  3.7 2.7 first_sweep.1
  6.4 1.6 collective-permute-start
  8.0 2.7 collective-permute-start.1
  12.2 3.0 collective-permute-start.7
  15.6 1.6 collective-permute-start.3
  17.3 2.9 collective-permute-start.4
  23.1 2.4 collective-permute-done.4.t2
  25.5 2.2 copy-done.2
  27.7 14.1 %second_sweep.1 = (f32[128,128]{1,0:T(8,128)S(1)}, bf16[128,128]{1,0:T(8,128)(2,1)S(1)}) custom-call(s32[384]{0:T(512)S(1)} %pad_add_fusion.slots, f32[128,128]{1,0:T(8,128)S(1)} %copy-done.8, f32[128,128]{1,0:T(8,128)S(1)} %get-tuple-element.16.x_group, bf16[512,128]{1,0:T(8,128)(2,1)S(1)} %constant_dynamic-update-slice_fusion.t0, ...), custom_call_target="tpu_custom_call" | custom-call | tf_op jit(solution)/shard_map/second_sweep/pallas_call | solution.py:158
  42.5 2.1 collective-permute-start.9
  45.3 3.0 collective-permute-start.15
  49.6 3.0 collective-permute-start.12
  53.5 4.6 %even_blocks.1.own = bf16[64,2,128,128]{3,2,1,0:T(8,128)(2,1)S(1)} custom-call(bf16[64,2,128,128]{3,2,1,0:T(8,128)(2,1)} %bitcast.38, bf16[64,2,128,128]{3,2,1,0:T(8,128)(2,1)} %bitcast.42, bf16[64,2,128,128]{3,2,1,0:T(8,128)(2,1)} %bitcast.48), custom_call_target="tpu_custom_call" | custom-call | tf_op jit(solution)/shard_map/even_blocks/pallas_call | solution.py:254
  58.1 2.0 copy-done.5
  60.1 10.6 %odd_blocks.1 = bf16[128,3,128,128]{3,2,1,0:T(8,128)(2,1)} custom-call(s32[64]{0:T(128)S(1)} %multiply_add_fusion.1.sends, bf16[64,2,128,128]{3,2,1,0:T(8,128)(2,1)S(1)} %bitcast.40, bf16[64,2,128,128]{3,2,1,0:T(8,128)(2,1)} %bitcast.43, bf16[64,2,128,128]{3,2,1,0:T(8,128)(2,1)} %bitcast.49), custom_call_target="tpu_custom_call" | custom-call | tf_op jit(solution)/shard_map/odd_blocks/pallas_call | solution.py:226
  70.8 14.1 %residual_pieces.1 = (f32[64,128]{1,0:T(8,128)S(1)}, bf16[128,128]{1,0:T(8,128)(2,1)S(1)}) custom-call(s32[384]{0:T(512)S(1)} %pad_add_fusion.slots, s32[64]{0:T(128)S(1)} %multiply_add_fusion.1.sends, f32[128,128]{1,0:T(8,128)S(1)} %copy-done.8, f32[128,128]{1,0:T(8,128)S(1)} %get-tuple-element.18.x_group.x, ...), custom_call_target="tpu_custom_call" | custom-call | tf_op jit(solution)/shard_map/residual_pieces/pallas_call | solution.py:178
  84.9 12.1 %all_to_all.15 = bf16[16,8,128]{2,1,0:T(8,128)(2,1)S(1)} all-to-all(bf16[16,8,128]{2,1,0:T(8,128)(2,1)S(1)} %bitcast.46), channel_id=1, replica_groups=mesh['rx'=16,'ry'=8] {'rx'}, dimensions={0} | all-to-all | bytes 65536 | tf_op jit(solution)/shard_map/all_to_all | solution.py:410
  97.0 5.0 %all-to-all-start = ((bf16[16,8,3,128,128]{4,3,2,1,0:T(8,128)(2,1)}), bf16[16,8,3,128,128]{4,3,2,1,0:T(8,128)(2,1)}, u32[]{:S(2)}, u32[]{:S(2)}) async-start(bf16[16,8,3,128,128]{4,3,2,1,0:T(8,128)(2,1)} %bitcast.50), calls=%async_computation | async-start | bytes 25165824 | tf_op jit(solution)/shard_map/all_to_all | solution.py:410
  102.2 198.2 %all-to-all-done = bf16[16,8,3,128,128]{4,3,2,1,0:T(8,128)(2,1)} async-done(((bf16[16,8,3,128,128]{4,3,2,1,0:T(8,128)(2,1)}), bf16[16,8,3,128,128]{4,3,2,1,0:T(8,128)(2,1)}, u32[]{:S(2)}, u32[]{:S(2)}) %all-to-all-start) | async-done | bytes 12582944 | tf_op jit(solution)/shard_map/all_to_all | solution.py:410
  300.4 2.2 copy-done.6
  302.6 9.6 %coarse.1 = (bf16[64,128,128]{2,1,0:T(8,128)(2,1)}, f32[64,128]{1,0:T(8,128)}, bf16[128,128]{1,0:T(8,128)(2,1)S(1)}, f32[64,128]{1,0:T(8,128)S(1)}) custom-call(s32[64]{0:T(128)S(1)} %multiply_add_fusion.recvs, bf16[128,3,128,128]{3,2,1,0:T(8,128)(2,1)} %bitcast.8.got, bf16[128,128]{1,0:T(8,128)(2,1)S(1)} %bitcast.44, f32[64,128]{1,0:T(8,128)S(1)} %get-tuple-element.23.even, ...), custom_call_target="tpu_custom_call" | custom-call | tf_op jit(solution)/shard_map/coarse/pallas_call | solution.py:308
  312.2 17.0 %all_to_all.16 = bf16[16,8,128]{2,1,0:T(8,128)(2,1)S(1)} all-to-all(bf16[16,8,128]{2,1,0:T(8,128)(2,1)S(1)} %bitcast.47), channel_id=1, replica_groups=mesh['rx'=16,'ry'=8] {'rx'}, dimensions={0} | all-to-all | bytes 65536 | tf_op jit(solution)/shard_map/all_to_all | solution.py:410
  329.2 2.7 finish.1
  (63 shorter events, 9.4 us)
Async XLA Ops:
  3.7 11.5 %copy-start.9 = (s32[64]{0:T(128)S(1)}, s32[64]{0:T(128)}, u32[]{:S(2)}) copy-start(s32[64]{0:T(128)} %param.17) | copy-start | bytes 772
  3.7 11.5 %copy-start.11 = (s32[64]{0:T(128)S(1)}, s32[64]{0:T(128)}, u32[]{:S(2)}) copy-start(s32[64]{0:T(128)} %param.16) | copy-start | bytes 772
  3.7 11.8 %copy-start.10 = (s32[128,2]{0,1:T(2,128)S(1)}, s32[128,2]{0,1:T(2,128)}, u32[]{:S(2)}) copy-start(s32[128,2]{0,1:T(2,128)} %param.15) | copy-start | bytes 3076
  3.7 21.8 %copy-start.8 = (f32[128,128]{1,0:T(8,128)S(1)}, f32[128,128]{1,0:T(8,128)}, u32[]{:S(2)}) copy-start(f32[128,128]{1,0:T(8,128)} %rhs.5) | copy-start | bytes 196612
  6.4 9.2 %collective-permute-start = (bf16[128,128]{1,0:T(8,128)(2,1)S(1)}, bf16[128,128]{1,0:T(8,128)(2,1)S(1)}, u32[]{:S(2)}, u32[]{:S(2)}) collective-permute-start(bf16[128,128]{1,0:T(8,128)(2,1)S(1)} %get-tuple-element.17), channel_id=1, source_target_pairs={{0,32},{8,40},{16,48},{24,56},{32,64},{40,72},{48,80},{56,88},{64,... | collective-permute-start | bytes 98312 | tf_op jit(solution)/shard_map/ppermute | solution.py:395
  8.0 7.6 %collective-permute-start.1 = (bf16[128,128]{1,0:T(8,128)(2,1)S(1)}, bf16[128,128]{1,0:T(8,128)(2,1)S(1)}, u32[]{:S(2)}, u32[]{:S(2)}) collective-permute-start(bf16[128,128]{1,0:T(8,128)(2,1)S(1)} %get-tuple-element.17), channel_id=1, source_target_pairs={{0,64},{8,72},{16,80},{24,88},{32,96},{40,104},{48,112},{56,120},{... | collective-permute-start | bytes 98312 | tf_op jit(solution)/shard_map/ppermute | solution.py:395
  10.7 4.8 %collective-permute-start.2 = (bf16[128,128]{1,0:T(8,128)(2,1)S(1)}, bf16[128,128]{1,0:T(8,128)(2,1)S(1)}, u32[]{:S(2)}, u32[]{:S(2)}) collective-permute-start(bf16[128,128]{1,0:T(8,128)(2,1)S(1)} %get-tuple-element.17), channel_id=1, source_target_pairs={{0,96},{8,104},{16,112},{24,120},{32,0},{40,8},{48,16},{56,24},{64... | collective-permute-start | bytes 98312 | tf_op jit(solution)/shard_map/ppermute | solution.py:395
  12.2 9.5 %collective-permute-start.6 = (bf16[128,128]{1,0:T(8,128)(2,1)S(1)}, bf16[128,128]{1,0:T(8,128)(2,1)S(1)}, u32[]{:S(2)}, u32[]{:S(2)}) collective-permute-start(bf16[128,128]{1,0:T(8,128)(2,1)S(1)} %get-tuple-element.17), channel_id=1, source_target_pairs={{0,1},{1,2},{2,3},{3,4},{4,5},{5,6},{6,7},{7,0},{8,9},{9,10},{10,1... | collective-permute-start | bytes 98312 | tf_op jit(solution)/shard_map/ppermute | solution.py:404
  12.2 9.5 %collective-permute-start.7 = (bf16[128,128]{1,0:T(8,128)(2,1)S(1)}, bf16[128,128]{1,0:T(8,128)(2,1)S(1)}, u32[]{:S(2)}, u32[]{:S(2)}) collective-permute-start(bf16[128,128]{1,0:T(8,128)(2,1)S(1)} %get-tuple-element.17), channel_id=1, source_target_pairs={{1,0},{2,1},{3,2},{4,3},{5,4},{6,5},{7,6},{0,7},{9,8},{10,9},{11,1... | collective-permute-start | bytes 98312 | tf_op jit(solution)/shard_map/ppermute | solution.py:404
  15.6 7.4 %collective-permute-start.3 = (bf16[512,128]{1,0:T(8,128)(2,1)S(1)}, bf16[512,128]{1,0:T(8,128)(2,1)S(1)}, u32[]{:S(2)}, u32[]{:S(2)}) collective-permute-start(bf16[512,128]{1,0:T(8,128)(2,1)S(1)} %constant_dynamic-update-slice_fusion.t0), channel_id=1, source_target_pairs={{0,8},{8,16},{16,24},{24,0},{32,40},{40,48},{48,56},{56,32},{64,72... | collective-permute-start | bytes 393224 | tf_op jit(solution)/shard_map/ppermute | solution.py:397
  17.3 8.2 %collective-permute-start.4 = (bf16[512,128]{1,0:T(8,128)(2,1)S(1)}, bf16[512,128]{1,0:T(8,128)(2,1)S(1)}, u32[]{:S(2)}, u32[]{:S(2)}) collective-permute-start(bf16[512,128]{1,0:T(8,128)(2,1)S(1)} %constant_dynamic-update-slice_fusion.t0), channel_id=1, source_target_pairs={{0,16},{8,24},{16,0},{24,8},{32,48},{40,56},{48,32},{56,40},{64,80... | collective-permute-start | bytes 393224 | tf_op jit(solution)/shard_map/ppermute | solution.py:397
  20.2 5.3 %collective-permute-start.5 = (bf16[512,128]{1,0:T(8,128)(2,1)S(1)}, bf16[512,128]{1,0:T(8,128)(2,1)S(1)}, u32[]{:S(2)}, u32[]{:S(2)}) collective-permute-start(bf16[512,128]{1,0:T(8,128)(2,1)S(1)} %constant_dynamic-update-slice_fusion.t0), channel_id=1, source_target_pairs={{0,24},{8,0},{16,8},{24,16},{32,56},{40,32},{48,40},{56,48},{64,88... | collective-permute-start | bytes 393224 | tf_op jit(solution)/shard_map/ppermute | solution.py:397
  41.8 6.4 %collective-permute-start.8 = (bf16[128,128]{1,0:T(8,128)(2,1)S(1)}, bf16[128,128]{1,0:T(8,128)(2,1)S(1)}, u32[]{:S(2)}, u32[]{:S(2)}) collective-permute-start(bf16[128,128]{1,0:T(8,128)(2,1)S(1)} %get-tuple-element.19), channel_id=1, source_target_pairs={{0,32},{8,40},{16,48},{24,56},{32,64},{40,72},{48,80},{56,88},{64,... | collective-permute-start | bytes 98312 | tf_op jit(solution)/shard_map/ppermute | solution.py:395
  42.5 5.7 %collective-permute-start.9 = (bf16[128,128]{1,0:T(8,128)(2,1)S(1)}, bf16[128,128]{1,0:T(8,128)(2,1)S(1)}, u32[]{:S(2)}, u32[]{:S(2)}) collective-permute-start(bf16[128,128]{1,0:T(8,128)(2,1)S(1)} %get-tuple-element.19), channel_id=1, source_target_pairs={{0,64},{8,72},{16,80},{24,88},{32,96},{40,104},{48,112},{56,120},{... | collective-permute-start | bytes 98312 | tf_op jit(solution)/shard_map/ppermute | solution.py:395
  44.6 3.9 %collective-permute-start.10 = (bf16[128,128]{1,0:T(8,128)(2,1)S(1)}, bf16[128,128]{1,0:T(8,128)(2,1)S(1)}, u32[]{:S(2)}, u32[]{:S(2)}) collective-permute-start(bf16[128,128]{1,0:T(8,128)(2,1)S(1)} %get-tuple-element.19), channel_id=1, source_target_pairs={{0,96},{8,104},{16,112},{24,120},{32,0},{40,8},{48,16},{56,24},{64... | collective-permute-start | bytes 98312 | tf_op jit(solution)/shard_map/ppermute | solution.py:395
  45.3 25.5 %collective-permute-start.14 = (bf16[128,128]{1,0:T(8,128)(2,1)S(1)}, bf16[128,128]{1,0:T(8,128)(2,1)S(1)}, u32[]{:S(2)}, u32[]{:S(2)}) collective-permute-start(bf16[128,128]{1,0:T(8,128)(2,1)S(1)} %get-tuple-element.19), channel_id=1, source_target_pairs={{0,1},{1,2},{2,3},{3,4},{4,5},{5,6},{6,7},{7,0},{8,9},{9,10},{10,1... | collective-permute-start | bytes 98312 | tf_op jit(solution)/shard_map/ppermute | solution.py:404
  45.3 25.5 %collective-permute-start.15 = (bf16[128,128]{1,0:T(8,128)(2,1)S(1)}, bf16[128,128]{1,0:T(8,128)(2,1)S(1)}, u32[]{:S(2)}, u32[]{:S(2)}) collective-permute-start(bf16[128,128]{1,0:T(8,128)(2,1)S(1)} %get-tuple-element.19), channel_id=1, source_target_pairs={{1,0},{2,1},{3,2},{4,3},{5,4},{6,5},{7,6},{0,7},{9,8},{10,9},{11,1... | collective-permute-start | bytes 98312 | tf_op jit(solution)/shard_map/ppermute | solution.py:404
  48.5 22.2 %collective-permute-start.11 = (bf16[512,128]{1,0:T(8,128)(2,1)S(1)}, bf16[512,128]{1,0:T(8,128)(2,1)S(1)}, u32[]{:S(2)}, u32[]{:S(2)}) collective-permute-start(bf16[512,128]{1,0:T(8,128)(2,1)S(1)} %constant_dynamic-update-slice_fusion.4.t0), channel_id=1, source_target_pairs={{0,8},{8,16},{16,24},{24,0},{32,40},{40,48},{48,56},{56,32},{64,72... | collective-permute-start | bytes 393224 | tf_op jit(solution)/shard_map/ppermute | solution.py:397
  49.6 21.2 %collective-permute-start.12 = (bf16[512,128]{1,0:T(8,128)(2,1)S(1)}, bf16[512,128]{1,0:T(8,128)(2,1)S(1)}, u32[]{:S(2)}, u32[]{:S(2)}) collective-permute-start(bf16[512,128]{1,0:T(8,128)(2,1)S(1)} %constant_dynamic-update-slice_fusion.4.t0), channel_id=1, source_target_pairs={{0,16},{8,24},{16,0},{24,8},{32,48},{40,56},{48,32},{56,40},{64,80... | collective-permute-start | bytes 393224 | tf_op jit(solution)/shard_map/ppermute | solution.py:397
  52.6 18.2 %collective-permute-start.13 = (bf16[512,128]{1,0:T(8,128)(2,1)S(1)}, bf16[512,128]{1,0:T(8,128)(2,1)S(1)}, u32[]{:S(2)}, u32[]{:S(2)}) collective-permute-start(bf16[512,128]{1,0:T(8,128)(2,1)S(1)} %constant_dynamic-update-slice_fusion.4.t0), channel_id=1, source_target_pairs={{0,24},{8,0},{16,8},{24,16},{32,56},{40,32},{48,40},{56,48},{64,88... | collective-permute-start | bytes 393224 | tf_op jit(solution)/shard_map/ppermute | solution.py:397
  53.5 6.6 %copy-start = (bf16[128,128,128]{2,1,0:T(8,128)(2,1)S(1)}, bf16[128,128,128]{2,1,0:T(8,128)(2,1)}, u32[]{:S(2)}) copy-start(bf16[128,128,128]{2,1,0:T(8,128)(2,1)} %prol.1) | copy-start | bytes 12582916
  60.1 10.7 %copy-start.3 = (bf16[128,128,128]{2,1,0:T(8,128)(2,1)S(1)}, bf16[128,128,128]{2,1,0:T(8,128)(2,1)}, u32[]{:S(2)}) copy-start(bf16[128,128,128]{2,1,0:T(8,128)(2,1)} %diag.3) | copy-start | bytes 12582916
  97.0 203.4 %all-to-all-start = ((bf16[16,8,3,128,128]{4,3,2,1,0:T(8,128)(2,1)}), bf16[16,8,3,128,128]{4,3,2,1,0:T(8,128)(2,1)}, u32[]{:S(2)}, u32[]{:S(2)}) async-start(bf16[16,8,3,128,128]{4,3,2,1,0:T(8,128)(2,1)} %bitcast.50), calls=%async_computation | async-start | bytes 25165824 | tf_op jit(solution)/shard_map/all_to_all | solution.py:410
  302.6 26.6 %copy-start.1 = (bf16[128,128,128]{2,1,0:T(8,128)(2,1)S(1)}, bf16[128,128,128]{2,1,0:T(8,128)(2,1)}, u32[]{:S(2)}) copy-start(bf16[128,128,128]{2,1,0:T(8,128)(2,1)} %prol.1) | copy-start | bytes 12582916
  (5 other events, 9.4 us)
where the time goes:
time: 333 us; the launch traced here: 332 us
  waiting for transfers between devices  202 us (61%)
  Pallas kernels  58.4 us (18%)
  starting transfers between devices  31 us (9%)
  blocking collectives  29.1 us (9%)
  local copies, waits for them, and re-layouts  9.72 us (3%)
    all_to_all x1, waiting for transfers between devices, exchange(): lax.all_to_all(packed.reshape((line, -1) + shape[1:]), 'rx', split_axis=0...  198 us
    all_to_all x2, blocking collectives, exchange(): lax.all_to_all(packed.reshape((line, -1) + shape[1:]), 'rx', split_axis=0...  29.1 us
    pallas_call x1, Pallas kernels, second_sweep(): pl.pallas_call(functools.partial(sweep_kernel, group, rows), out_shape=(j...  14.1 us
    pallas_call x1, Pallas kernels, residual_pieces(): pl.pallas_call(functools.partial(residual_kernel, group, rows), out_shape...  14.1 us
    ppermute x6, starting transfers between devices, gather_line(): return [row] + [lax.ppermute(row, 'rx', along_y(d)) for d in range(1, side)]  10.8 us
    pallas_call x1, Pallas kernels, odd_blocks(): pl.pallas_call(functools.partial(odd_kernel, group, half), out_shape=jax....  10.6 us
    pallas_call x1, Pallas kernels, coarse(): pl.pallas_call(functools.partial(coarse_kernel, group, half), out_shape=(...  9.62 us
    unnamed x30, local copies, waits for them, and re-layouts  9.46 us
  transfers between devices with their start and end apart: 17, of which 5 were waited for; matrix products, arithmetic and copies ran while one was open for 0% of the time, Pallas kernels for 5%

commit v1 on v0

--- a/solution.py
+++ b/solution.py
@@ -458,9 +458,9 @@
     even, mail = residual_pieces(
         slots, sends, rhs, x, tables, low, high, a_diag, a_pair, a_far, prolong
     )
-    leaving, own, mail = lax.optimization_barrier((leaving, own, mail))
+    mail = exchange(mail)
+    leaving, own, mail, recvs = lax.optimization_barrier((leaving, own, mail, recvs))
     got = exchange(leaving)
-    mail = exchange(mail)
     blocks, restricted, reply, lift = coarse(recvs, got, mail, even, own, prolong)
     fine = finish(sends, exchange(reply), lift, x, prolong)
     return fine, blocks, restricted

time: 333 us -> 271 us (0.81)
  waiting for transfers between devices: 202 us -> 19.3 us
  blocking collectives: 29.1 us -> 158 us
  starting transfers between devices: 31 us -> 24.2 us
    all_to_all x1, waiting for transfers between devices: 198 us -> 0.01 us  [exchange(): lax.all_to_all(packed.reshape((line, -1) + shape[1:]), 'rx', split_axis=0...]
    all_to_all x2, blocking collectives: 29.1 us -> 158 us  [exchange(): lax.all_to_all(packed.reshape((line, -1) + shape[1:]), 'rx', split_axis=0...]
    ppermute x6, waiting for transfers between devices: 0.3 us -> 7.62 us  [gather_line(): lax.ppermute(block, 'rx', along_x(d))]
    ppermute x6, starting transfers between devices: 10.8 us -> 6.8 us  [gather_line(): return [row] + [lax.ppermute(row, 'rx', along_y(d)) for d in range(1, side)]]
    ppermute x6, waiting for transfers between devices: 3.77 us -> 7.32 us  [gather_line(): return [row] + [lax.ppermute(row, 'rx', along_y(d)) for d in range(1, side)]]
  transfers between devices with their start and end apart: 17 -> 17, of which waited for: 5 -> 8; matrix products, arithmetic and copies ran while one was open for 0% -> 0% of each run, Pallas kernels for 5% -> 6%
where the time goes in v1:
time: 271 us; the launch traced here: 270 us
  blocking collectives  158 us (58%)
  Pallas kernels  59 us (22%)
  starting transfers between devices  24.2 us (9%)
  waiting for transfers between devices  19.3 us (7%)
  local copies, waits for them, and re-layouts  7.53 us (3%)
    all_to_all x2, blocking collectives, exchange(): lax.all_to_all(packed.reshape((line, -1) + shape[1:]), 'rx', split_axis=0...  158 us
    pallas_call x1, Pallas kernels, residual_pieces(): pl.pallas_call(functools.partial(residual_kernel, group, rows), out_shape...  14.7 us
    pallas_call x1, Pallas kernels, second_sweep(): pl.pallas_call(functools.partial(sweep_kernel, group, rows), out_shape=(j...  14.4 us
    pallas_call x1, Pallas kernels, odd_blocks(): pl.pallas_call(functools.partial(odd_kernel, group, half), out_shape=jax....  10.3 us
    pallas_call x1, Pallas kernels, coarse(): pl.pallas_call(functools.partial(coarse_kernel, group, half), out_shape=(...  9.62 us
    ppermute x6, waiting for transfers between devices, gather_line(): lax.ppermute(block, 'rx', along_x(d))  7.62 us
    ppermute x6, starting transfers between devices, gather_line(): lax.ppermute(block, 'rx', along_x(d))  7.45 us
    ppermute x6, waiting for transfers between devices, gather_line(): return [row] + [lax.ppermute(row, 'rx', along_y(d)) for d in range(1, side)]  7.32 us
  transfers between devices with their start and end apart: 17, of which 8 were waited for; matrix products, arithmetic and copies ran while one was open for 0% of the time, Pallas kernels for 6%

profile of v1, /device:TPU:0, one launch (start us, length us, event | category | flops | bytes accessed | tf_op | source)
XLA Modules:
  0.0 269.9 jit_solution(12706514740445089431)
XLA Ops:
  0.6 2.2 copy-done.4
  3.7 2.7 first_sweep.1
  6.4 3.6 %collective-permute-start.7 = (bf16[128,128]{1,0:T(8,128)(2,1)S(1)}, bf16[128,128]{1,0:T(8,128)(2,1)S(1)}, u32[]{:S(2)}, u32[]{:S(2)}) collective-permute-start(bf16[128,128]{1,0:T(8,128)(2,1)S(1)} %get-tuple-element.18), channel_id=1, source_target_pairs={{1,0},{2,1},{3,2},{4,3},{5,4},{6,5},{7,6},{0,7},{9,8},{10,9},{11,1... | collective-permute-start | bytes 98312 | tf_op jit(solution)/shard_map/ppermute | solution.py:404
  9.9 2.8 %collective-permute-start.2 = (bf16[128,128]{1,0:T(8,128)(2,1)S(1)}, bf16[128,128]{1,0:T(8,128)(2,1)S(1)}, u32[]{:S(2)}, u32[]{:S(2)}) collective-permute-start(bf16[128,128]{1,0:T(8,128)(2,1)S(1)} %get-tuple-element.18), channel_id=1, source_target_pairs={{0,96},{8,104},{16,112},{24,120},{32,0},{40,8},{48,16},{56,24},{64... | collective-permute-start | bytes 98312 | tf_op jit(solution)/shard_map/ppermute | solution.py:395
  14.9 3.7 %collective-permute-done = bf16[128,128]{1,0:T(8,128)(2,1)S(1)} collective-permute-done((bf16[128,128]{1,0:T(8,128)(2,1)S(1)}, bf16[128,128]{1,0:T(8,128)(2,1)S(1)}, u32[]{:S(2)}, u32[]{:S(2)}) %collective-permute-start) | collective-permute-done | bytes 32800 | tf_op jit(solution)/shard_map/ppermute | solution.py:395
  18.7 3.1 %collective-permute-start.5 = (bf16[512,128]{1,0:T(8,128)(2,1)S(1)}, bf16[512,128]{1,0:T(8,128)(2,1)S(1)}, u32[]{:S(2)}, u32[]{:S(2)}) collective-permute-start(bf16[512,128]{1,0:T(8,128)(2,1)S(1)} %constant_dynamic-update-slice_fusion.t0), channel_id=1, source_target_pairs={{0,24},{8,0},{16,8},{24,16},{32,56},{40,32},{48,40},{56,48},{64,88... | collective-permute-start | bytes 393224 | tf_op jit(solution)/shard_map/ppermute | solution.py:397
  23.4 2.3 collective-permute-done.5.t3
  25.7 2.7 collective-permute-done.4.t2
  28.3 1.3 collective-permute-done.3.t1
  29.6 2.2 copy-done.2
  31.8 14.4 %second_sweep.1 = (f32[128,128]{1,0:T(8,128)S(1)}, bf16[128,128]{1,0:T(8,128)(2,1)S(1)}) custom-call(s32[384]{0:T(512)S(1)} %pad_add_fusion.slots, f32[128,128]{1,0:T(8,128)S(1)} %copy-done.8, f32[128,128]{1,0:T(8,128)S(1)} %get-tuple-element.17.x_group, bf16[512,128]{1,0:T(8,128)(2,1)S(1)} %constant_dynamic-update-slice_fusion.t0, ...), custom_call_target="tpu_custom_call" | custom-call | tf_op jit(solution)/shard_map/second_sweep/pallas_call | solution.py:158
  46.7 1.3 collective-permute-start.9
  49.3 3.9 %collective-permute-done.8 = bf16[128,128]{1,0:T(8,128)(2,1)S(1)} collective-permute-done((bf16[128,128]{1,0:T(8,128)(2,1)S(1)}, bf16[128,128]{1,0:T(8,128)(2,1)S(1)}, u32[]{:S(2)}, u32[]{:S(2)}) %collective-permute-start.8) | collective-permute-done | bytes 32800 | tf_op jit(solution)/shard_map/ppermute | solution.py:395
  56.3 1.4 collective-permute-done.15.high
  57.7 3.0 %collective-permute-done.14.low = bf16[128,128]{1,0:T(8,128)(2,1)S(1)} collective-permute-done((bf16[128,128]{1,0:T(8,128)(2,1)S(1)}, bf16[128,128]{1,0:T(8,128)(2,1)S(1)}, u32[]{:S(2)}, u32[]{:S(2)}) %collective-permute-start.14) | collective-permute-done | bytes 32800 | tf_op jit(solution)/shard_map/ppermute | solution.py:404
  61.8 14.7 %residual_pieces.1 = (f32[64,128]{1,0:T(8,128)S(1)}, bf16[128,128]{1,0:T(8,128)(2,1)}) custom-call(s32[384]{0:T(512)S(1)} %pad_add_fusion.slots, s32[64]{0:T(128)S(1)} %multiply_add_fusion.1.sends, f32[128,128]{1,0:T(8,128)S(1)} %copy-done.8, f32[128,128]{1,0:T(8,128)S(1)} %get-tuple-element.19.x_group.x, ...), custom_call_target="tpu_custom_call" | custom-call | tf_op jit(solution)/shard_map/residual_pieces/pallas_call | solution.py:178
  76.4 5.6 %all-to-all-start = ((bf16[16,8,128]{2,1,0:T(8,128)(2,1)}), bf16[16,8,128]{2,1,0:T(8,128)(2,1)S(1)}, u32[]{:S(2)}, u32[]{:S(2)}) async-start(bf16[16,8,128]{2,1,0:T(8,128)(2,1)} %bitcast.7), calls=%async_computation | async-start | bytes 65536 | tf_op jit(solution)/shard_map/all_to_all | solution.py:410
  82.1 4.6 %even_blocks.1.own = bf16[64,2,128,128]{3,2,1,0:T(8,128)(2,1)S(1)} custom-call(bf16[64,2,128,128]{3,2,1,0:T(8,128)(2,1)} %bitcast.38, bf16[64,2,128,128]{3,2,1,0:T(8,128)(2,1)} %bitcast.42, bf16[64,2,128,128]{3,2,1,0:T(8,128)(2,1)} %bitcast.47), custom_call_target="tpu_custom_call" | custom-call | tf_op jit(solution)/shard_map/even_blocks/pallas_call | solution.py:254
  86.7 2.0 copy-done.5
  88.7 10.3 %odd_blocks.1 = bf16[128,3,128,128]{3,2,1,0:T(8,128)(2,1)} custom-call(s32[64]{0:T(128)S(1)} %multiply_add_fusion.1.sends, bf16[64,2,128,128]{3,2,1,0:T(8,128)(2,1)S(1)} %bitcast.40, bf16[64,2,128,128]{3,2,1,0:T(8,128)(2,1)} %bitcast.43, bf16[64,2,128,128]{3,2,1,0:T(8,128)(2,1)} %bitcast.48), custom_call_target="tpu_custom_call" | custom-call | tf_op jit(solution)/shard_map/odd_blocks/pallas_call | solution.py:226
  99.1 146.9 %all_to_all.15 = bf16[16,8,3,128,128]{4,3,2,1,0:T(8,128)(2,1)} all-to-all(bf16[16,8,3,128,128]{4,3,2,1,0:T(8,128)(2,1)} %bitcast.50), channel_id=1, replica_groups=mesh['rx'=16,'ry'=8] {'rx'}, dimensions={0} | all-to-all | bytes 25165824 | tf_op jit(solution)/shard_map/all_to_all | solution.py:410
  246.0 9.6 %coarse.1 = (bf16[64,128,128]{2,1,0:T(8,128)(2,1)}, f32[64,128]{1,0:T(8,128)}, bf16[128,128]{1,0:T(8,128)(2,1)S(1)}, f32[64,128]{1,0:T(8,128)S(1)}) custom-call(s32[64]{0:T(128)S(1)} %multiply_add_fusion.recvs, bf16[128,3,128,128]{3,2,1,0:T(8,128)(2,1)} %bitcast.49, bf16[128,128]{1,0:T(8,128)(2,1)S(1)} %bitcast.44, f32[64,128]{1,0:T(8,128)S(1)} %get-tuple-element.25.even, ...), custom_call_target="tpu_custom_call" | custom-call | tf_op jit(solution)/shard_map/coarse/pallas_call | solution.py:308
  255.6 11.6 %all_to_all.16 = bf16[16,8,128]{2,1,0:T(8,128)(2,1)S(1)} all-to-all(bf16[16,8,128]{2,1,0:T(8,128)(2,1)S(1)} %bitcast.46), channel_id=1, replica_groups=mesh['rx'=16,'ry'=8] {'rx'}, dimensions={0} | all-to-all | bytes 65536 | tf_op jit(solution)/shard_map/all_to_all | solution.py:410
  267.2 2.7 finish.1
  (63 shorter events, 10.6 us)
Async XLA Ops:
  3.7 10.7 %copy-start.9 = (s32[64]{0:T(128)S(1)}, s32[64]{0:T(128)}, u32[]{:S(2)}) copy-start(s32[64]{0:T(128)} %param.17) | copy-start | bytes 772
  3.7 11.0 %copy-start.10 = (s32[128,2]{0,1:T(2,128)S(1)}, s32[128,2]{0,1:T(2,128)}, u32[]{:S(2)}) copy-start(s32[128,2]{0,1:T(2,128)} %param.15) | copy-start | bytes 3076
  3.7 11.0 %copy-start.11 = (s32[64]{0:T(128)S(1)}, s32[64]{0:T(128)}, u32[]{:S(2)}) copy-start(s32[64]{0:T(128)} %param.16) | copy-start | bytes 772
  3.7 26.0 %copy-start.8 = (f32[128,128]{1,0:T(8,128)S(1)}, f32[128,128]{1,0:T(8,128)}, u32[]{:S(2)}) copy-start(f32[128,128]{1,0:T(8,128)} %rhs.5) | copy-start | bytes 196612
  6.4 17.1 %collective-permute-start.7 = (bf16[128,128]{1,0:T(8,128)(2,1)S(1)}, bf16[128,128]{1,0:T(8,128)(2,1)S(1)}, u32[]{:S(2)}, u32[]{:S(2)}) collective-permute-start(bf16[128,128]{1,0:T(8,128)(2,1)S(1)} %get-tuple-element.18), channel_id=1, source_target_pairs={{1,0},{2,1},{3,2},{4,3},{5,4},{6,5},{7,6},{0,7},{9,8},{10,9},{11,1... | collective-permute-start | bytes 98312 | tf_op jit(solution)/shard_map/ppermute | solution.py:404
  9.9 13.5 %collective-permute-start.6 = (bf16[128,128]{1,0:T(8,128)(2,1)S(1)}, bf16[128,128]{1,0:T(8,128)(2,1)S(1)}, u32[]{:S(2)}, u32[]{:S(2)}) collective-permute-start(bf16[128,128]{1,0:T(8,128)(2,1)S(1)} %get-tuple-element.18), channel_id=1, source_target_pairs={{0,1},{1,2},{2,3},{3,4},{4,5},{5,6},{6,7},{7,0},{8,9},{9,10},{10,1... | collective-permute-start | bytes 98312 | tf_op jit(solution)/shard_map/ppermute | solution.py:404
  9.9 8.7 %collective-permute-start.2 = (bf16[128,128]{1,0:T(8,128)(2,1)S(1)}, bf16[128,128]{1,0:T(8,128)(2,1)S(1)}, u32[]{:S(2)}, u32[]{:S(2)}) collective-permute-start(bf16[128,128]{1,0:T(8,128)(2,1)S(1)} %get-tuple-element.18), channel_id=1, source_target_pairs={{0,96},{8,104},{16,112},{24,120},{32,0},{40,8},{48,16},{56,24},{64... | collective-permute-start | bytes 98312 | tf_op jit(solution)/shard_map/ppermute | solution.py:395
  12.7 5.9 %collective-permute-start.1 = (bf16[128,128]{1,0:T(8,128)(2,1)S(1)}, bf16[128,128]{1,0:T(8,128)(2,1)S(1)}, u32[]{:S(2)}, u32[]{:S(2)}) collective-permute-start(bf16[128,128]{1,0:T(8,128)(2,1)S(1)} %get-tuple-element.18), channel_id=1, source_target_pairs={{0,64},{8,72},{16,80},{24,88},{32,96},{40,104},{48,112},{56,120},{... | collective-permute-start | bytes 98312 | tf_op jit(solution)/shard_map/ppermute | solution.py:395
  13.5 5.1 %collective-permute-start = (bf16[128,128]{1,0:T(8,128)(2,1)S(1)}, bf16[128,128]{1,0:T(8,128)(2,1)S(1)}, u32[]{:S(2)}, u32[]{:S(2)}) collective-permute-start(bf16[128,128]{1,0:T(8,128)(2,1)S(1)} %get-tuple-element.18), channel_id=1, source_target_pairs={{0,32},{8,40},{16,48},{24,56},{32,64},{40,72},{48,80},{56,88},{64,... | collective-permute-start | bytes 98312 | tf_op jit(solution)/shard_map/ppermute | solution.py:395
  18.7 7.0 %collective-permute-start.5 = (bf16[512,128]{1,0:T(8,128)(2,1)S(1)}, bf16[512,128]{1,0:T(8,128)(2,1)S(1)}, u32[]{:S(2)}, u32[]{:S(2)}) collective-permute-start(bf16[512,128]{1,0:T(8,128)(2,1)S(1)} %constant_dynamic-update-slice_fusion.t0), channel_id=1, source_target_pairs={{0,24},{8,0},{16,8},{24,16},{32,56},{40,32},{48,40},{56,48},{64,88... | collective-permute-start | bytes 393224 | tf_op jit(solution)/shard_map/ppermute | solution.py:397
  21.8 6.6 %collective-permute-start.4 = (bf16[512,128]{1,0:T(8,128)(2,1)S(1)}, bf16[512,128]{1,0:T(8,128)(2,1)S(1)}, u32[]{:S(2)}, u32[]{:S(2)}) collective-permute-start(bf16[512,128]{1,0:T(8,128)(2,1)S(1)} %constant_dynamic-update-slice_fusion.t0), channel_id=1, source_target_pairs={{0,16},{8,24},{16,0},{24,8},{32,48},{40,56},{48,32},{56,40},{64,80... | collective-permute-start | bytes 393224 | tf_op jit(solution)/shard_map/ppermute | solution.py:397
  22.4 7.2 %collective-permute-start.3 = (bf16[512,128]{1,0:T(8,128)(2,1)S(1)}, bf16[512,128]{1,0:T(8,128)(2,1)S(1)}, u32[]{:S(2)}, u32[]{:S(2)}) collective-permute-start(bf16[512,128]{1,0:T(8,128)(2,1)S(1)} %constant_dynamic-update-slice_fusion.t0), channel_id=1, source_target_pairs={{0,8},{8,16},{16,24},{24,0},{32,40},{40,48},{48,56},{56,32},{64,72... | collective-permute-start | bytes 393224 | tf_op jit(solution)/shard_map/ppermute | solution.py:397
  31.8 29.9 %copy-start.3 = (bf16[128,128,128]{2,1,0:T(8,128)(2,1)S(1)}, bf16[128,128,128]{2,1,0:T(8,128)(2,1)}, u32[]{:S(2)}) copy-start(bf16[128,128,128]{2,1,0:T(8,128)(2,1)} %diag.3) | copy-start | bytes 12582916
  46.3 7.0 %collective-permute-start.10 = (bf16[128,128]{1,0:T(8,128)(2,1)S(1)}, bf16[128,128]{1,0:T(8,128)(2,1)S(1)}, u32[]{:S(2)}, u32[]{:S(2)}) collective-permute-start(bf16[128,128]{1,0:T(8,128)(2,1)S(1)} %get-tuple-element.20), channel_id=1, source_target_pairs={{0,96},{8,104},{16,112},{24,120},{32,0},{40,8},{48,16},{56,24},{64... | collective-permute-start | bytes 98312 | tf_op jit(solution)/shard_map/ppermute | solution.py:395
  46.7 6.5 %collective-permute-start.9 = (bf16[128,128]{1,0:T(8,128)(2,1)S(1)}, bf16[128,128]{1,0:T(8,128)(2,1)S(1)}, u32[]{:S(2)}, u32[]{:S(2)}) collective-permute-start(bf16[128,128]{1,0:T(8,128)(2,1)S(1)} %get-tuple-element.20), channel_id=1, source_target_pairs={{0,64},{8,72},{16,80},{24,88},{32,96},{40,104},{48,112},{56,120},{... | collective-permute-start | bytes 98312 | tf_op jit(solution)/shard_map/ppermute | solution.py:395
  48.1 5.1 %collective-permute-start.8 = (bf16[128,128]{1,0:T(8,128)(2,1)S(1)}, bf16[128,128]{1,0:T(8,128)(2,1)S(1)}, u32[]{:S(2)}, u32[]{:S(2)}) collective-permute-start(bf16[128,128]{1,0:T(8,128)(2,1)S(1)} %get-tuple-element.20), channel_id=1, source_target_pairs={{0,32},{8,40},{16,48},{24,56},{32,64},{40,72},{48,80},{56,88},{64,... | collective-permute-start | bytes 98312 | tf_op jit(solution)/shard_map/ppermute | solution.py:395
  53.3 7.4 %collective-permute-start.13 = (bf16[512,128]{1,0:T(8,128)(2,1)S(1)}, bf16[512,128]{1,0:T(8,128)(2,1)S(1)}, u32[]{:S(2)}, u32[]{:S(2)}) collective-permute-start(bf16[512,128]{1,0:T(8,128)(2,1)S(1)} %constant_dynamic-update-slice_fusion.4.t0), channel_id=1, source_target_pairs={{0,24},{8,0},{16,8},{24,16},{32,56},{40,32},{48,40},{56,48},{64,88... | collective-permute-start | bytes 393224 | tf_op jit(solution)/shard_map/ppermute | solution.py:397
  53.9 6.8 %collective-permute-start.12 = (bf16[512,128]{1,0:T(8,128)(2,1)S(1)}, bf16[512,128]{1,0:T(8,128)(2,1)S(1)}, u32[]{:S(2)}, u32[]{:S(2)}) collective-permute-start(bf16[512,128]{1,0:T(8,128)(2,1)S(1)} %constant_dynamic-update-slice_fusion.4.t0), channel_id=1, source_target_pairs={{0,16},{8,24},{16,0},{24,8},{32,48},{40,56},{48,32},{56,40},{64,80... | collective-permute-start | bytes 393224 | tf_op jit(solution)/shard_map/ppermute | solution.py:397
  54.5 7.2 %collective-permute-start.11 = (bf16[512,128]{1,0:T(8,128)(2,1)S(1)}, bf16[512,128]{1,0:T(8,128)(2,1)S(1)}, u32[]{:S(2)}, u32[]{:S(2)}) collective-permute-start(bf16[512,128]{1,0:T(8,128)(2,1)S(1)} %constant_dynamic-update-slice_fusion.4.t0), channel_id=1, source_target_pairs={{0,8},{8,16},{16,24},{24,0},{32,40},{40,48},{48,56},{56,32},{64,72... | collective-permute-start | bytes 393224 | tf_op jit(solution)/shard_map/ppermute | solution.py:397
  55.4 2.3 collective-permute-start.15
  56.1 4.6 %collective-permute-start.14 = (bf16[128,128]{1,0:T(8,128)(2,1)S(1)}, bf16[128,128]{1,0:T(8,128)(2,1)S(1)}, u32[]{:S(2)}, u32[]{:S(2)}) collective-permute-start(bf16[128,128]{1,0:T(8,128)(2,1)S(1)} %get-tuple-element.20), channel_id=1, source_target_pairs={{0,1},{1,2},{2,3},{3,4},{4,5},{5,6},{6,7},{7,0},{8,9},{9,10},{10,1... | collective-permute-start | bytes 98312 | tf_op jit(solution)/shard_map/ppermute | solution.py:404
  76.4 22.6 %all-to-all-start = ((bf16[16,8,128]{2,1,0:T(8,128)(2,1)}), bf16[16,8,128]{2,1,0:T(8,128)(2,1)S(1)}, u32[]{:S(2)}, u32[]{:S(2)}) async-start(bf16[16,8,128]{2,1,0:T(8,128)(2,1)} %bitcast.7), calls=%async_computation | async-start | bytes 65536 | tf_op jit(solution)/shard_map/all_to_all | solution.py:410
  99.1 146.9 %copy-start.6 = (bf16[64,2,128,128]{3,2,1,0:T(8,128)(2,1)S(1)}, bf16[64,2,128,128]{3,2,1,0:T(8,128)(2,1)}, u32[]{:S(2)}) copy-start(bf16[64,2,128,128]{3,2,1,0:T(8,128)(2,1)} %copy-done.5) | copy-start | bytes 12582916
  246.0 21.3 %copy-start.1 = (bf16[128,128,128]{2,1,0:T(8,128)(2,1)S(1)}, bf16[128,128,128]{2,1,0:T(8,128)(2,1)}, u32[]{:S(2)}) copy-start(bf16[128,128,128]{2,1,0:T(8,128)(2,1)} %prol.1) | copy-start | bytes 12582916
  (5 other events, 13.8 us)

commit v2 on v1

--- a/solution.py
+++ b/solution.py
@@ -9,6 +9,11 @@
 
 OMEGA = 0.7
 THETA = 0.08
+ORDER = (
+    *((1, 1), (3, 3), (1, 3), (3, 1), (1, 0), (2, 1), (0, 3), (3, 0)),
+    *((2, 3), (0, 1), (1, 2), (3, 2), (2, 2), (0, 2), (2, 0)),
+)
+WINDOW = 4
 B = 128
 VMEM_LIMIT = 48 * 1024 * 1024
 BF = jnp.bfloat16
@@ -78,12 +83,10 @@
     )(rhs, inv)
 
 
-def defect_rows(i, group, slots, rows, rhs, x, x_group, tables, low, high, diag, pair, far, tab, side, held):
+def defect_rows(i, group, slots, rows, rhs, x_group, table, low, high, diag, pair, far, tab, side, held):
     @pl.when(i == 0)
     def _():
-        quarter = tables[0].shape[0]
-        for k, t in enumerate(tables):
-            tab[k * quarter : (k + 1) * quarter] = t[...].astype(F32)
+        tab[...] = table[...].astype(F32)
         side[0:rows] = low[...].astype(F32)
         side[rows : 2 * rows] = high[...].astype(F32)
 
@@ -99,18 +102,18 @@
         held[j : j + 1] = rhs[j : j + 1] - joined(total)
 
 
-def sweep_kernel(group, rows, slots, rhs, x_group, t0, t1, t2, t3, low, high, diag, pair, far, inv, out, out_low, tab, side, held):
+def sweep_kernel(group, rows, slots, rhs, x_group, table, low, high, diag, pair, far, inv, out, out_low, tab, side, held):
     i = pl.program_id(0)
-    defect_rows(i, group, slots, rows, rhs, None, x_group, (t0, t1, t2, t3), low, high, diag, pair, far, tab, side, held)
+    defect_rows(i, group, slots, rows, rhs, x_group, table, low, high, diag, pair, far, tab, side, held)
     for j in range(group):
         step = joined(dot(split(held[j : j + 1]), inv[j], NT))
         out[j : j + 1] = x_group[j : j + 1] + OMEGA * step
     out_low[...] = out[...].astype(BF)
 
 
-def residual_kernel(group, rows, slots, sends, rhs, x_group, t0, t1, t2, t3, low, high, diag, pair, far, prol, even, packed, tab, side, held, mail):
+def residual_kernel(group, rows, slots, sends, rhs, x_group, table, low, high, diag, pair, far, prol, even, packed, tab, side, held, mail):
     i = pl.program_id(0)
-    defect_rows(i, group, slots, rows, rhs, None, x_group, (t0, t1, t2, t3), low, high, diag, pair, far, tab, side, held)
+    defect_rows(i, group, slots, rows, rhs, x_group, table, low, high, diag, pair, far, tab, side, held)
 
     @pl.when(i == 0)
     def _():
@@ -134,7 +137,7 @@
     return [
         row,
         row,
-        *[whole((4 * rows, B))] * 4,
+        whole((16 * rows, B)),
         whole((rows, B)),
         whole((rows, B)),
         block,
@@ -152,7 +155,7 @@
     ]
 
 
-def second_sweep(slots, rhs, x, tables, low, high, diag, pair, far, inv, group=16):
+def second_sweep(slots, rhs, x, table, low, high, diag, pair, far, inv, group=16):
     rows = rhs.shape[0]
     row = pl.BlockSpec((group, B), lambda i, *_: (i, 0))
     return pl.pallas_call(
@@ -170,10 +173,10 @@
         ),
         compiler_params=params(),
         name="second_sweep",
-    )(slots, rhs, x, *tables, low, high, diag, pair, far, inv)
-
-
-def residual_pieces(slots, sends, rhs, x, tables, low, high, diag, pair, far, prol, group=16):
+    )(slots, rhs, x, table, low, high, diag, pair, far, inv)
+
+
+def residual_pieces(slots, sends, rhs, x, table, low, high, diag, pair, far, prol, group=16):
     rows = rhs.shape[0]
     return pl.pallas_call(
         functools.partial(residual_kernel, group, rows),
@@ -193,59 +196,66 @@
         ),
         compiler_params=params(),
         name="residual_pieces",
-    )(slots, sends, rhs, x, *tables, low, high, diag, pair, far, prol)
-
-
-def odd_kernel(group, half, sends, prol, diag, pair, out, buf, sem):
+    )(slots, sends, rhs, x, table, low, high, diag, pair, far, prol)
+
+
+def odd_kernel(group, ranks, places, starts, prol, diag, pair, *rest):
+    outs, (both, inner, buf, sem) = rest[:-4], rest[-4:]
     i = pl.program_id(0)
-
-    def copy(item):
-        return pltpu.make_async_copy(buf.at[item], out.at[sends[item]], sem.at[item])
-
-    for j in range(group):
-        item = i * group + j
-        p = prol[j, 0]
-        lower = dot(p, diag[j, 0], TN).astype(BF)
-        buf[item, 0] = p
-        buf[item, 1] = dot(p, pair[j, 0], TN).astype(BF)
-        buf[item, 2] = dot(lower, p, NN).astype(BF)
-        copy(item).start()
+    for j in range(group):
+        right = jnp.concatenate([diag[j, 0], pair[j, 0]], axis=1)
+        both[j] = dot(prol[j, 0], right, TN).astype(BF)
+    for j in range(group):
+        inner[j] = dot(both[j, :, :B], prol[j, 0], NN).astype(BF)
+    for j in range(group):
+        place = places[i * group + j]
+        buf[place, 0] = prol[j, 0]
+        buf[place, 1] = both[j, :, B:]
+        buf[place, 2] = inner[j]
+
+    def copy(k):
+        return pltpu.make_async_copy(
+            buf.at[pl.ds(starts[k], ranks)], outs[k - 1], sem.at[k]
+        )
 
     @pl.when(i == pl.num_programs(0) - 1)
     def _():
-        def wait(item, carry):
-            copy(item).wait()
-            return carry
-
-        lax.fori_loop(0, half, wait, 0)
-
-
-def odd_blocks(sends, prol, diag, pair, group=8):
+        for step in ("start", "wait"):
+            for k in range(1, len(outs) + 1):
+
+                @pl.when(starts[k] >= 0)
+                def _():
+                    getattr(copy(k), step)()
+
+
+def odd_blocks(places, starts, ranks, prol, diag, pair, group=16):
     half = prol.shape[0] // 2
+    parts = starts.shape[0] - 1
     odd = pl.BlockSpec((group, 1, B, B), lambda i, *_: (i, 1, 0, 0))
     return pl.pallas_call(
-        functools.partial(odd_kernel, group, half),
-        out_shape=jax.ShapeDtypeStruct((2 * half, 3, B, B), BF),
+        functools.partial(odd_kernel, group, ranks),
+        out_shape=(jax.ShapeDtypeStruct((ranks, 3, B, B), BF),) * parts,
         grid_spec=pltpu.PrefetchScalarGridSpec(
-            num_scalar_prefetch=1,
+            num_scalar_prefetch=2,
             grid=(half // group,),
             in_specs=[odd, odd, odd],
-            out_specs=pl.BlockSpec(memory_space=pl.ANY),
+            out_specs=(pl.BlockSpec(memory_space=pl.ANY),) * parts,
             scratch_shapes=[
+                pltpu.VMEM((group, B, 2 * B), BF),
+                pltpu.VMEM((group, B, B), BF),
                 pltpu.VMEM((half, 3, B, B), BF),
-                pltpu.SemaphoreType.DMA((half,)),
+                pltpu.SemaphoreType.DMA((parts + 1,)),
             ],
         ),
         compiler_params=params(),
         name="odd_blocks",
-    )(sends, *[a.reshape(half, 2, B, B) for a in (prol, diag, pair)])
+    )(places, starts, *[a.reshape(half, 2, B, B) for a in (prol, diag, pair)])
 
 
 def even_kernel(prol, diag, pair, out):
     for j in range(prol.shape[0]):
-        p = prol[j, 0]
-        out[j, 0] = dot(p, diag[j, 0], TN).astype(BF)
-        out[j, 1] = dot(p, pair[j, 0], TN).astype(BF)
+        both = dot(prol[j, 0], jnp.concatenate([diag[j, 0], pair[j, 0]], axis=1), TN)
+        out[j] = both.astype(BF)
 
 
 def even_blocks(prol, diag, pair, group=16):
@@ -253,60 +263,66 @@
     even = pl.BlockSpec((group, 1, B, B), lambda i, *_: (i, 0, 0, 0))
     return pl.pallas_call(
         even_kernel,
-        out_shape=jax.ShapeDtypeStruct((half, 2, B, B), BF),
+        out_shape=jax.ShapeDtypeStruct((half, B, 2 * B), BF),
         grid=(half // group,),
         in_specs=[even, even, even],
-        out_specs=pl.BlockSpec((group, 2, B, B), lambda i: (i, 0, 0, 0)),
+        out_specs=pl.BlockSpec((group, B, 2 * B), lambda i: (i, 0, 0)),
         compiler_params=params(),
         name="even_blocks",
     )(*[a.reshape(half, 2, B, B) for a in (prol, diag, pair)])
 
 
-def coarse_kernel(group, half, recvs, got, mail, even, own, prol, blocks, restricted, packed, lift, buf, sem, letters, reply):
+def coarse_kernel(group, ranks, recvs, places, starts, mail, even, own, prol, *rest):
+    parts = rest[:-9]
+    blocks, restricted, packed, lift, buf, sem, letters, reply, held = rest[-9:]
     i = pl.program_id(0)
 
-    def copy(item):
-        return pltpu.make_async_copy(got.at[recvs[item]], buf.at[item], sem.at[item])
+    def copy(k):
+        return pltpu.make_async_copy(
+            parts[k - 1], buf.at[pl.ds(starts[k], ranks)], sem.at[k]
+        )
 
     @pl.when(i == 0)
     def _():
-        def start(item, carry):
-            copy(item).start()
-            return carry
-
-        lax.fori_loop(0, half, start, 0)
+        for step in ("start", "wait"):
+            for k in range(1, len(parts) + 1):
+
+                @pl.when(starts[k] >= 0)
+                def _():
+                    getattr(copy(k), step)()
+
         letters[...] = mail[...].astype(F32)
         reply[...] = jnp.zeros_like(reply)
 
     for j in range(group):
-        item = i * group + j
-        copy(item).wait()
-    for j in range(group):
-        item = i * group + j
+        place = places[i * group + j]
         p = prol[j, 0]
-        total = dot(own[j, 0], p, NN) + dot(own[j, 1], buf[item, 0], NN)
-        total = total + dot(buf[item, 1], p, NN) + buf[item, 2].astype(F32)
-        blocks[j] = total.astype(BF)
-    for j in range(group):
-        item = i * group + j
-        slot = recvs[item]
-        r = even[j : j + 1] + letters[pl.ds(slot, 1)]
-        restricted[j : j + 1] = r
+        left = jnp.concatenate([own[j, :, B:], buf[place, 1]], axis=1)
+        right = jnp.concatenate([buf[place, 0], p], axis=0)
+        total = dot(own[j, :, :B], p, NN) + dot(left, right, NN)
+        blocks[j] = (total + buf[place, 2].astype(F32)).astype(BF)
+    for j in range(group):
+        slot = recvs[i * group + j]
+        restricted[j : j + 1] = even[j : j + 1] + letters[pl.ds(slot, 1)]
+    for j in range(group):
+        r = restricted[j : j + 1]
         c = THETA * r
-        c = c + THETA * (r - joined(dot(split(c), blocks[j], NT)))
-        reply[pl.ds(slot, 1)] = c
-        lift[j : j + 1] = joined(dot(split(c), prol[j, 0], NT))
+        held[j : j + 1] = c + THETA * (r - joined(dot(split(c), blocks[j], NT)))
+    for j in range(group):
+        lift[j : j + 1] = joined(dot(split(held[j : j + 1]), prol[j, 0], NT))
+    for j in range(group):
+        reply[pl.ds(recvs[i * group + j], 1)] = held[j : j + 1]
 
     @pl.when(i == pl.num_programs(0) - 1)
     def _():
         packed[...] = reply[...].astype(BF)
 
 
-def coarse(recvs, got, mail, even, own, prol, group=16):
+def coarse(recvs, places, starts, ranks, parts, mail, even, own, prol, group=16):
     half = even.shape[0]
     row = pl.BlockSpec((group, B), lambda i, *_: (i, 0))
     return pl.pallas_call(
-        functools.partial(coarse_kernel, group, half),
+        functools.partial(coarse_kernel, group, ranks),
         out_shape=(
             jax.ShapeDtypeStruct((half, B, B), BF),
             jax.ShapeDtypeStruct((half, B), F32),
@@ -314,15 +330,15 @@
             jax.ShapeDtypeStruct((half, B), F32),
         ),
         grid_spec=pltpu.PrefetchScalarGridSpec(
-            num_scalar_prefetch=1,
+            num_scalar_prefetch=3,
             grid=(half // group,),
             in_specs=[
-                pl.BlockSpec(memory_space=pl.ANY),
                 whole((2 * half, B)),
                 row,
-                pl.BlockSpec((group, 2, B, B), lambda i, *_: (i, 0, 0, 0)),
+                pl.BlockSpec((group, B, 2 * B), lambda i, *_: (i, 0, 0)),
                 pl.BlockSpec((group, 1, B, B), lambda i, *_: (i, 0, 0, 0)),
-            ],
+            ]
+            + [pl.BlockSpec(memory_space=pl.ANY)] * len(parts),
             out_specs=(
                 pl.BlockSpec((group, B, B), lambda i, *_: (i, 0, 0)),
                 row,
@@ -331,14 +347,15 @@
             ),
             scratch_shapes=[
                 pltpu.VMEM((half, 3, B, B), BF),
-                pltpu.SemaphoreType.DMA((half,)),
+                pltpu.SemaphoreType.DMA((len(parts) + 1,)),
                 pltpu.VMEM((2 * half, B), F32),
                 pltpu.VMEM((2 * half, B), F32),
+                pltpu.VMEM((group, B), F32),
             ],
         ),
         compiler_params=params(),
         name="coarse",
-    )(recvs, got, mail, even, own, prol.reshape(half, 2, B, B))
+    )(recvs, places, starts, mail, even, own, prol.reshape(half, 2, B, B), *parts)
 
 
 def finish_kernel(group, sends, mail, lift, x, prol, out, letters):
@@ -377,24 +394,17 @@
     )(sends, mail, lift, x, prol.reshape(half, 2, B, B))
 
 
-def gather_line(block, side):
-    def along_x(d):
-        return [
-            (x * side + y, (x + d) % side * side + y)
-            for x in range(side)
-            for y in range(side)
-        ]
-
-    def along_y(d):
-        return [
-            (x * side + y, x * side + (y + d) % side)
-            for x in range(side)
-            for y in range(side)
-        ]
-
-    row = [block] + [lax.ppermute(block, "rx", along_x(d)) for d in range(1, side)]
-    row = jnp.concatenate(row, axis=0)
-    return [row] + [lax.ppermute(row, "rx", along_y(d)) for d in range(1, side)]
+def along(side, dx, dy):
+    return [
+        (x * side + y, (x + dx) % side * side + (y + dy) % side)
+        for x in range(side)
+        for y in range(side)
+    ]
+
+
+def gather_line(block):
+    line = lax.axis_size("rx")
+    return exchange(jnp.broadcast_to(block, (line,) + block.shape)).reshape(-1, B)
 
 
 def neighbours(block):
@@ -425,43 +435,77 @@
     mate = jnp.stack([partner, 2 * odd_owner], axis=1).reshape(rows)
 
     def line_slot(global_row):
-        line = global_row // rows // side_size
-        back_x = (line_pos // grid_side - line // grid_side) % grid_side
-        back_y = (line_pos - line) % grid_side
-        return (back_y * grid_side + back_x) * rows + global_row % rows
+        return global_row // rows // side_size * rows + global_row % rows
 
     side_dev = col_index[:, 1] // rows
     below = side_dev % side_size == (side_pos - 1) % side_size
     side_slot = jnp.where(below, 0, rows) + col_index[:, 1] % rows
     slots = jnp.concatenate([line_slot(mate), line_slot(col_index[:, 0]), side_slot])
 
+    item_ids = jnp.arange(half, dtype=jnp.int32)
+    def offset_of(line, ahead):
+        dx = ahead * (line // grid_side - line_pos // grid_side) % grid_side
+        dy = ahead * (line - line_pos) % grid_side
+        return dx * grid_side + dy
+
+    def places_of(offset, rank):
+        slot = offset * capacity + rank
+        offsets = jnp.arange(line_size, dtype=jnp.int32)[:, None]
+        places = jnp.sum(slot[None, :] < slot[:, None], axis=1, dtype=jnp.int32)
+        starts = jnp.sum(offset[None, :] < offsets, axis=1, dtype=jnp.int32)
+        used = jnp.any(offset[None, :] == offsets, axis=1)
+        return places, jnp.where(used, starts, -1)
+
     target_line = odd_owner // half // side_size
     same_target = target_line[:, None] == target_line[None, :]
     earlier = odd_owner[None, :] < odd_owner[:, None]
-    sends = target_line * capacity + jnp.sum(same_target & earlier, axis=1, dtype=jnp.int32)
+    send_rank = jnp.sum(same_target & earlier, axis=1, dtype=jnp.int32)
+    sends = target_line * capacity + send_rank
+    send_places, send_starts = places_of(offset_of(target_line, 1), send_rank)
     source_line = partner // rows // side_size
     same_source = source_line[:, None] == source_line[None, :]
-    position = jnp.arange(half, dtype=jnp.int32)
-    before = position[None, :] < position[:, None]
-    recvs = source_line * capacity + jnp.sum(same_source & before, axis=1, dtype=jnp.int32)
-
+    before = item_ids[None, :] < item_ids[:, None]
+    recv_rank = jnp.sum(same_source & before, axis=1, dtype=jnp.int32)
+    recvs = source_line * capacity + recv_rank
+    recv_places, recv_starts = places_of(offset_of(source_line, -1), recv_rank)
+
+    barrier = lax.optimization_barrier
+    leaving = list(
+        odd_blocks(send_places, send_starts, capacity, prolong, a_diag, a_pair)
+    )
+    arrived = [None] * len(leaving)
+
+    def leave(first, last, gate):
+        picked = [dx * grid_side + dy - 1 for dx, dy in ORDER[first:last]]
+        waits = [dx * grid_side + dy - 1 for dx, dy in ORDER[max(first - WINDOW, 0) : max(last - WINDOW, 0)]]
+        ins, old, gate = barrier(([leaving[k] for k in picked], [arrived[k] for k in waits], gate))
+        for k, part in zip(waits, old):
+            arrived[k] = part
+        for k, part in zip(picked, ins):
+            dx, dy = divmod(k + 1, grid_side)
+            arrived[k] = lax.ppermute(part, "rx", along(grid_side, dx, dy))
+        return gate
+
+    rhs = leave(0, 4, rhs)
     x, x_low = first_sweep(rhs, approx_inv)
     low, high = neighbours(x_low)
-    tables = gather_line(x_low, grid_side)
-    leaving = odd_blocks(sends, prolong, a_diag, a_pair)
+    table = gather_line(x_low)
+    table = leave(4, 8, table)
     x, x_low = second_sweep(
-        slots, rhs, x, tables, low, high, a_diag, a_pair, a_far, approx_inv
+        slots, rhs, x, table, low, high, a_diag, a_pair, a_far, approx_inv
     )
     low, high = neighbours(x_low)
-    tables = gather_line(x_low, grid_side)
+    table = gather_line(x_low)
+    table = leave(8, 12, table)
     own = even_blocks(prolong, a_diag, a_pair)
     even, mail = residual_pieces(
-        slots, sends, rhs, x, tables, low, high, a_diag, a_pair, a_far, prolong
-    )
+        slots, sends, rhs, x, table, low, high, a_diag, a_pair, a_far, prolong
+    )
+    mail = leave(12, 15, mail)
     mail = exchange(mail)
-    leaving, own, mail, recvs = lax.optimization_barrier((leaving, own, mail, recvs))
-    got = exchange(leaving)
-    blocks, restricted, reply, lift = coarse(recvs, got, mail, even, own, prolong)
+    blocks, restricted, reply, lift = coarse(
+        recvs, recv_places, recv_starts, capacity, arrived, mail, even, own, prolong
+    )
     fine = finish(sends, exchange(reply), lift, x, prolong)
     return fine, blocks, restricted
 

time: 271 us -> 232 us (0.86)
  blocking collectives: 158 us -> 28.4 us
  waiting for transfers between devices: 19.3 us -> 87.3 us
  starting transfers between devices: 24.2 us -> 42.4 us
  local copies, waits for them, and re-layouts: 7.53 us -> 10.7 us
    all_to_all x2, blocking collectives: 158 us -> 28.4 us  [exchange(): lax.all_to_all(packed.reshape((line, -1) + shape[1:]), 'rx', split_axis=0...]
    all_to_all x1 -> x2, waiting for transfers between devices: 0.01 us -> 44.5 us  [exchange(): lax.all_to_all(packed.reshape((line, -1) + shape[1:]), 'rx', split_axis=0...]
    ppermute x12 -> x15, waiting for transfers between devices: 14.9 us -> 34.5 us  [leave(): arrived[k] = lax.ppermute(part, 'rx', along(grid_side, dx, dy))]
    ppermute x12 -> x15, starting transfers between devices: 14.3 us -> 29.3 us  [leave(): arrived[k] = lax.ppermute(part, 'rx', along(grid_side, dx, dy))]
    ppermute x2, waiting for transfers between devices: 2.95 us -> 6.96 us  [neighbours(): lax.ppermute(block, 'ry', forward)]
    all_to_all x1 -> x2, starting transfers between devices: 5.62 us -> 8 us  [exchange(): lax.all_to_all(packed.reshape((line, -1) + shape[1:]), 'rx', split_axis=0...]
    unnamed x30 -> x46, local copies, waits for them, and re-layouts: 7.28 us -> 9.41 us
  transfers between devices with their start and end apart: 17 -> 21, of which waited for: 8 -> 6; matrix products, arithmetic and copies ran while one was open for 0% -> 1% of each run, Pallas kernels for 6% -> 16%
where the time goes in v2:
time: 232 us; the launch traced here: 230 us
  waiting for transfers between devices  87.3 us (38%)
  Pallas kernels  57.4 us (25%)
  starting transfers between devices  42.4 us (18%)
  blocking collectives  28.4 us (12%)
  local copies, waits for them, and re-layouts  10.7 us (5%)
  other arithmetic  2.71 us (1%)
    all_to_all x2, waiting for transfers between devices, exchange(): lax.all_to_all(packed.reshape((line, -1) + shape[1:]), 'rx', split_axis=0...  44.5 us
    ppermute x15, waiting for transfers between devices, leave(): arrived[k] = lax.ppermute(part, 'rx', along(grid_side, dx, dy))  34.5 us
    ppermute x15, starting transfers between devices, leave(): arrived[k] = lax.ppermute(part, 'rx', along(grid_side, dx, dy))  29.3 us
    all_to_all x2, blocking collectives, exchange(): lax.all_to_all(packed.reshape((line, -1) + shape[1:]), 'rx', split_axis=0...  28.4 us
    pallas_call x1, Pallas kernels, residual_pieces(): pl.pallas_call(functools.partial(residual_kernel, group, rows), out_shape...  14.7 us
    pallas_call x1, Pallas kernels, second_sweep(): pl.pallas_call(functools.partial(sweep_kernel, group, rows), out_shape=(j...  14.4 us
    pallas_call x1, Pallas kernels, coarse(): pl.pallas_call(functools.partial(coarse_kernel, group, ranks), out_shape=...  10.5 us
    unnamed x46, local copies, waits for them, and re-layouts  9.41 us
  transfers between devices with their start and end apart: 21, of which 6 were waited for; matrix products, arithmetic and copies ran while one was open for 1% of the time, Pallas kernels for 16%

profile of v2, /device:TPU:0, one launch (start us, length us, event | category | flops | bytes accessed | tf_op | source)
XLA Modules:
  0.0 230.0 jit_solution(5797527699188689825)
XLA Ops:
  2.7 8.3 %odd_blocks.1 = (bf16[8,3,128,128]{3,2,1,0:T(8,128)(2,1)S(1)}, bf16[8,3,128,128]{3,2,1,0:T(8,128)(2,1)}, bf16[8,3,128,128]{3,2,1,0:T(8,128)(2,1)S(1)}, bf16[8,3,...) custom-call(s32[64]{0:T(128)S(1)} %convert_reduce_fusion.places, ...), custom_call_target="tpu_custom_call" | custom-call | tf_op jit(solution)/shard_map/odd_blocks/pallas_call | solution.py:235
  11.1 2.7 %collective-permute-start = (bf16[8,3,128,128]{3,2,1,0:T(8,128)(2,1)}, bf16[8,3,128,128]{3,2,1,0:T(8,128)(2,1)S(1)}, u32[]{:S(2)}, u32[]{:S(2)}) collective-permute-start(bf16[8,3,128,128]{3,2,1,0:T(8,128)(2,1)} %get-tuple-element.73), channel_id=1, source_target_pairs={{0,40},{8,48},{16,56},{24,32},{32,72},{40,80},{48,88},{56,64},{64,... | collective-permute-start | bytes 2359304 | tf_op jit(solution)/shard_map/ppermute | solution.py:486
  13.8 2.8 %collective-permute-start.1 = (bf16[8,3,128,128]{3,2,1,0:T(8,128)(2,1)}, bf16[8,3,128,128]{3,2,1,0:T(8,128)(2,1)}, u32[]{:S(2)}, u32[]{:S(2)}) collective-permute-start(bf16[8,3,128,128]{3,2,1,0:T(8,128)(2,1)} %get-tuple-element.74), channel_id=1, source_target_pairs={{0,120},{8,96},{16,104},{24,112},{32,24},{40,0},{48,8},{56,16},{64... | collective-permute-start | bytes 2359304 | tf_op jit(solution)/shard_map/ppermute | solution.py:486
  18.1 2.6 %collective-permute-start.3 = (bf16[8,3,128,128]{3,2,1,0:T(8,128)(2,1)}, bf16[8,3,128,128]{3,2,1,0:T(8,128)(2,1)}, u32[]{:S(2)}, u32[]{:S(2)}) collective-permute-start(bf16[8,3,128,128]{3,2,1,0:T(8,128)(2,1)} %get-tuple-element.76), channel_id=1, source_target_pairs={{0,104},{8,112},{16,120},{24,96},{32,8},{40,16},{48,24},{56,0},{64... | collective-permute-start | bytes 2359304 | tf_op jit(solution)/shard_map/ppermute | solution.py:486
  20.7 2.7 %first_sweep.1 = (f32[128,128]{1,0:T(8,128)S(1)}, bf16[128,128]{1,0:T(8,128)(2,1)S(1)}) custom-call(f32[128,128]{1,0:T(8,128)S(1)} %copy-done.11, bf16[128,128,128]{2,1,0:T(8,128)(2,1)S(1)} %copy-done.3), custom_call_target="tpu_custom_call" | custom-call | tf_op jit(solution)/shard_map/first_sweep/pallas_call | solution.py:66
  24.3 4.5 %all-to-all-start = ((bf16[16,1,128,128]{3,2,1,0:T(8,128)(2,1)}), bf16[16,1,128,128]{3,2,1,0:T(8,128)(2,1)S(1)}, u32[]{:S(2)}, u32[]{:S(2)}) async-start(bf16[16,1,128,128]{3,2,1,0:T(8,128)(2,1)} %reshape.56), calls=%async_computation | async-start | bytes 1048576 | tf_op jit(solution)/shard_map/all_to_all | solution.py:420
  31.2 28.1 %all-to-all-done = bf16[16,1,128,128]{3,2,1,0:T(8,128)(2,1)S(1)} async-done(((bf16[16,1,128,128]{3,2,1,0:T(8,128)(2,1)}), bf16[16,1,128,128]{3,2,1,0:T(8,128)(2,1)S(1)}, u32[]{:S(2)}, u32[]{:S(2)}) %all-to-all-start) | async-done | bytes 524320 | tf_op jit(solution)/shard_map/all_to_all | solution.py:420
  59.5 3.2 %collective-permute-start.5 = (bf16[8,3,128,128]{3,2,1,0:T(8,128)(2,1)}, bf16[8,3,128,128]{3,2,1,0:T(8,128)(2,1)S(1)}, u32[]{:S(2)}, u32[]{:S(2)}) collective-permute-start(bf16[8,3,128,128]{3,2,1,0:T(8,128)(2,1)} %get-tuple-element.80), channel_id=1, source_target_pairs={{0,72},{8,80},{16,88},{24,64},{32,104},{40,112},{48,120},{56,96},{... | collective-permute-start | bytes 2359304 | tf_op jit(solution)/shard_map/ppermute | solution.py:486
  65.9 4.5 %collective-permute-done.8.low = bf16[128,128]{1,0:T(8,128)(2,1)S(1)} collective-permute-done((bf16[128,128]{1,0:T(8,128)(2,1)S(1)}, bf16[128,128]{1,0:T(8,128)(2,1)S(1)}, u32[]{:S(2)}, u32[]{:S(2)}) %collective-permute-start.8) | collective-permute-done | bytes 32800 | tf_op jit(solution)/shard_map/ppermute | solution.py:414
  72.6 14.4 %second_sweep.1 = (f32[128,128]{1,0:T(8,128)S(1)}, bf16[128,128]{1,0:T(8,128)(2,1)S(1)}) custom-call(s32[384]{0:T(512)S(1)} %pad_add_fusion.slots, f32[128,128]{1,0:T(8,128)S(1)} %copy-done.11, f32[128,128]{1,0:T(8,128)S(1)} %get-tuple-element.83.x_group, bf16[2048,128]{1,0:T(8,128)(2,1)S(1)} %bitcast.44, bf16[128,128]{1,0:T(8,128)(2,1)S(1)} %collective-permute-done.8.low, ...), custom_call_target="tpu_custom_call" | custom-call | tf_op jit(solution)/shard_map/second_sweep/pallas_call | solution.py:161
  87.1 16.3 %all_to_all.20 = bf16[16,1,128,128]{3,2,1,0:T(8,128)(2,1)S(1)} all-to-all(bf16[16,1,128,128]{3,2,1,0:T(8,128)(2,1)S(1)} %reshape.58), channel_id=1, replica_groups=mesh['rx'=16,'ry'=8] {'rx'}, dimensions={0} | all-to-all | bytes 1048576 | tf_op jit(solution)/shard_map/all_to_all | solution.py:420
  103.4 2.7 %collective-permute-start.10 = (bf16[8,3,128,128]{3,2,1,0:T(8,128)(2,1)}, bf16[8,3,128,128]{3,2,1,0:T(8,128)(2,1)S(1)}, u32[]{:S(2)}, u32[]{:S(2)}) collective-permute-start(bf16[8,3,128,128]{3,2,1,0:T(8,128)(2,1)} %get-tuple-element.86), channel_id=1, source_target_pairs={{0,88},{8,64},{16,72},{24,80},{32,120},{40,96},{48,104},{56,112},{... | collective-permute-start | bytes 2359304 | tf_op jit(solution)/shard_map/ppermute | solution.py:486
  106.2 3.5 %collective-permute-start.12 = (bf16[8,3,128,128]{3,2,1,0:T(8,128)(2,1)S(1)}, bf16[8,3,128,128]{3,2,1,0:T(8,128)(2,1)S(1)}, u32[]{:S(2)}, u32[]{:S(2)}) collective-permute-start(bf16[8,3,128,128]{3,2,1,0:T(8,128)(2,1)S(1)} %copy-done.13), channel_id=1, source_target_pairs={{0,48},{8,56},{16,32},{24,40},{32,80},{40,88},{48,64},{56,72},{64,... | collective-permute-start | bytes 2359304 | tf_op jit(solution)/shard_map/ppermute | solution.py:486
  109.7 3.0 %collective-permute-start.14 = (bf16[128,128]{1,0:T(8,128)(2,1)S(1)}, bf16[128,128]{1,0:T(8,128)(2,1)S(1)}, u32[]{:S(2)}, u32[]{:S(2)}) collective-permute-start(bf16[128,128]{1,0:T(8,128)(2,1)S(1)} %get-tuple-element.85), channel_id=1, source_target_pairs={{1,0},{2,1},{3,2},{4,3},{5,4},{6,5},{7,6},{0,7},{9,8},{10,9},{11,1... | collective-permute-start | bytes 98312 | tf_op jit(solution)/shard_map/ppermute | solution.py:414
  114.8 2.4 %collective-permute-done.13.low = bf16[128,128]{1,0:T(8,128)(2,1)S(1)} collective-permute-done((bf16[128,128]{1,0:T(8,128)(2,1)S(1)}, bf16[128,128]{1,0:T(8,128)(2,1)S(1)}, u32[]{:S(2)}, u32[]{:S(2)}) %collective-permute-start.13) | collective-permute-done | bytes 32800 | tf_op jit(solution)/shard_map/ppermute | solution.py:414
  117.2 14.7 %residual_pieces.1 = (f32[64,128]{1,0:T(8,128)S(1)}, bf16[128,128]{1,0:T(8,128)(2,1)}) custom-call(s32[384]{0:T(512)S(1)} %pad_add_fusion.slots, s32[64]{0:T(128)S(1)} %get-tuple-element.119.sends, f32[128,128]{1,0:T(8,128)S(1)} %copy-done.11, f32[128,128]{1,0:T(8,128)S(1)} %get-tuple-element.89.x_group.x, bf16[2048,128]{1,0:T(8,128)(2,1)S(1)} %bitcast.45, ...), custom_call_target="tpu_custom_call" | custom-call | tf_op jit(solution)/shard_map/residual_pieces/pallas_call | solution.py:181
  131.9 34.4 %collective-permute-done.11.rest_0_ = bf16[8,3,128,128]{3,2,1,0:T(8,128)(2,1)S(1)} collective-permute-done((bf16[8,3,128,128]{3,2,1,0:T(8,128)(2,1)S(1)}, bf16[8,3,128,128]{3,2,1,0:T(8,128)(2,1)S(1)}, u32[]{:S(2)}, u32[]{:S(2)}) %collective-permute-start.11) | collective-permute-done | bytes 786464 | tf_op jit(solution)/shard_map/ppermute | solution.py:486
  168.1 6.5 %collective-permute-start.17 = (bf16[8,3,128,128]{3,2,1,0:T(8,128)(2,1)}, bf16[8,3,128,128]{3,2,1,0:T(8,128)(2,1)}, u32[]{:S(2)}, u32[]{:S(2)}) collective-permute-start(bf16[8,3,128,128]{3,2,1,0:T(8,128)(2,1)} %get-tuple-element.103), channel_id=1, source_target_pairs={{0,80},{8,88},{16,64},{24,72},{32,112},{40,120},{48,96},{56,104},{... | collective-permute-start | bytes 2359304 | tf_op jit(solution)/shard_map/ppermute | solution.py:486
  174.9 3.5 %all-to-all-start.2 = ((bf16[16,8,128]{2,1,0:T(8,128)(2,1)}), bf16[16,8,128]{2,1,0:T(8,128)(2,1)S(1)}, u32[]{:S(2)}, u32[]{:S(2)}) async-start(bf16[16,8,128]{2,1,0:T(8,128)(2,1)} %bitcast.9), calls=%async_computation.2 | async-start | bytes 65536 | tf_op jit(solution)/shard_map/all_to_all | solution.py:420
  178.6 4.3 %even_blocks.1.own = bf16[64,128,256]{2,1,0:T(8,128)(2,1)S(1)} custom-call(bf16[64,2,128,128]{3,2,1,0:T(8,128)(2,1)} %bitcast.39, bf16[64,2,128,128]{3,2,1,0:T(8,128)(2,1)} %bitcast.43, bf16[64,2,128,128]{3,2,1,0:T(8,128)(2,1)} %bitcast.50), custom_call_target="tpu_custom_call" | custom-call | tf_op jit(solution)/shard_map/even_blocks/pallas_call | solution.py:264
  184.9 16.4 %all-to-all-done.2 = bf16[16,8,128]{2,1,0:T(8,128)(2,1)S(1)} async-done(((bf16[16,8,128]{2,1,0:T(8,128)(2,1)}), bf16[16,8,128]{2,1,0:T(8,128)(2,1)S(1)}, u32[]{:S(2)}, u32[]{:S(2)}) %all-to-all-start.2) | async-done | bytes 32800 | tf_op jit(solution)/shard_map/all_to_all | solution.py:420
  204.7 10.5 %coarse.1 = (bf16[64,128,128]{2,1,0:T(8,128)(2,1)}, f32[64,128]{1,0:T(8,128)}, bf16[128,128]{1,0:T(8,128)(2,1)S(1)}, f32[64,128]{1,0:T(8,128)S(1)}) custom-call(s32[64]{0:T(128)S(1)} %get-tuple-element.120.recvs, s32[64]{0:T(128)S(1)} %convert_reduce_fusion.1.places, s32[16]{0:T(128)S(1)} %broadcast_select_fusion.1.starts, bf16[128,128]{1,0:T(8,128)(2,1)S(1)} %bitcast.46, ...), custom_call_target="tpu_custom_call" | custom-call | tf_op jit(solution)/shard_map/coarse/pallas_call | solution.py:324
  215.2 12.2 %all_to_all.21 = bf16[16,8,128]{2,1,0:T(8,128)(2,1)S(1)} all-to-all(bf16[16,8,128]{2,1,0:T(8,128)(2,1)S(1)} %bitcast.48), channel_id=1, replica_groups=mesh['rx'=16,'ry'=8] {'rx'}, dimensions={0} | all-to-all | bytes 65536 | tf_op jit(solution)/shard_map/all_to_all | solution.py:420
  227.3 2.7 %finish.1 = f32[128,128]{1,0:T(8,128)} custom-call(s32[64]{0:T(128)S(1)} %get-tuple-element.119.sends, bf16[128,128]{1,0:T(8,128)(2,1)S(1)} %bitcast.47, f32[64,128]{1,0:T(8,128)S(1)} %get-tuple-element.110.lift, f32[128,128]{1,0:T(8,128)S(1)} %get-tuple-element.89.x_group.x, bf16[64,2,128,128]{3,2,1,0:T(8,128)(2,1)S(1)} %bitcast.41), custom_call_target="tpu_custom_call" | custom-call | tf_op jit(solution)/shard_map/finish/pallas_call | solution.py:377
  (95 shorter events, 22.4 us)
Async XLA Ops:
  11.1 48.2 %collective-permute-start = (bf16[8,3,128,128]{3,2,1,0:T(8,128)(2,1)}, bf16[8,3,128,128]{3,2,1,0:T(8,128)(2,1)S(1)}, u32[]{:S(2)}, u32[]{:S(2)}) collective-permute-start(bf16[8,3,128,128]{3,2,1,0:T(8,128)(2,1)} %get-tuple-element.73), channel_id=1, source_target_pairs={{0,40},{8,48},{16,56},{24,32},{32,72},{40,80},{48,88},{56,64},{64,... | collective-permute-start | bytes 2359304 | tf_op jit(solution)/shard_map/ppermute | solution.py:486
  13.8 45.5 %collective-permute-start.1 = (bf16[8,3,128,128]{3,2,1,0:T(8,128)(2,1)}, bf16[8,3,128,128]{3,2,1,0:T(8,128)(2,1)}, u32[]{:S(2)}, u32[]{:S(2)}) collective-permute-start(bf16[8,3,128,128]{3,2,1,0:T(8,128)(2,1)} %get-tuple-element.74), channel_id=1, source_target_pairs={{0,120},{8,96},{16,104},{24,112},{32,24},{40,0},{48,8},{56,16},{64... | collective-permute-start | bytes 2359304 | tf_op jit(solution)/shard_map/ppermute | solution.py:486
  16.5 42.8 %collective-permute-start.2 = (bf16[8,3,128,128]{3,2,1,0:T(8,128)(2,1)}, bf16[8,3,128,128]{3,2,1,0:T(8,128)(2,1)S(1)}, u32[]{:S(2)}, u32[]{:S(2)}) collective-permute-start(bf16[8,3,128,128]{3,2,1,0:T(8,128)(2,1)} %get-tuple-element.75), channel_id=1, source_target_pairs={{0,56},{8,32},{16,40},{24,48},{32,88},{40,64},{48,72},{56,80},{64,... | collective-permute-start | bytes 2359304 | tf_op jit(solution)/shard_map/ppermute | solution.py:486
  18.1 41.2 %collective-permute-start.3 = (bf16[8,3,128,128]{3,2,1,0:T(8,128)(2,1)}, bf16[8,3,128,128]{3,2,1,0:T(8,128)(2,1)}, u32[]{:S(2)}, u32[]{:S(2)}) collective-permute-start(bf16[8,3,128,128]{3,2,1,0:T(8,128)(2,1)} %get-tuple-element.76), channel_id=1, source_target_pairs={{0,104},{8,112},{16,120},{24,96},{32,8},{40,16},{48,24},{56,0},{64... | collective-permute-start | bytes 2359304 | tf_op jit(solution)/shard_map/ppermute | solution.py:486
  24.3 35.0 %all-to-all-start = ((bf16[16,1,128,128]{3,2,1,0:T(8,128)(2,1)}), bf16[16,1,128,128]{3,2,1,0:T(8,128)(2,1)S(1)}, u32[]{:S(2)}, u32[]{:S(2)}) async-start(bf16[16,1,128,128]{3,2,1,0:T(8,128)(2,1)} %reshape.56), calls=%async_computation | async-start | bytes 1048576 | tf_op jit(solution)/shard_map/all_to_all | solution.py:420
  28.8 37.0 %collective-permute-start.9 = (bf16[128,128]{1,0:T(8,128)(2,1)S(1)}, bf16[128,128]{1,0:T(8,128)(2,1)S(1)}, u32[]{:S(2)}, u32[]{:S(2)}) collective-permute-start(bf16[128,128]{1,0:T(8,128)(2,1)S(1)} %get-tuple-element.78), channel_id=1, source_target_pairs={{1,0},{2,1},{3,2},{4,3},{5,4},{6,5},{7,6},{0,7},{9,8},{10,9},{11,1... | collective-permute-start | bytes 98312 | tf_op jit(solution)/shard_map/ppermute | solution.py:414
  59.3 44.1 %collective-permute-start.4 = (bf16[8,3,128,128]{3,2,1,0:T(8,128)(2,1)}, bf16[8,3,128,128]{3,2,1,0:T(8,128)(2,1)S(1)}, u32[]{:S(2)}, u32[]{:S(2)}) collective-permute-start(bf16[8,3,128,128]{3,2,1,0:T(8,128)(2,1)} %copy-done.17), channel_id=1, source_target_pairs={{0,32},{8,40},{16,48},{24,56},{32,64},{40,72},{48,80},{56,88},{64,... | collective-permute-start | bytes 2359304 | tf_op jit(solution)/shard_map/ppermute | solution.py:486
  59.5 43.9 %collective-permute-start.5 = (bf16[8,3,128,128]{3,2,1,0:T(8,128)(2,1)}, bf16[8,3,128,128]{3,2,1,0:T(8,128)(2,1)S(1)}, u32[]{:S(2)}, u32[]{:S(2)}) collective-permute-start(bf16[8,3,128,128]{3,2,1,0:T(8,128)(2,1)} %get-tuple-element.80), channel_id=1, source_target_pairs={{0,72},{8,80},{16,88},{24,64},{32,104},{40,112},{48,120},{56,96},{... | collective-permute-start | bytes 2359304 | tf_op jit(solution)/shard_map/ppermute | solution.py:486
  62.7 40.7 %collective-permute-start.6 = (bf16[8,3,128,128]{3,2,1,0:T(8,128)(2,1)}, bf16[8,3,128,128]{3,2,1,0:T(8,128)(2,1)S(1)}, u32[]{:S(2)}, u32[]{:S(2)}) collective-permute-start(bf16[8,3,128,128]{3,2,1,0:T(8,128)(2,1)} %copy-done.16), channel_id=1, source_target_pairs={{0,24},{8,0},{16,8},{24,16},{32,56},{40,32},{48,40},{56,48},{64,88... | collective-permute-start | bytes 2359304 | tf_op jit(solution)/shard_map/ppermute | solution.py:486
  65.1 38.4 %collective-permute-start.7 = (bf16[8,3,128,128]{3,2,1,0:T(8,128)(2,1)}, bf16[8,3,128,128]{3,2,1,0:T(8,128)(2,1)S(1)}, u32[]{:S(2)}, u32[]{:S(2)}) collective-permute-start(bf16[8,3,128,128]{3,2,1,0:T(8,128)(2,1)} %get-tuple-element.82), channel_id=1, source_target_pairs={{0,96},{8,104},{16,112},{24,120},{32,0},{40,8},{48,16},{56,24},{64... | collective-permute-start | bytes 2359304 | tf_op jit(solution)/shard_map/ppermute | solution.py:486
  65.8 4.6 %collective-permute-start.8 = (bf16[128,128]{1,0:T(8,128)(2,1)S(1)}, bf16[128,128]{1,0:T(8,128)(2,1)S(1)}, u32[]{:S(2)}, u32[]{:S(2)}) collective-permute-start(bf16[128,128]{1,0:T(8,128)(2,1)S(1)} %get-tuple-element.78), channel_id=1, source_target_pairs={{0,1},{1,2},{2,3},{3,4},{4,5},{5,6},{6,7},{7,0},{8,9},{9,10},{10,1... | collective-permute-start | bytes 98312 | tf_op jit(solution)/shard_map/ppermute | solution.py:414
  72.6 33.6 %copy-start.13 = (bf16[8,3,128,128]{3,2,1,0:T(8,128)(2,1)S(1)}, bf16[8,3,128,128]{3,2,1,0:T(8,128)(2,1)}, u32[]{:S(2)}) copy-start(bf16[8,3,128,128]{3,2,1,0:T(8,128)(2,1)} %copy-done.12) | copy-start | bytes 2359300
  72.6 44.6 %copy-start.2 = (bf16[128,128,128]{2,1,0:T(8,128)(2,1)S(1)}, bf16[128,128,128]{2,1,0:T(8,128)(2,1)}, u32[]{:S(2)}) copy-start(bf16[128,128,128]{2,1,0:T(8,128)(2,1)} %diag.3) | copy-start | bytes 12582916
  103.4 28.4 %collective-permute-start.10 = (bf16[8,3,128,128]{3,2,1,0:T(8,128)(2,1)}, bf16[8,3,128,128]{3,2,1,0:T(8,128)(2,1)S(1)}, u32[]{:S(2)}, u32[]{:S(2)}) collective-permute-start(bf16[8,3,128,128]{3,2,1,0:T(8,128)(2,1)} %get-tuple-element.86), channel_id=1, source_target_pairs={{0,88},{8,64},{16,72},{24,80},{32,120},{40,96},{48,104},{56,112},{... | collective-permute-start | bytes 2359304 | tf_op jit(solution)/shard_map/ppermute | solution.py:486
  106.1 60.2 %collective-permute-start.11 = (bf16[8,3,128,128]{3,2,1,0:T(8,128)(2,1)S(1)}, bf16[8,3,128,128]{3,2,1,0:T(8,128)(2,1)S(1)}, u32[]{:S(2)}, u32[]{:S(2)}) collective-permute-start(bf16[8,3,128,128]{3,2,1,0:T(8,128)(2,1)S(1)} %copy-done.15), channel_id=1, source_target_pairs={{0,8},{8,16},{16,24},{24,0},{32,40},{40,48},{48,56},{56,32},{64,72... | collective-permute-start | bytes 2359304 | tf_op jit(solution)/shard_map/ppermute | solution.py:486
  106.2 61.1 %collective-permute-start.12 = (bf16[8,3,128,128]{3,2,1,0:T(8,128)(2,1)S(1)}, bf16[8,3,128,128]{3,2,1,0:T(8,128)(2,1)S(1)}, u32[]{:S(2)}, u32[]{:S(2)}) collective-permute-start(bf16[8,3,128,128]{3,2,1,0:T(8,128)(2,1)S(1)} %copy-done.13), channel_id=1, source_target_pairs={{0,48},{8,56},{16,32},{24,40},{32,80},{40,88},{48,64},{56,72},{64,... | collective-permute-start | bytes 2359304 | tf_op jit(solution)/shard_map/ppermute | solution.py:486
  109.7 4.6 %collective-permute-start.14 = (bf16[128,128]{1,0:T(8,128)(2,1)S(1)}, bf16[128,128]{1,0:T(8,128)(2,1)S(1)}, u32[]{:S(2)}, u32[]{:S(2)}) collective-permute-start(bf16[128,128]{1,0:T(8,128)(2,1)S(1)} %get-tuple-element.85), channel_id=1, source_target_pairs={{1,0},{2,1},{3,2},{4,3},{5,4},{6,5},{7,6},{0,7},{9,8},{10,9},{11,1... | collective-permute-start | bytes 98312 | tf_op jit(solution)/shard_map/ppermute | solution.py:414
  112.7 4.6 %collective-permute-start.13 = (bf16[128,128]{1,0:T(8,128)(2,1)S(1)}, bf16[128,128]{1,0:T(8,128)(2,1)S(1)}, u32[]{:S(2)}, u32[]{:S(2)}) collective-permute-start(bf16[128,128]{1,0:T(8,128)(2,1)S(1)} %get-tuple-element.85), channel_id=1, source_target_pairs={{0,1},{1,2},{2,3},{3,4},{4,5},{5,6},{6,7},{7,0},{8,9},{9,10},{10,1... | collective-permute-start | bytes 98312 | tf_op jit(solution)/shard_map/ppermute | solution.py:414
  114.3 70.6 %collective-permute-start.18 = (bf16[8,3,128,128]{3,2,1,0:T(8,128)(2,1)}, bf16[8,3,128,128]{3,2,1,0:T(8,128)(2,1)}, u32[]{:S(2)}, u32[]{:S(2)}) collective-permute-start(bf16[8,3,128,128]{3,2,1,0:T(8,128)(2,1)} %get-tuple-element.107), channel_id=1, source_target_pairs={{0,112},{8,120},{16,96},{24,104},{32,16},{40,24},{48,0},{56,8},{64... | collective-permute-start | bytes 2359304 | tf_op jit(solution)/shard_map/ppermute | solution.py:486
  131.9 69.4 %copy-start.20 = (bf16[8,3,128,128]{3,2,1,0:T(8,128)(2,1)}, bf16[8,3,128,128]{3,2,1,0:T(8,128)(2,1)S(1)}, u32[]{:S(2)}) copy-start(bf16[8,3,128,128]{3,2,1,0:T(8,128)(2,1)S(1)} %collective-permute-done.10.rest_10_) | copy-start | bytes 2359300
  168.1 33.1 %collective-permute-start.15 = (bf16[8,3,128,128]{3,2,1,0:T(8,128)(2,1)}, bf16[8,3,128,128]{3,2,1,0:T(8,128)(2,1)}, u32[]{:S(2)}, u32[]{:S(2)}) collective-permute-start(bf16[8,3,128,128]{3,2,1,0:T(8,128)(2,1)} %get-tuple-element.95), channel_id=1, source_target_pairs={{0,16},{8,24},{16,0},{24,8},{32,48},{40,56},{48,32},{56,40},{64,80... | collective-permute-start | bytes 2359304 | tf_op jit(solution)/shard_map/ppermute | solution.py:486
  168.1 33.1 %collective-permute-start.16 = (bf16[8,3,128,128]{3,2,1,0:T(8,128)(2,1)}, bf16[8,3,128,128]{3,2,1,0:T(8,128)(2,1)}, u32[]{:S(2)}, u32[]{:S(2)}) collective-permute-start(bf16[8,3,128,128]{3,2,1,0:T(8,128)(2,1)} %get-tuple-element.101), channel_id=1, source_target_pairs={{0,64},{8,72},{16,80},{24,88},{32,96},{40,104},{48,112},{56,120},{... | collective-permute-start | bytes 2359304 | tf_op jit(solution)/shard_map/ppermute | solution.py:486
  168.1 33.1 %collective-permute-start.17 = (bf16[8,3,128,128]{3,2,1,0:T(8,128)(2,1)}, bf16[8,3,128,128]{3,2,1,0:T(8,128)(2,1)}, u32[]{:S(2)}, u32[]{:S(2)}) collective-permute-start(bf16[8,3,128,128]{3,2,1,0:T(8,128)(2,1)} %get-tuple-element.103), channel_id=1, source_target_pairs={{0,80},{8,88},{16,64},{24,72},{32,112},{40,120},{48,96},{56,104},{... | collective-permute-start | bytes 2359304 | tf_op jit(solution)/shard_map/ppermute | solution.py:486
  174.9 26.3 %all-to-all-start.2 = ((bf16[16,8,128]{2,1,0:T(8,128)(2,1)}), bf16[16,8,128]{2,1,0:T(8,128)(2,1)S(1)}, u32[]{:S(2)}, u32[]{:S(2)}) async-start(bf16[16,8,128]{2,1,0:T(8,128)(2,1)} %bitcast.9), calls=%async_computation.2 | async-start | bytes 65536 | tf_op jit(solution)/shard_map/all_to_all | solution.py:420
  (20 other events, 276.3 us)

commit v3 on v2

--- a/solution.py
+++ b/solution.py
@@ -10,8 +10,10 @@
 OMEGA = 0.7
 THETA = 0.08
 ORDER = (
-    *((1, 1), (3, 3), (1, 3), (3, 1), (1, 0), (2, 1), (0, 3), (3, 0)),
-    *((2, 3), (0, 1), (1, 2), (3, 2), (2, 2), (0, 2), (2, 0)),
+    *((1, 1), (3, 3), (1, 3), (3, 1)),
+    *((2, 1), (2, 3), (0, 1), (0, 3)),
+    *((1, 2), (3, 2), (1, 0), (3, 0)),
+    *((2, 2), (2, 0), (0, 2)),
 )
 WINDOW = 4
 B = 128
@@ -215,13 +217,13 @@
 
     def copy(k):
         return pltpu.make_async_copy(
-            buf.at[pl.ds(starts[k], ranks)], outs[k - 1], sem.at[k]
+            buf.at[pl.ds(starts[k], ranks)], outs[k], sem.at[k]
         )
 
     @pl.when(i == pl.num_programs(0) - 1)
     def _():
         for step in ("start", "wait"):
-            for k in range(1, len(outs) + 1):
+            for k in range(len(outs)):
 
                 @pl.when(starts[k] >= 0)
                 def _():
@@ -230,7 +232,7 @@
 
 def odd_blocks(places, starts, ranks, prol, diag, pair, group=16):
     half = prol.shape[0] // 2
-    parts = starts.shape[0] - 1
+    parts = starts.shape[0]
     odd = pl.BlockSpec((group, 1, B, B), lambda i, *_: (i, 1, 0, 0))
     return pl.pallas_call(
         functools.partial(odd_kernel, group, ranks),
@@ -244,7 +246,7 @@
                 pltpu.VMEM((group, B, 2 * B), BF),
                 pltpu.VMEM((group, B, B), BF),
                 pltpu.VMEM((half, 3, B, B), BF),
-                pltpu.SemaphoreType.DMA((parts + 1,)),
+                pltpu.SemaphoreType.DMA((parts,)),
             ],
         ),
         compiler_params=params(),
@@ -252,77 +254,196 @@
     )(places, starts, *[a.reshape(half, 2, B, B) for a in (prol, diag, pair)])
 
 
-def even_kernel(prol, diag, pair, out):
-    for j in range(prol.shape[0]):
-        both = dot(prol[j, 0], jnp.concatenate([diag[j, 0], pair[j, 0]], axis=1), TN)
-        out[j] = both.astype(BF)
-
-
-def even_blocks(prol, diag, pair, group=16):
+def even_kernel(group, places, prol, diag, pair, out, both):
+    i = pl.program_id(0)
+    for j in range(group):
+        right = jnp.concatenate([diag[j, 0], pair[j, 0]], axis=1)
+        both[j] = dot(prol[j, 0], right, TN).astype(BF)
+    for j in range(group):
+        place = places[i * group + j]
+        out[place, :, : 2 * B] = both[j]
+        out[place, :, 2 * B :] = prol[j, 0]
+
+
+def even_blocks(places, prol, diag, pair, group=16):
     half = prol.shape[0] // 2
     even = pl.BlockSpec((group, 1, B, B), lambda i, *_: (i, 0, 0, 0))
     return pl.pallas_call(
-        even_kernel,
-        out_shape=jax.ShapeDtypeStruct((half, B, 2 * B), BF),
-        grid=(half // group,),
-        in_specs=[even, even, even],
-        out_specs=pl.BlockSpec((group, B, 2 * B), lambda i: (i, 0, 0)),
+        functools.partial(even_kernel, group),
+        out_shape=jax.ShapeDtypeStruct((half, B, 3 * B), BF),
+        grid_spec=pltpu.PrefetchScalarGridSpec(
+            num_scalar_prefetch=1,
+            grid=(half // group,),
+            in_specs=[even, even, even],
+            out_specs=whole((half, B, 3 * B)),
+            scratch_shapes=[pltpu.VMEM((group, B, 2 * B), BF)],
+        ),
         compiler_params=params(),
         name="even_blocks",
-    )(*[a.reshape(half, 2, B, B) for a in (prol, diag, pair)])
-
-
-def coarse_kernel(group, ranks, recvs, places, starts, mail, even, own, prol, *rest):
-    parts = rest[:-9]
-    blocks, restricted, packed, lift, buf, sem, letters, reply, held = rest[-9:]
+    )(places, *[a.reshape(half, 2, B, B) for a in (prol, diag, pair)])
+
+
+def coarse_rows(i, first, ranks, items, recvs, even, own, buf, blk, sem, letters, blocks, restricted, reply, lift, held, last):
+    def copy(at):
+        return pltpu.make_async_copy(blk.at[at], blocks.at[items[first + at]], sem.at[at])
+
+    base = i * ranks
+    for j in range(ranks):
+        p = own[j, :, 2 * B :]
+        left = jnp.concatenate([own[j, :, B : 2 * B], buf[base + j, 1]], axis=1)
+        right = jnp.concatenate([buf[base + j, 0], p], axis=0)
+        total = dot(own[j, :, :B], p, NN) + dot(left, right, NN)
+        blk[base + j] = (total + buf[base + j, 2].astype(F32)).astype(BF)
+    for j in range(ranks):
+        copy(base + j).start()
+    for j in range(ranks):
+        item = items[first + base + j]
+        r = even[pl.ds(item, 1)] + letters[pl.ds(recvs[item], 1)]
+        held[j : j + 1] = r
+    for j in range(ranks):
+        r = held[j : j + 1]
+        c = THETA * r
+        c = c + THETA * (r - joined(dot(split(c), blk[base + j], NT)))
+        held[ranks + j : ranks + j + 1] = c
+    for j in range(ranks):
+        c = held[ranks + j : ranks + j + 1]
+        held[2 * ranks + j : 2 * ranks + j + 1] = joined(dot(split(c), own[j, :, 2 * B :], NT))
+    for j in range(ranks):
+        item = items[first + base + j]
+        restricted[pl.ds(item, 1)] = held[j : j + 1]
+        reply[pl.ds(recvs[item], 1)] = held[ranks + j : ranks + j + 1]
+        lift[pl.ds(item, 1)] = held[2 * ranks + j : 2 * ranks + j + 1]
+
+    @pl.when(last)
+    def _():
+        for at in range(blk.shape[0]):
+            copy(at).wait()
+
+
+def early_kernel(ranks, early, items, recvs, starts, mail, even, own, *rest):
+    parts = rest[:-11]
+    blocks, rest_out, restricted, reply, lift, buf, blk, sem, part_sem, letters, held = rest[-11:]
     i = pl.program_id(0)
 
-    def copy(k):
+    def near(k):
         return pltpu.make_async_copy(
-            parts[k - 1], buf.at[pl.ds(starts[k], ranks)], sem.at[k]
+            parts[k], buf.at[pl.ds(starts[k], ranks)], part_sem.at[k]
         )
 
+    later = pltpu.make_async_copy(
+        buf.at[pl.ds(early, buf.shape[0] - early)], rest_out, part_sem.at[len(parts)]
+    )
+
     @pl.when(i == 0)
     def _():
         for step in ("start", "wait"):
-            for k in range(1, len(parts) + 1):
+            for k in range(len(parts)):
 
                 @pl.when(starts[k] >= 0)
                 def _():
-                    getattr(copy(k), step)()
-
+                    getattr(near(k), step)()
+
+        later.start()
         letters[...] = mail[...].astype(F32)
         reply[...] = jnp.zeros_like(reply)
-
-    for j in range(group):
-        place = places[i * group + j]
-        p = prol[j, 0]
-        left = jnp.concatenate([own[j, :, B:], buf[place, 1]], axis=1)
-        right = jnp.concatenate([buf[place, 0], p], axis=0)
-        total = dot(own[j, :, :B], p, NN) + dot(left, right, NN)
-        blocks[j] = (total + buf[place, 2].astype(F32)).astype(BF)
-    for j in range(group):
-        slot = recvs[i * group + j]
-        restricted[j : j + 1] = even[j : j + 1] + letters[pl.ds(slot, 1)]
-    for j in range(group):
-        r = restricted[j : j + 1]
-        c = THETA * r
-        held[j : j + 1] = c + THETA * (r - joined(dot(split(c), blocks[j], NT)))
-    for j in range(group):
-        lift[j : j + 1] = joined(dot(split(held[j : j + 1]), prol[j, 0], NT))
-    for j in range(group):
-        reply[pl.ds(recvs[i * group + j], 1)] = held[j : j + 1]
-
-    @pl.when(i == pl.num_programs(0) - 1)
+        restricted[...] = jnp.zeros_like(restricted)
+        lift[...] = jnp.zeros_like(lift)
+
+    last = i == pl.num_programs(0) - 1
+
+    @pl.when(last)
+    def _():
+        later.wait()
+
+    coarse_rows(i, 0, ranks, items, recvs, even, own, buf, blk, sem, letters, blocks, restricted, reply, lift, held, last)
+
+
+def late_kernel(ranks, early, seen, items, recvs, starts, mail, even, own, before_r, before_y, before_l, blocks_in, rest_in, *rest):
+    parts = rest[:-10]
+    blocks, restricted, packed, lift, buf, blk, sem, part_sem, letters, held_all = rest[-10:]
+    reply, held = held_all.at[pl.ds(0, letters.shape[0])], held_all.at[pl.ds(letters.shape[0], 4 * ranks)]
+    i = pl.program_id(0)
+    groups = buf.shape[0] // ranks
+
+    def fresh(k):
+        return pltpu.make_async_copy(
+            parts[k - seen], buf.at[pl.ds(starts[k] - early, ranks)], part_sem.at[k]
+        )
+
+    def kept(k):
+        at = pl.ds(starts[k] - early, ranks)
+        return pltpu.make_async_copy(rest_in.at[at], buf.at[at], part_sem.at[k])
+
+    @pl.when(i == 0)
+    def _():
+        for step in ("start", "wait"):
+            for k in range(early // ranks, seen + len(parts)):
+
+                @pl.when(starts[k] >= early)
+                def _():
+                    getattr(kept(k) if k < seen else fresh(k), step)()
+
+        letters[...] = mail[...].astype(F32)
+        reply[...] = before_y[...]
+        restricted[...] = before_r[...]
+        lift[...] = before_l[...]
+
+    last = i == groups - 1
+    coarse_rows(i, early, ranks, items, recvs, even, own, buf, blk, sem, letters, blocks, restricted, reply, lift, held, last)
+
+    @pl.when(last)
     def _():
         packed[...] = reply[...].astype(BF)
 
 
-def coarse(recvs, places, starts, ranks, parts, mail, even, own, prol, group=16):
+def coarse_early(items, recvs, starts, ranks, early, parts, mail, even, own):
     half = even.shape[0]
-    row = pl.BlockSpec((group, B), lambda i, *_: (i, 0))
-    return pl.pallas_call(
-        functools.partial(coarse_kernel, group, ranks),
+    anywhere = pl.BlockSpec(memory_space=pl.ANY)
+    return pl.pallas_call(
+        functools.partial(early_kernel, ranks, early),
+        out_shape=(
+            jax.ShapeDtypeStruct((half, B, B), BF),
+            jax.ShapeDtypeStruct((half - early, 3, B, B), BF),
+            jax.ShapeDtypeStruct((half, B), F32),
+            jax.ShapeDtypeStruct((2 * half, B), F32),
+            jax.ShapeDtypeStruct((half, B), F32),
+        ),
+        grid_spec=pltpu.PrefetchScalarGridSpec(
+            num_scalar_prefetch=3,
+            grid=(early // ranks,),
+            in_specs=[
+                whole((2 * half, B)),
+                whole((half, B)),
+                pl.BlockSpec((ranks, B, 3 * B), lambda i, *_: (i, 0, 0)),
+            ]
+            + [anywhere] * len(parts),
+            out_specs=(
+                anywhere,
+                anywhere,
+                whole((half, B)),
+                whole((2 * half, B)),
+                whole((half, B)),
+            ),
+            scratch_shapes=[
+                pltpu.VMEM((half, 3, B, B), BF),
+                pltpu.VMEM((early, B, B), BF),
+                pltpu.SemaphoreType.DMA((early,)),
+                pltpu.SemaphoreType.DMA((len(parts) + 1,)),
+                pltpu.VMEM((2 * half, B), F32),
+                pltpu.VMEM((4 * ranks, B), F32),
+            ],
+        ),
+        compiler_params=params(),
+        name="coarse_early",
+    )(items, recvs, starts, mail, even, own, *parts)
+
+
+def coarse_late(items, recvs, starts, ranks, early, seen, parts, mail, even, own, restricted, reply, lift, blocks, kept):
+    half = even.shape[0]
+    late = half - early
+    anywhere = pl.BlockSpec(memory_space=pl.ANY)
+    return pl.pallas_call(
+        functools.partial(late_kernel, ranks, early, seen),
         out_shape=(
             jax.ShapeDtypeStruct((half, B, B), BF),
             jax.ShapeDtypeStruct((half, B), F32),
@@ -331,31 +452,32 @@
         ),
         grid_spec=pltpu.PrefetchScalarGridSpec(
             num_scalar_prefetch=3,
-            grid=(half // group,),
+            grid=(late // ranks,),
             in_specs=[
                 whole((2 * half, B)),
-                row,
-                pl.BlockSpec((group, B, 2 * B), lambda i, *_: (i, 0, 0)),
-                pl.BlockSpec((group, 1, B, B), lambda i, *_: (i, 0, 0, 0)),
+                whole((half, B)),
+                pl.BlockSpec((ranks, B, 3 * B), lambda i, *_: (i + early // ranks, 0, 0)),
+                whole((half, B)),
+                whole((2 * half, B)),
+                whole((half, B)),
+                anywhere,
+                anywhere,
             ]
-            + [pl.BlockSpec(memory_space=pl.ANY)] * len(parts),
-            out_specs=(
-                pl.BlockSpec((group, B, B), lambda i, *_: (i, 0, 0)),
-                row,
-                whole((2 * half, B)),
-                row,
-            ),
+            + [anywhere] * len(parts),
+            out_specs=(anywhere, whole((half, B)), whole((2 * half, B)), whole((half, B))),
             scratch_shapes=[
-                pltpu.VMEM((half, 3, B, B), BF),
-                pltpu.SemaphoreType.DMA((len(parts) + 1,)),
+                pltpu.VMEM((late, 3, B, B), BF),
+                pltpu.VMEM((late, B, B), BF),
+                pltpu.SemaphoreType.DMA((late,)),
+                pltpu.SemaphoreType.DMA((seen + len(parts),)),
                 pltpu.VMEM((2 * half, B), F32),
-                pltpu.VMEM((2 * half, B), F32),
-                pltpu.VMEM((group, B), F32),
+                pltpu.VMEM((2 * half + 4 * ranks, B), F32),
             ],
         ),
-        compiler_params=params(),
-        name="coarse",
-    )(recvs, places, starts, mail, even, own, prol.reshape(half, 2, B, B), *parts)
+        input_output_aliases={9: 0},
+        compiler_params=params(),
+        name="coarse_late",
+    )(items, recvs, starts, mail, even, own, restricted, reply, lift, blocks, kept, *parts)
 
 
 def finish_kernel(group, sends, mail, lift, x, prol, out, letters):
@@ -404,7 +526,9 @@
 
 def gather_line(block):
     line = lax.axis_size("rx")
-    return exchange(jnp.broadcast_to(block, (line,) + block.shape)).reshape(-1, B)
+    copies = jnp.broadcast_to(block, (line,) + block.shape)
+    gathered = lax.all_to_all(copies, "rx", split_axis=0, concat_axis=0, tiled=True)
+    return gathered.reshape(-1, B)
 
 
 def neighbours(block):
@@ -443,17 +567,20 @@
     slots = jnp.concatenate([line_slot(mate), line_slot(col_index[:, 0]), side_slot])
 
     item_ids = jnp.arange(half, dtype=jnp.int32)
-    def offset_of(line, ahead):
+    codes = jnp.array([dx * grid_side + dy for dx, dy in ORDER], jnp.int32)[:, None]
+    turns = jnp.arange(len(ORDER), dtype=jnp.int32)[:, None]
+
+    def turn_of(line, ahead):
         dx = ahead * (line // grid_side - line_pos // grid_side) % grid_side
         dy = ahead * (line - line_pos) % grid_side
-        return dx * grid_side + dy
-
-    def places_of(offset, rank):
-        slot = offset * capacity + rank
-        offsets = jnp.arange(line_size, dtype=jnp.int32)[:, None]
+        hits = (dx * grid_side + dy)[None, :] == codes
+        return jnp.sum(jnp.where(hits, turns, 0), axis=0, dtype=jnp.int32)
+
+    def places_of(turn, rank):
+        slot = turn * capacity + rank
         places = jnp.sum(slot[None, :] < slot[:, None], axis=1, dtype=jnp.int32)
-        starts = jnp.sum(offset[None, :] < offsets, axis=1, dtype=jnp.int32)
-        used = jnp.any(offset[None, :] == offsets, axis=1)
+        starts = jnp.sum(turn[None, :] < turns, axis=1, dtype=jnp.int32)
+        used = jnp.any(turn[None, :] == turns, axis=1)
         return places, jnp.where(used, starts, -1)
 
     target_line = odd_owner // half // side_size
@@ -461,29 +588,26 @@
     earlier = odd_owner[None, :] < odd_owner[:, None]
     send_rank = jnp.sum(same_target & earlier, axis=1, dtype=jnp.int32)
     sends = target_line * capacity + send_rank
-    send_places, send_starts = places_of(offset_of(target_line, 1), send_rank)
+    send_places, send_starts = places_of(turn_of(target_line, 1), send_rank)
     source_line = partner // rows // side_size
     same_source = source_line[:, None] == source_line[None, :]
     before = item_ids[None, :] < item_ids[:, None]
     recv_rank = jnp.sum(same_source & before, axis=1, dtype=jnp.int32)
     recvs = source_line * capacity + recv_rank
-    recv_places, recv_starts = places_of(offset_of(source_line, -1), recv_rank)
-
-    barrier = lax.optimization_barrier
-    leaving = list(
-        odd_blocks(send_places, send_starts, capacity, prolong, a_diag, a_pair)
-    )
-    arrived = [None] * len(leaving)
+    recv_places, recv_starts = places_of(turn_of(source_line, -1), recv_rank)
+
+    hits = recv_places[None, :] == item_ids[:, None]
+    items = jnp.sum(jnp.where(hits, item_ids[None, :], 0), axis=1, dtype=jnp.int32)
+
+    leaving = odd_blocks(send_places, send_starts, capacity, prolong, a_diag, a_pair)
+    arrived = []
 
     def leave(first, last, gate):
-        picked = [dx * grid_side + dy - 1 for dx, dy in ORDER[first:last]]
-        waits = [dx * grid_side + dy - 1 for dx, dy in ORDER[max(first - WINDOW, 0) : max(last - WINDOW, 0)]]
-        ins, old, gate = barrier(([leaving[k] for k in picked], [arrived[k] for k in waits], gate))
-        for k, part in zip(waits, old):
-            arrived[k] = part
-        for k, part in zip(picked, ins):
-            dx, dy = divmod(k + 1, grid_side)
-            arrived[k] = lax.ppermute(part, "rx", along(grid_side, dx, dy))
+        wait = max(first - WINDOW, 0)
+        ins, old, gate = lax.optimization_barrier((leaving[first:last], arrived[wait:], gate))
+        arrived[wait:] = old
+        for part, (dx, dy) in zip(ins, ORDER[first:last]):
+            arrived.append(lax.ppermute(part, "rx", along(grid_side, dx, dy)))
         return gate
 
     rhs = leave(0, 4, rhs)
@@ -497,14 +621,19 @@
     low, high = neighbours(x_low)
     table = gather_line(x_low)
     table = leave(8, 12, table)
-    own = even_blocks(prolong, a_diag, a_pair)
+    own = even_blocks(recv_places, prolong, a_diag, a_pair)
     even, mail = residual_pieces(
         slots, sends, rhs, x, table, low, high, a_diag, a_pair, a_far, prolong
     )
+    mail = exchange(mail)
     mail = leave(12, 15, mail)
-    mail = exchange(mail)
-    blocks, restricted, reply, lift = coarse(
-        recvs, recv_places, recv_starts, capacity, arrived, mail, even, own, prolong
+    late = 3 * capacity
+    early = half - late
+    blocks, kept, restricted, reply, lift = coarse_early(
+        items, recvs, recv_starts, capacity, early, arrived[:12], mail, even, own
+    )
+    blocks, restricted, reply, lift = coarse_late(
+        items, recvs, recv_starts, capacity, early, 12, arrived[12:], mail, even, own, restricted, reply, lift, blocks, kept
     )
     fine = finish(sends, exchange(reply), lift, x, prolong)
     return fine, blocks, restricted

time: 232 us -> 224 us (0.966)
  waiting for transfers between devices: 87.3 us -> 69.1 us
  Pallas kernels: 57.4 us -> 65.5 us
  starting transfers between devices: 42.4 us -> 48.1 us
  local copies, waits for them, and re-layouts: 10.7 us -> 7.37 us
    all_to_all x0 -> x1, waiting for transfers between devices: none -> 28.6 us  [gather_line(): lax.all_to_all(copies, 'rx', split_axis=0, concat_axis=0, tiled=True)]
    all_to_all x2 -> x1, waiting for transfers between devices: 44.5 us -> 19.9 us  [exchange(): lax.all_to_all(packed.reshape((line, -1) + shape[1:]), 'rx', split_axis=0...]
    ppermute x15, waiting for transfers between devices: 34.5 us -> 12 us  [leave(): arrived.append(lax.ppermute(part, 'rx', along(grid_side, dx, dy)))]
    all_to_all x2 -> x1, blocking collectives: 28.4 us -> 12.2 us  [exchange(): lax.all_to_all(packed.reshape((line, -1) + shape[1:]), 'rx', split_axis=0...]
    all_to_all x0 -> x1, blocking collectives: none -> 15.7 us  [gather_line(): lax.all_to_all(copies, 'rx', split_axis=0, concat_axis=0, tiled=True)]
    pallas_call x2 -> x3, Pallas kernels: 14.8 us -> 22.9 us  [the longest x1 9.27 us: coarse_early(): pl.pallas_call(functools.partial(early_kernel, ranks, early), out_shape=(...]
    ppermute x15, starting transfers between devices: 29.3 us -> 34 us  [leave(): arrived.append(lax.ppermute(part, 'rx', along(grid_side, dx, dy)))]
    all_to_all x0 -> x1, starting transfers between devices: none -> 4.5 us  [gather_line(): lax.all_to_all(copies, 'rx', split_axis=0, concat_axis=0, tiled=True)]
  transfers between devices with their start and end apart: 21 -> 21, of which waited for: 6 -> 7; matrix products, arithmetic and copies ran while one was open for 1% -> 1% of each run, Pallas kernels for 16% -> 22%
where the time goes in v3:
time: 224 us; the launch traced here: 223 us
  waiting for transfers between devices  69.1 us (31%)
  Pallas kernels  65.5 us (29%)
  starting transfers between devices  48.1 us (21%)
  blocking collectives  27.8 us (12%)
  local copies, waits for them, and re-layouts  7.37 us (3%)
  other arithmetic  3.55 us (2%)
    ppermute x15, starting transfers between devices, leave(): arrived.append(lax.ppermute(part, 'rx', along(grid_side, dx, dy)))  34 us
    all_to_all x1, waiting for transfers between devices, gather_line(): lax.all_to_all(copies, 'rx', split_axis=0, concat_axis=0, tiled=True)  28.6 us
    all_to_all x1, waiting for transfers between devices, exchange(): lax.all_to_all(packed.reshape((line, -1) + shape[1:]), 'rx', split_axis=0...  19.9 us
    all_to_all x1, blocking collectives, gather_line(): lax.all_to_all(copies, 'rx', split_axis=0, concat_axis=0, tiled=True)  15.7 us
    pallas_call x1, Pallas kernels, residual_pieces(): pl.pallas_call(functools.partial(residual_kernel, group, rows), out_shape...  14.7 us
    pallas_call x1, Pallas kernels, second_sweep(): pl.pallas_call(functools.partial(sweep_kernel, group, rows), out_shape=(j...  14.4 us
    all_to_all x1, blocking collectives, exchange(): lax.all_to_all(packed.reshape((line, -1) + shape[1:]), 'rx', split_axis=0...  12.2 us
    ppermute x15, waiting for transfers between devices, leave(): arrived.append(lax.ppermute(part, 'rx', along(grid_side, dx, dy)))  12 us
  transfers between devices with their start and end apart: 21, of which 7 were waited for; matrix products, arithmetic and copies ran while one was open for 1% of the time, Pallas kernels for 22%

profile of v3, /device:TPU:0, one launch (start us, length us, event | category | flops | bytes accessed | tf_op | source)
XLA Modules:
  0.0 222.6 jit_solution(10695544668224400353)
XLA Ops:
  3.5 8.2 %odd_blocks.1 = (bf16[8,3,128,128]{3,2,1,0:T(8,128)(2,1)}, bf16[8,3,128,128]{3,2,1,0:T(8,128)(2,1)}, bf16[8,3,128,128]{3,2,1,0:T(8,128)(2,1)}, bf16[8,3,128,128]...) custom-call(s32[64]{0:T(128)S(1)} %convert_reduce_fusion.places, ...), custom_call_target="tpu_custom_call" | custom-call | tf_op jit(solution)/shard_map/odd_blocks/pallas_call | solution.py:237
  11.7 2.7 %collective-permute-start = (bf16[8,3,128,128]{3,2,1,0:T(8,128)(2,1)}, bf16[8,3,128,128]{3,2,1,0:T(8,128)(2,1)S(1)}, u32[]{:S(2)}, u32[]{:S(2)}) collective-permute-start(bf16[8,3,128,128]{3,2,1,0:T(8,128)(2,1)} %get-tuple-element.79), channel_id=1, source_target_pairs={{0,40},{8,48},{16,56},{24,32},{32,72},{40,80},{48,88},{56,64},{64,... | collective-permute-start | bytes 2359304 | tf_op jit(solution)/shard_map/ppermute | solution.py:610
  14.4 2.8 %collective-permute-start.1 = (bf16[8,3,128,128]{3,2,1,0:T(8,128)(2,1)}, bf16[8,3,128,128]{3,2,1,0:T(8,128)(2,1)S(1)}, u32[]{:S(2)}, u32[]{:S(2)}) collective-permute-start(bf16[8,3,128,128]{3,2,1,0:T(8,128)(2,1)} %get-tuple-element.80), channel_id=1, source_target_pairs={{0,120},{8,96},{16,104},{24,112},{32,24},{40,0},{48,8},{56,16},{64... | collective-permute-start | bytes 2359304 | tf_op jit(solution)/shard_map/ppermute | solution.py:610
  18.7 2.6 %collective-permute-start.3 = (bf16[8,3,128,128]{3,2,1,0:T(8,128)(2,1)}, bf16[8,3,128,128]{3,2,1,0:T(8,128)(2,1)}, u32[]{:S(2)}, u32[]{:S(2)}) collective-permute-start(bf16[8,3,128,128]{3,2,1,0:T(8,128)(2,1)} %get-tuple-element.82), channel_id=1, source_target_pairs={{0,104},{8,112},{16,120},{24,96},{32,8},{40,16},{48,24},{56,0},{64... | collective-permute-start | bytes 2359304 | tf_op jit(solution)/shard_map/ppermute | solution.py:610
  21.3 2.7 %first_sweep.1 = (f32[128,128]{1,0:T(8,128)S(1)}, bf16[128,128]{1,0:T(8,128)(2,1)S(1)}) custom-call(f32[128,128]{1,0:T(8,128)S(1)} %copy-done.12, bf16[128,128,128]{2,1,0:T(8,128)(2,1)S(1)} %copy-done.4), custom_call_target="tpu_custom_call" | custom-call | tf_op jit(solution)/shard_map/first_sweep/pallas_call | solution.py:68
  24.9 4.5 %all-to-all-start = ((bf16[16,128,128]{2,1,0:T(8,128)(2,1)}), bf16[16,128,128]{2,1,0:T(8,128)(2,1)S(1)}, u32[]{:S(2)}, u32[]{:S(2)}) async-start(bf16[16,128,128]{2,1,0:T(8,128)(2,1)} %broadcast_in_dim.83), calls=%async_computation | async-start | bytes 1048576 | tf_op jit(solution)/shard_map/all_to_all | solution.py:530
  31.8 28.6 %all-to-all-done = bf16[16,128,128]{2,1,0:T(8,128)(2,1)S(1)} async-done(((bf16[16,128,128]{2,1,0:T(8,128)(2,1)}), bf16[16,128,128]{2,1,0:T(8,128)(2,1)S(1)}, u32[]{:S(2)}, u32[]{:S(2)}) %all-to-all-start) | async-done | bytes 524320 | tf_op jit(solution)/shard_map/all_to_all | solution.py:530
  61.4 4.7 %collective-permute-start.5 = (bf16[8,3,128,128]{3,2,1,0:T(8,128)(2,1)}, bf16[8,3,128,128]{3,2,1,0:T(8,128)(2,1)S(1)}, u32[]{:S(2)}, u32[]{:S(2)}) collective-permute-start(bf16[8,3,128,128]{3,2,1,0:T(8,128)(2,1)} %copy-done.14), channel_id=1, source_target_pairs={{0,88},{8,64},{16,72},{24,80},{32,120},{40,96},{48,104},{56,112},{... | collective-permute-start | bytes 2359304 | tf_op jit(solution)/shard_map/ppermute | solution.py:610
  66.1 3.2 %collective-permute-start.7 = (bf16[8,3,128,128]{3,2,1,0:T(8,128)(2,1)}, bf16[8,3,128,128]{3,2,1,0:T(8,128)(2,1)S(1)}, u32[]{:S(2)}, u32[]{:S(2)}) collective-permute-start(bf16[8,3,128,128]{3,2,1,0:T(8,128)(2,1)} %get-tuple-element.88), channel_id=1, source_target_pairs={{0,24},{8,0},{16,8},{24,16},{32,56},{40,32},{48,40},{56,48},{64,88... | collective-permute-start | bytes 2359304 | tf_op jit(solution)/shard_map/ppermute | solution.py:610
  69.4 4.5 %collective-permute-done.8.low = bf16[128,128]{1,0:T(8,128)(2,1)S(1)} collective-permute-done((bf16[128,128]{1,0:T(8,128)(2,1)S(1)}, bf16[128,128]{1,0:T(8,128)(2,1)S(1)}, u32[]{:S(2)}, u32[]{:S(2)}) %collective-permute-start.8) | collective-permute-done | bytes 32800 | tf_op jit(solution)/shard_map/ppermute | solution.py:538
  76.1 14.4 %second_sweep.1 = (f32[128,128]{1,0:T(8,128)S(1)}, bf16[128,128]{1,0:T(8,128)(2,1)S(1)}) custom-call(s32[384]{0:T(512)S(1)} %pad_add_fusion.slots, f32[128,128]{1,0:T(8,128)S(1)} %copy-done.12, f32[128,128]{1,0:T(8,128)S(1)} %get-tuple-element.89.x_group, bf16[2048,128]{1,0:T(8,128)(2,1)S(1)} %bitcast.43, bf16[128,128]{1,0:T(8,128)(2,1)S(1)} %collective-permute-done.8.low, ...), custom_call_target="tpu_custom_call" | custom-call | tf_op jit(solution)/shard_map/second_sweep/pallas_call | solution.py:163
  90.7 15.7 %all_to_all.20 = bf16[16,128,128]{2,1,0:T(8,128)(2,1)S(1)} all-to-all(bf16[16,128,128]{2,1,0:T(8,128)(2,1)S(1)} %broadcast_in_dim.84), channel_id=1, replica_groups=mesh['rx'=16,'ry'=8] {'rx'}, dimensions={0} | all-to-all | bytes 1048576 | tf_op jit(solution)/shard_map/all_to_all | solution.py:530
  108.9 3.2 %collective-permute-start.11 = (bf16[8,3,128,128]{3,2,1,0:T(8,128)(2,1)}, bf16[8,3,128,128]{3,2,1,0:T(8,128)(2,1)}, u32[]{:S(2)}, u32[]{:S(2)}) collective-permute-start(bf16[8,3,128,128]{3,2,1,0:T(8,128)(2,1)} %get-tuple-element.93), channel_id=1, source_target_pairs={{0,112},{8,120},{16,96},{24,104},{32,16},{40,24},{48,0},{56,8},{64... | collective-permute-start | bytes 2359304 | tf_op jit(solution)/shard_map/ppermute | solution.py:610
  112.1 3.2 %collective-permute-start.13 = (bf16[8,3,128,128]{3,2,1,0:T(8,128)(2,1)}, bf16[8,3,128,128]{3,2,1,0:T(8,128)(2,1)}, u32[]{:S(2)}, u32[]{:S(2)}) collective-permute-start(bf16[8,3,128,128]{3,2,1,0:T(8,128)(2,1)} %get-tuple-element.95), channel_id=1, source_target_pairs={{0,96},{8,104},{16,112},{24,120},{32,0},{40,8},{48,16},{56,24},{64... | collective-permute-start | bytes 2359304 | tf_op jit(solution)/shard_map/ppermute | solution.py:610
  121.9 14.7 %residual_pieces.1 = (f32[64,128]{1,0:T(8,128)S(1)}, bf16[128,128]{1,0:T(8,128)(2,1)}) custom-call(s32[384]{0:T(512)S(1)} %pad_add_fusion.slots, s32[64]{0:T(128)S(1)} %get-tuple-element.135.sends, f32[128,128]{1,0:T(8,128)S(1)} %copy-done.12, f32[128,128]{1,0:T(8,128)S(1)} %get-tuple-element.96.x_group.x, bf16[2048,128]{1,0:T(8,128)(2,1)S(1)} %bitcast.44, ...), custom_call_target="tpu_custom_call" | custom-call | tf_op jit(solution)/shard_map/residual_pieces/pallas_call | solution.py:183
  136.6 5.1 %all-to-all-start.2 = ((bf16[16,8,128]{2,1,0:T(8,128)(2,1)}), bf16[16,8,128]{2,1,0:T(8,128)(2,1)S(1)}, u32[]{:S(2)}, u32[]{:S(2)}) async-start(bf16[16,8,128]{2,1,0:T(8,128)(2,1)} %bitcast.9), calls=%async_computation.2 | async-start | bytes 65536 | tf_op jit(solution)/shard_map/all_to_all | solution.py:544
  141.9 19.9 %all-to-all-done.2 = bf16[16,8,128]{2,1,0:T(8,128)(2,1)S(1)} async-done(((bf16[16,8,128]{2,1,0:T(8,128)(2,1)}), bf16[16,8,128]{2,1,0:T(8,128)(2,1)S(1)}, u32[]{:S(2)}, u32[]{:S(2)}) %all-to-all-start.2) | async-done | bytes 32800 | tf_op jit(solution)/shard_map/all_to_all | solution.py:544
  162.4 3.9 %collective-permute-start.17 = (bf16[8,3,128,128]{3,2,1,0:T(8,128)(2,1)}, bf16[8,3,128,128]{3,2,1,0:T(8,128)(2,1)S(1)}, u32[]{:S(2)}, u32[]{:S(2)}) collective-permute-start(bf16[8,3,128,128]{3,2,1,0:T(8,128)(2,1)} %get-tuple-element.119), channel_id=1, source_target_pairs={{0,64},{8,72},{16,80},{24,88},{32,96},{40,104},{48,112},{56,120},{... | collective-permute-start | bytes 2359304 | tf_op jit(solution)/shard_map/ppermute | solution.py:610
  170.8 7.4 %even_blocks.1.own = bf16[64,128,384]{2,1,0:T(8,128)(2,1)} custom-call(s32[64]{0:T(128)S(1)} %convert_reduce_fusion.1.places, bf16[64,2,128,128]{3,2,1,0:T(8,128)(2,1)S(1)} %bitcast.39, bf16[64,2,128,128]{3,2,1,0:T(8,128)(2,1)} %bitcast.42, bf16[64,2,128,128]{3,2,1,0:T(8,128)(2,1)} %bitcast.50), custom_call_target="tpu_custom_call" | custom-call | tf_op jit(solution)/shard_map/even_blocks/pallas_call | solution.py:271
  178.6 9.3 %coarse_early.1 = (bf16[64,128,128]{2,1,0:T(8,128)(2,1)}, bf16[24,3,128,128]{3,2,1,0:T(8,128)(2,1)}, f32[64,128]{1,0:T(8,128)S(1)}, f32[128,128]{1,0:T(8,128)S(1)}, f32[64,128]{1,0:T(8,128)S(1)}) custom-call(s32[64]{0:T(128)S(1)} %select_reduce_fusion.items, s32[64]{0:T(128)S(1)} %get-tuple-element.136.recvs, s32[15]{0:T(128)S(1)} %broadcast_select_fusion.1.starts, ...), custom_call_target="tpu_custom_call" | custom-call | tf_op jit(solution)/shard_map/coarse_early/pallas_call | solution.py:402
  187.8 10.7 %collective-permute-done.17.rest_1_ = bf16[8,3,128,128]{3,2,1,0:T(8,128)(2,1)S(1)} collective-permute-done((bf16[8,3,128,128]{3,2,1,0:T(8,128)(2,1)}, bf16[8,3,128,128]{3,2,1,0:T(8,128)(2,1)S(1)}, u32[]{:S(2)}, u32[]{:S(2)}) %collective-permute-start.17) | collective-permute-done | bytes 786464 | tf_op jit(solution)/shard_map/ppermute | solution.py:610
  201.4 6.3 %coarse_late.1 = (bf16[64,128,128]{2,1,0:T(8,128)(2,1)}, f32[64,128]{1,0:T(8,128)}, bf16[128,128]{1,0:T(8,128)(2,1)S(1)}, f32[64,128]{1,0:T(8,128)S(1)}) custom-call(s32[64]{0:T(128)S(1)} %select_reduce_fusion.items, s32[64]{0:T(128)S(1)} %get-tuple-element.136.recvs, s32[15]{0:T(128)S(1)} %broadcast_select_fusion.1.starts, ...), custom_call_target="tpu_custom_call", output_to_operand_aliasing={{0}: (9, {})} | custom-call | tf_op jit(solution)/shard_map/coarse_late/pallas_call | solution.py:445
  207.7 12.2 %all_to_all.21 = bf16[16,8,128]{2,1,0:T(8,128)(2,1)S(1)} all-to-all(bf16[16,8,128]{2,1,0:T(8,128)(2,1)S(1)} %bitcast.48), channel_id=1, replica_groups=mesh['rx'=16,'ry'=8] {'rx'}, dimensions={0} | all-to-all | bytes 65536 | tf_op jit(solution)/shard_map/all_to_all | solution.py:544
  219.9 2.7 %finish.1 = f32[128,128]{1,0:T(8,128)} custom-call(s32[64]{0:T(128)S(1)} %get-tuple-element.135.sends, bf16[128,128]{1,0:T(8,128)(2,1)S(1)} %bitcast.47, f32[64,128]{1,0:T(8,128)S(1)} %get-tuple-element.122.lift, f32[128,128]{1,0:T(8,128)S(1)} %get-tuple-element.96.x_group.x, bf16[64,2,128,128]{3,2,1,0:T(8,128)(2,1)S(1)} %bitcast.40), custom_call_target="tpu_custom_call" | custom-call | tf_op jit(solution)/shard_map/finish/pallas_call | solution.py:499
  (91 shorter events, 28.7 us)
Async XLA Ops:
  11.7 48.6 %collective-permute-start = (bf16[8,3,128,128]{3,2,1,0:T(8,128)(2,1)}, bf16[8,3,128,128]{3,2,1,0:T(8,128)(2,1)S(1)}, u32[]{:S(2)}, u32[]{:S(2)}) collective-permute-start(bf16[8,3,128,128]{3,2,1,0:T(8,128)(2,1)} %get-tuple-element.79), channel_id=1, source_target_pairs={{0,40},{8,48},{16,56},{24,32},{32,72},{40,80},{48,88},{56,64},{64,... | collective-permute-start | bytes 2359304 | tf_op jit(solution)/shard_map/ppermute | solution.py:610
  14.4 46.0 %collective-permute-start.1 = (bf16[8,3,128,128]{3,2,1,0:T(8,128)(2,1)}, bf16[8,3,128,128]{3,2,1,0:T(8,128)(2,1)S(1)}, u32[]{:S(2)}, u32[]{:S(2)}) collective-permute-start(bf16[8,3,128,128]{3,2,1,0:T(8,128)(2,1)} %get-tuple-element.80), channel_id=1, source_target_pairs={{0,120},{8,96},{16,104},{24,112},{32,24},{40,0},{48,8},{56,16},{64... | collective-permute-start | bytes 2359304 | tf_op jit(solution)/shard_map/ppermute | solution.py:610
  17.2 43.2 %collective-permute-start.2 = (bf16[8,3,128,128]{3,2,1,0:T(8,128)(2,1)}, bf16[8,3,128,128]{3,2,1,0:T(8,128)(2,1)S(1)}, u32[]{:S(2)}, u32[]{:S(2)}) collective-permute-start(bf16[8,3,128,128]{3,2,1,0:T(8,128)(2,1)} %get-tuple-element.81), channel_id=1, source_target_pairs={{0,56},{8,32},{16,40},{24,48},{32,88},{40,64},{48,72},{56,80},{64,... | collective-permute-start | bytes 2359304 | tf_op jit(solution)/shard_map/ppermute | solution.py:610
  18.7 41.6 %collective-permute-start.3 = (bf16[8,3,128,128]{3,2,1,0:T(8,128)(2,1)}, bf16[8,3,128,128]{3,2,1,0:T(8,128)(2,1)}, u32[]{:S(2)}, u32[]{:S(2)}) collective-permute-start(bf16[8,3,128,128]{3,2,1,0:T(8,128)(2,1)} %get-tuple-element.82), channel_id=1, source_target_pairs={{0,104},{8,112},{16,120},{24,96},{32,8},{40,16},{48,24},{56,0},{64... | collective-permute-start | bytes 2359304 | tf_op jit(solution)/shard_map/ppermute | solution.py:610
  24.9 35.5 %all-to-all-start = ((bf16[16,128,128]{2,1,0:T(8,128)(2,1)}), bf16[16,128,128]{2,1,0:T(8,128)(2,1)S(1)}, u32[]{:S(2)}, u32[]{:S(2)}) async-start(bf16[16,128,128]{2,1,0:T(8,128)(2,1)} %broadcast_in_dim.83), calls=%async_computation | async-start | bytes 1048576 | tf_op jit(solution)/shard_map/all_to_all | solution.py:530
  29.4 39.9 %collective-permute-start.9 = (bf16[128,128]{1,0:T(8,128)(2,1)S(1)}, bf16[128,128]{1,0:T(8,128)(2,1)S(1)}, u32[]{:S(2)}, u32[]{:S(2)}) collective-permute-start(bf16[128,128]{1,0:T(8,128)(2,1)S(1)} %get-tuple-element.84), channel_id=1, source_target_pairs={{1,0},{2,1},{3,2},{4,3},{5,4},{6,5},{7,6},{0,7},{9,8},{10,9},{11,1... | collective-permute-start | bytes 98312 | tf_op jit(solution)/shard_map/ppermute | solution.py:538
  60.4 46.0 %collective-permute-start.4 = (bf16[8,3,128,128]{3,2,1,0:T(8,128)(2,1)}, bf16[8,3,128,128]{3,2,1,0:T(8,128)(2,1)S(1)}, u32[]{:S(2)}, u32[]{:S(2)}) collective-permute-start(bf16[8,3,128,128]{3,2,1,0:T(8,128)(2,1)} %copy-done.15), channel_id=1, source_target_pairs={{0,72},{8,80},{16,88},{24,64},{32,104},{40,112},{48,120},{56,96},{... | collective-permute-start | bytes 2359304 | tf_op jit(solution)/shard_map/ppermute | solution.py:610
  61.4 44.9 %collective-permute-start.5 = (bf16[8,3,128,128]{3,2,1,0:T(8,128)(2,1)}, bf16[8,3,128,128]{3,2,1,0:T(8,128)(2,1)S(1)}, u32[]{:S(2)}, u32[]{:S(2)}) collective-permute-start(bf16[8,3,128,128]{3,2,1,0:T(8,128)(2,1)} %copy-done.14), channel_id=1, source_target_pairs={{0,88},{8,64},{16,72},{24,80},{32,120},{40,96},{48,104},{56,112},{... | collective-permute-start | bytes 2359304 | tf_op jit(solution)/shard_map/ppermute | solution.py:610
  66.1 40.3 %collective-permute-start.6 = (bf16[8,3,128,128]{3,2,1,0:T(8,128)(2,1)}, bf16[8,3,128,128]{3,2,1,0:T(8,128)(2,1)S(1)}, u32[]{:S(2)}, u32[]{:S(2)}) collective-permute-start(bf16[8,3,128,128]{3,2,1,0:T(8,128)(2,1)} %copy-done.13), channel_id=1, source_target_pairs={{0,8},{8,16},{16,24},{24,0},{32,40},{40,48},{48,56},{56,32},{64,72... | collective-permute-start | bytes 2359304 | tf_op jit(solution)/shard_map/ppermute | solution.py:610
  66.1 40.3 %collective-permute-start.7 = (bf16[8,3,128,128]{3,2,1,0:T(8,128)(2,1)}, bf16[8,3,128,128]{3,2,1,0:T(8,128)(2,1)S(1)}, u32[]{:S(2)}, u32[]{:S(2)}) collective-permute-start(bf16[8,3,128,128]{3,2,1,0:T(8,128)(2,1)} %get-tuple-element.88), channel_id=1, source_target_pairs={{0,24},{8,0},{16,8},{24,16},{32,56},{40,32},{48,40},{56,48},{64,88... | collective-permute-start | bytes 2359304 | tf_op jit(solution)/shard_map/ppermute | solution.py:610
  69.4 4.6 %collective-permute-start.8 = (bf16[128,128]{1,0:T(8,128)(2,1)S(1)}, bf16[128,128]{1,0:T(8,128)(2,1)S(1)}, u32[]{:S(2)}, u32[]{:S(2)}) collective-permute-start(bf16[128,128]{1,0:T(8,128)(2,1)S(1)} %get-tuple-element.84), channel_id=1, source_target_pairs={{0,1},{1,2},{2,3},{3,4},{4,5},{5,6},{6,7},{7,0},{8,9},{9,10},{10,1... | collective-permute-start | bytes 98312 | tf_op jit(solution)/shard_map/ppermute | solution.py:538
  76.1 45.8 %copy-start.3 = (bf16[128,128,128]{2,1,0:T(8,128)(2,1)S(1)}, bf16[128,128,128]{2,1,0:T(8,128)(2,1)}, u32[]{:S(2)}) copy-start(bf16[128,128,128]{2,1,0:T(8,128)(2,1)} %diag.3) | copy-start | bytes 12582916
  106.3 30.3 %copy-start.6 = (bf16[8,3,128,128]{3,2,1,0:T(8,128)(2,1)}, bf16[8,3,128,128]{3,2,1,0:T(8,128)(2,1)S(1)}, u32[]{:S(2)}) copy-start(bf16[8,3,128,128]{3,2,1,0:T(8,128)(2,1)S(1)} %collective-permute-done.4.rest_4_) | copy-start | bytes 2359300
  106.3 30.2 %copy-start.8 = (bf16[8,3,128,128]{3,2,1,0:T(8,128)(2,1)}, bf16[8,3,128,128]{3,2,1,0:T(8,128)(2,1)S(1)}, u32[]{:S(2)}) copy-start(bf16[8,3,128,128]{3,2,1,0:T(8,128)(2,1)S(1)} %collective-permute-done.5.rest_5_) | copy-start | bytes 2359300
  106.4 55.4 %collective-permute-start.10 = (bf16[8,3,128,128]{3,2,1,0:T(8,128)(2,1)}, bf16[8,3,128,128]{3,2,1,0:T(8,128)(2,1)S(1)}, u32[]{:S(2)}, u32[]{:S(2)}) collective-permute-start(bf16[8,3,128,128]{3,2,1,0:T(8,128)(2,1)} %get-tuple-element.92), channel_id=1, source_target_pairs={{0,48},{8,56},{16,32},{24,40},{32,80},{40,88},{48,64},{56,72},{64,... | collective-permute-start | bytes 2359304 | tf_op jit(solution)/shard_map/ppermute | solution.py:610
  108.9 52.9 %collective-permute-start.11 = (bf16[8,3,128,128]{3,2,1,0:T(8,128)(2,1)}, bf16[8,3,128,128]{3,2,1,0:T(8,128)(2,1)}, u32[]{:S(2)}, u32[]{:S(2)}) collective-permute-start(bf16[8,3,128,128]{3,2,1,0:T(8,128)(2,1)} %get-tuple-element.93), channel_id=1, source_target_pairs={{0,112},{8,120},{16,96},{24,104},{32,16},{40,24},{48,0},{56,8},{64... | collective-permute-start | bytes 2359304 | tf_op jit(solution)/shard_map/ppermute | solution.py:610
  112.1 49.7 %collective-permute-start.12 = (bf16[8,3,128,128]{3,2,1,0:T(8,128)(2,1)}, bf16[8,3,128,128]{3,2,1,0:T(8,128)(2,1)}, u32[]{:S(2)}, u32[]{:S(2)}) collective-permute-start(bf16[8,3,128,128]{3,2,1,0:T(8,128)(2,1)} %get-tuple-element.94), channel_id=1, source_target_pairs={{0,32},{8,40},{16,48},{24,56},{32,64},{40,72},{48,80},{56,88},{64,... | collective-permute-start | bytes 2359304 | tf_op jit(solution)/shard_map/ppermute | solution.py:610
  112.1 49.7 %collective-permute-start.13 = (bf16[8,3,128,128]{3,2,1,0:T(8,128)(2,1)}, bf16[8,3,128,128]{3,2,1,0:T(8,128)(2,1)}, u32[]{:S(2)}, u32[]{:S(2)}) collective-permute-start(bf16[8,3,128,128]{3,2,1,0:T(8,128)(2,1)} %get-tuple-element.95), channel_id=1, source_target_pairs={{0,96},{8,104},{16,112},{24,120},{32,0},{40,8},{48,16},{56,24},{64... | collective-permute-start | bytes 2359304 | tf_op jit(solution)/shard_map/ppermute | solution.py:610
  115.3 1.6 collective-permute-start.15
  117.0 4.9 %collective-permute-start.14 = (bf16[128,128]{1,0:T(8,128)(2,1)S(1)}, bf16[128,128]{1,0:T(8,128)(2,1)S(1)}, u32[]{:S(2)}, u32[]{:S(2)}) collective-permute-start(bf16[128,128]{1,0:T(8,128)(2,1)S(1)} %get-tuple-element.91), channel_id=1, source_target_pairs={{0,1},{1,2},{2,3},{3,4},{4,5},{5,6},{6,7},{7,0},{8,9},{9,10},{10,1... | collective-permute-start | bytes 98312 | tf_op jit(solution)/shard_map/ppermute | solution.py:538
  136.6 25.2 %all-to-all-start.2 = ((bf16[16,8,128]{2,1,0:T(8,128)(2,1)}), bf16[16,8,128]{2,1,0:T(8,128)(2,1)S(1)}, u32[]{:S(2)}, u32[]{:S(2)}) async-start(bf16[16,8,128]{2,1,0:T(8,128)(2,1)} %bitcast.9), calls=%async_computation.2 | async-start | bytes 65536 | tf_op jit(solution)/shard_map/all_to_all | solution.py:544
  161.8 26.0 %collective-permute-start.16 = (bf16[8,3,128,128]{3,2,1,0:T(8,128)(2,1)}, bf16[8,3,128,128]{3,2,1,0:T(8,128)(2,1)S(1)}, u32[]{:S(2)}, u32[]{:S(2)}) collective-permute-start(bf16[8,3,128,128]{3,2,1,0:T(8,128)(2,1)} %get-tuple-element.118), channel_id=1, source_target_pairs={{0,80},{8,88},{16,64},{24,72},{32,112},{40,120},{48,96},{56,104},{... | collective-permute-start | bytes 2359304 | tf_op jit(solution)/shard_map/ppermute | solution.py:610
  162.4 36.1 %collective-permute-start.17 = (bf16[8,3,128,128]{3,2,1,0:T(8,128)(2,1)}, bf16[8,3,128,128]{3,2,1,0:T(8,128)(2,1)S(1)}, u32[]{:S(2)}, u32[]{:S(2)}) collective-permute-start(bf16[8,3,128,128]{3,2,1,0:T(8,128)(2,1)} %get-tuple-element.119), channel_id=1, source_target_pairs={{0,64},{8,72},{16,80},{24,88},{32,96},{40,104},{48,112},{56,120},{... | collective-permute-start | bytes 2359304 | tf_op jit(solution)/shard_map/ppermute | solution.py:610
  166.3 33.5 %collective-permute-start.18 = (bf16[8,3,128,128]{3,2,1,0:T(8,128)(2,1)}, bf16[8,3,128,128]{3,2,1,0:T(8,128)(2,1)S(1)}, u32[]{:S(2)}, u32[]{:S(2)}) collective-permute-start(bf16[8,3,128,128]{3,2,1,0:T(8,128)(2,1)} %get-tuple-element.120), channel_id=1, source_target_pairs={{0,16},{8,24},{16,0},{24,8},{32,48},{40,56},{48,32},{56,40},{64,80... | collective-permute-start | bytes 2359304 | tf_op jit(solution)/shard_map/ppermute | solution.py:610
  (17 other events, 237.0 us)

commit v4 on v3

--- a/solution.py
+++ b/solution.py
@@ -330,10 +330,6 @@
             parts[k], buf.at[pl.ds(starts[k], ranks)], part_sem.at[k]
         )
 
-    later = pltpu.make_async_copy(
-        buf.at[pl.ds(early, buf.shape[0] - early)], rest_out, part_sem.at[len(parts)]
-    )
-
     @pl.when(i == 0)
     def _():
         for step in ("start", "wait"):
@@ -343,18 +339,13 @@
                 def _():
                     getattr(near(k), step)()
 
-        later.start()
+        rest_out[...] = buf[early:]
         letters[...] = mail[...].astype(F32)
         reply[...] = jnp.zeros_like(reply)
         restricted[...] = jnp.zeros_like(restricted)
         lift[...] = jnp.zeros_like(lift)
 
     last = i == pl.num_programs(0) - 1
-
-    @pl.when(last)
-    def _():
-        later.wait()
-
     coarse_rows(i, 0, ranks, items, recvs, even, own, buf, blk, sem, letters, blocks, restricted, reply, lift, held, last)
 
 
@@ -419,7 +410,7 @@
             + [anywhere] * len(parts),
             out_specs=(
                 anywhere,
-                anywhere,
+                whole((half - early, 3, B, B)),
                 whole((half, B)),
                 whole((2 * half, B)),
                 whole((half, B)),
@@ -428,7 +419,7 @@
                 pltpu.VMEM((half, 3, B, B), BF),
                 pltpu.VMEM((early, B, B), BF),
                 pltpu.SemaphoreType.DMA((early,)),
-                pltpu.SemaphoreType.DMA((len(parts) + 1,)),
+                pltpu.SemaphoreType.DMA((len(parts),)),
                 pltpu.VMEM((2 * half, B), F32),
                 pltpu.VMEM((4 * ranks, B), F32),
             ],
@@ -620,20 +611,20 @@
     )
     low, high = neighbours(x_low)
     table = gather_line(x_low)
-    table = leave(8, 12, table)
+    table = leave(8, 13, table)
     own = even_blocks(recv_places, prolong, a_diag, a_pair)
     even, mail = residual_pieces(
         slots, sends, rhs, x, table, low, high, a_diag, a_pair, a_far, prolong
     )
     mail = exchange(mail)
-    mail = leave(12, 15, mail)
-    late = 3 * capacity
+    mail = leave(13, 15, mail)
+    late = 2 * capacity
     early = half - late
     blocks, kept, restricted, reply, lift = coarse_early(
-        items, recvs, recv_starts, capacity, early, arrived[:12], mail, even, own
+        items, recvs, recv_starts, capacity, early, arrived[:13], mail, even, own
     )
     blocks, restricted, reply, lift = coarse_late(
-        items, recvs, recv_starts, capacity, early, 12, arrived[12:], mail, even, own, restricted, reply, lift, blocks, kept
+        items, recvs, recv_starts, capacity, early, 13, arrived[13:], mail, even, own, restricted, reply, lift, blocks, kept
     )
     fine = finish(sends, exchange(reply), lift, x, prolong)
     return fine, blocks, restricted

time: 224 us -> 225 us (level)
  waiting for transfers between devices: 69.1 us -> 56.8 us
  starting transfers between devices: 48.1 us -> 56.7 us
  blocking collectives: 27.8 us -> 31.4 us
    ppermute x15, waiting for transfers between devices: 12 us -> 0.04 us  [leave(): arrived.append(lax.ppermute(part, 'rx', along(grid_side, dx, dy)))]
    ppermute x15, starting transfers between devices: 34 us -> 39.6 us  [leave(): arrived.append(lax.ppermute(part, 'rx', along(grid_side, dx, dy)))]
    all_to_all x1, blocking collectives: 12.2 us -> 15.6 us  [exchange(): lax.all_to_all(packed.reshape((line, -1) + shape[1:]), 'rx', split_axis=0...]
    all_to_all x1, starting transfers between devices: 5.07 us -> 8.38 us  [exchange(): lax.all_to_all(packed.reshape((line, -1) + shape[1:]), 'rx', split_axis=0...]
  transfers between devices with their start and end apart: 21 -> 21, of which waited for: 7 -> 5; matrix products, arithmetic and copies ran while one was open for 1% -> 1% of each run, Pallas kernels for 22% -> 23%
where the time goes in v4:
time: 225 us; the launch traced here: 223 us
  Pallas kernels  66 us (29%)
  waiting for transfers between devices  56.8 us (25%)
  starting transfers between devices  56.7 us (25%)
  blocking collectives  31.4 us (14%)
  local copies, waits for them, and re-layouts  7.11 us (3%)
  other arithmetic  3.55 us (2%)
    ppermute x15, starting transfers between devices, leave(): arrived.append(lax.ppermute(part, 'rx', along(grid_side, dx, dy)))  39.6 us
    all_to_all x1, waiting for transfers between devices, gather_line(): lax.all_to_all(copies, 'rx', split_axis=0, concat_axis=0, tiled=True)  28.9 us
    all_to_all x1, waiting for transfers between devices, exchange(): lax.all_to_all(packed.reshape((line, -1) + shape[1:]), 'rx', split_axis=0...  19 us
    all_to_all x1, blocking collectives, gather_line(): lax.all_to_all(copies, 'rx', split_axis=0, concat_axis=0, tiled=True)  15.7 us
    all_to_all x1, blocking collectives, exchange(): lax.all_to_all(packed.reshape((line, -1) + shape[1:]), 'rx', split_axis=0...  15.6 us
    pallas_call x1, Pallas kernels, residual_pieces(): pl.pallas_call(functools.partial(residual_kernel, group, rows), out_shape...  14.7 us
    pallas_call x1, Pallas kernels, second_sweep(): pl.pallas_call(functools.partial(sweep_kernel, group, rows), out_shape=(j...  14.4 us
    pallas_call x1, Pallas kernels, coarse_early(): pl.pallas_call(functools.partial(early_kernel, ranks, early), out_shape=(...  11 us
  transfers between devices with their start and end apart: 21, of which 5 were waited for; matrix products, arithmetic and copies ran while one was open for 1% of the time, Pallas kernels for 23%

profile of v4, /device:TPU:0, one launch (start us, length us, event | category | flops | bytes accessed | tf_op | source)
XLA Modules:
  0.0 222.6 jit_solution(16673121646708113682)
XLA Ops:
  3.5 8.1 %odd_blocks.1 = (bf16[8,3,128,128]{3,2,1,0:T(8,128)(2,1)}, bf16[8,3,128,128]{3,2,1,0:T(8,128)(2,1)}, bf16[8,3,128,128]{3,2,1,0:T(8,128)(2,1)}, bf16[8,3,128,128]...) custom-call(s32[64]{0:T(128)S(1)} %convert_reduce_fusion.places, ...), custom_call_target="tpu_custom_call" | custom-call | tf_op jit(solution)/shard_map/odd_blocks/pallas_call | solution.py:237
  14.3 3.1 %collective-permute-start.1 = (bf16[8,3,128,128]{3,2,1,0:T(8,128)(2,1)}, bf16[8,3,128,128]{3,2,1,0:T(8,128)(2,1)S(1)}, u32[]{:S(2)}, u32[]{:S(2)}) collective-permute-start(bf16[8,3,128,128]{3,2,1,0:T(8,128)(2,1)} %get-tuple-element.80), channel_id=1, source_target_pairs={{0,120},{8,96},{16,104},{24,112},{32,24},{40,0},{48,8},{56,16},{64... | collective-permute-start | bytes 2359304 | tf_op jit(solution)/shard_map/ppermute | solution.py:601
  21.6 2.7 %first_sweep.1 = (f32[128,128]{1,0:T(8,128)S(1)}, bf16[128,128]{1,0:T(8,128)(2,1)S(1)}) custom-call(f32[128,128]{1,0:T(8,128)S(1)} %copy-done.12, bf16[128,128,128]{2,1,0:T(8,128)(2,1)S(1)} %copy-done.4), custom_call_target="tpu_custom_call" | custom-call | tf_op jit(solution)/shard_map/first_sweep/pallas_call | solution.py:68
  25.2 4.5 %all-to-all-start = ((bf16[16,128,128]{2,1,0:T(8,128)(2,1)}), bf16[16,128,128]{2,1,0:T(8,128)(2,1)S(1)}, u32[]{:S(2)}, u32[]{:S(2)}) async-start(bf16[16,128,128]{2,1,0:T(8,128)(2,1)} %broadcast_in_dim.83), calls=%async_computation | async-start | bytes 1048576 | tf_op jit(solution)/shard_map/all_to_all | solution.py:521
  31.8 28.9 %all-to-all-done = bf16[16,128,128]{2,1,0:T(8,128)(2,1)S(1)} async-done(((bf16[16,128,128]{2,1,0:T(8,128)(2,1)}), bf16[16,128,128]{2,1,0:T(8,128)(2,1)S(1)}, u32[]{:S(2)}, u32[]{:S(2)}) %all-to-all-start) | async-done | bytes 524320 | tf_op jit(solution)/shard_map/all_to_all | solution.py:521
  62.2 4.2 %collective-permute-start.5 = (bf16[8,3,128,128]{3,2,1,0:T(8,128)(2,1)}, bf16[8,3,128,128]{3,2,1,0:T(8,128)(2,1)S(1)}, u32[]{:S(2)}, u32[]{:S(2)}) collective-permute-start(bf16[8,3,128,128]{3,2,1,0:T(8,128)(2,1)} %copy-done.14), channel_id=1, source_target_pairs={{0,88},{8,64},{16,72},{24,80},{32,120},{40,96},{48,104},{56,112},{... | collective-permute-start | bytes 2359304 | tf_op jit(solution)/shard_map/ppermute | solution.py:601
  66.4 3.2 %collective-permute-start.7 = (bf16[8,3,128,128]{3,2,1,0:T(8,128)(2,1)}, bf16[8,3,128,128]{3,2,1,0:T(8,128)(2,1)S(1)}, u32[]{:S(2)}, u32[]{:S(2)}) collective-permute-start(bf16[8,3,128,128]{3,2,1,0:T(8,128)(2,1)} %get-tuple-element.88), channel_id=1, source_target_pairs={{0,24},{8,0},{16,8},{24,16},{32,56},{40,32},{48,40},{56,48},{64,88... | collective-permute-start | bytes 2359304 | tf_op jit(solution)/shard_map/ppermute | solution.py:601
  69.7 4.5 %collective-permute-done.8.low = bf16[128,128]{1,0:T(8,128)(2,1)S(1)} collective-permute-done((bf16[128,128]{1,0:T(8,128)(2,1)S(1)}, bf16[128,128]{1,0:T(8,128)(2,1)S(1)}, u32[]{:S(2)}, u32[]{:S(2)}) %collective-permute-start.8) | collective-permute-done | bytes 32800 | tf_op jit(solution)/shard_map/ppermute | solution.py:529
  76.4 14.4 %second_sweep.1 = (f32[128,128]{1,0:T(8,128)S(1)}, bf16[128,128]{1,0:T(8,128)(2,1)S(1)}) custom-call(s32[384]{0:T(512)S(1)} %pad_add_fusion.slots, f32[128,128]{1,0:T(8,128)S(1)} %copy-done.12, f32[128,128]{1,0:T(8,128)S(1)} %get-tuple-element.89.x_group, bf16[2048,128]{1,0:T(8,128)(2,1)S(1)} %bitcast.43, bf16[128,128]{1,0:T(8,128)(2,1)S(1)} %collective-permute-done.8.low, ...), custom_call_target="tpu_custom_call" | custom-call | tf_op jit(solution)/shard_map/second_sweep/pallas_call | solution.py:163
  91.0 15.7 %all_to_all.20 = bf16[16,128,128]{2,1,0:T(8,128)(2,1)S(1)} all-to-all(bf16[16,128,128]{2,1,0:T(8,128)(2,1)S(1)} %broadcast_in_dim.84), channel_id=1, replica_groups=mesh['rx'=16,'ry'=8] {'rx'}, dimensions={0} | all-to-all | bytes 1048576 | tf_op jit(solution)/shard_map/all_to_all | solution.py:521
  106.8 3.8 %collective-permute-start.10 = (bf16[8,3,128,128]{3,2,1,0:T(8,128)(2,1)}, bf16[8,3,128,128]{3,2,1,0:T(8,128)(2,1)S(1)}, u32[]{:S(2)}, u32[]{:S(2)}) collective-permute-start(bf16[8,3,128,128]{3,2,1,0:T(8,128)(2,1)} %get-tuple-element.92), channel_id=1, source_target_pairs={{0,112},{8,120},{16,96},{24,104},{32,16},{40,24},{48,0},{56,8},{64... | collective-permute-start | bytes 2359304 | tf_op jit(solution)/shard_map/ppermute | solution.py:601
  110.9 2.9 %collective-permute-start.12 = (bf16[8,3,128,128]{3,2,1,0:T(8,128)(2,1)}, bf16[8,3,128,128]{3,2,1,0:T(8,128)(2,1)}, u32[]{:S(2)}, u32[]{:S(2)}) collective-permute-start(bf16[8,3,128,128]{3,2,1,0:T(8,128)(2,1)} %get-tuple-element.94), channel_id=1, source_target_pairs={{0,96},{8,104},{16,112},{24,120},{32,0},{40,8},{48,16},{56,24},{64... | collective-permute-start | bytes 2359304 | tf_op jit(solution)/shard_map/ppermute | solution.py:601
  118.0 2.8 %collective-permute-done.14.low = bf16[128,128]{1,0:T(8,128)(2,1)S(1)} collective-permute-done((bf16[128,128]{1,0:T(8,128)(2,1)S(1)}, bf16[128,128]{1,0:T(8,128)(2,1)S(1)}, u32[]{:S(2)}, u32[]{:S(2)}) %collective-permute-start.14) | collective-permute-done | bytes 32800 | tf_op jit(solution)/shard_map/ppermute | solution.py:529
  120.7 14.7 %residual_pieces.1 = (f32[64,128]{1,0:T(8,128)S(1)}, bf16[128,128]{1,0:T(8,128)(2,1)}) custom-call(s32[384]{0:T(512)S(1)} %pad_add_fusion.slots, s32[64]{0:T(128)S(1)} %get-tuple-element.135.sends, f32[128,128]{1,0:T(8,128)S(1)} %copy-done.12, f32[128,128]{1,0:T(8,128)S(1)} %get-tuple-element.96.x_group.x, bf16[2048,128]{1,0:T(8,128)(2,1)S(1)} %bitcast.44, ...), custom_call_target="tpu_custom_call" | custom-call | tf_op jit(solution)/shard_map/residual_pieces/pallas_call | solution.py:183
  135.4 8.4 %all-to-all-start.2 = ((bf16[16,8,128]{2,1,0:T(8,128)(2,1)}), bf16[16,8,128]{2,1,0:T(8,128)(2,1)S(1)}, u32[]{:S(2)}, u32[]{:S(2)}) async-start(bf16[16,8,128]{2,1,0:T(8,128)(2,1)} %bitcast.9), calls=%async_computation.2 | async-start | bytes 65536 | tf_op jit(solution)/shard_map/all_to_all | solution.py:535
  144.0 4.4 %collective-permute-start.16 = (bf16[8,3,128,128]{3,2,1,0:T(8,128)(2,1)}, bf16[8,3,128,128]{3,2,1,0:T(8,128)(2,1)}, u32[]{:S(2)}, u32[]{:S(2)}) collective-permute-start(bf16[8,3,128,128]{3,2,1,0:T(8,128)(2,1)} %get-tuple-element.109), channel_id=1, source_target_pairs={{0,48},{8,56},{16,32},{24,40},{32,80},{40,88},{48,64},{56,72},{64,... | collective-permute-start | bytes 2359304 | tf_op jit(solution)/shard_map/ppermute | solution.py:601
  148.4 19.0 %all-to-all-done.2 = bf16[16,8,128]{2,1,0:T(8,128)(2,1)S(1)} async-done(((bf16[16,8,128]{2,1,0:T(8,128)(2,1)}), bf16[16,8,128]{2,1,0:T(8,128)(2,1)S(1)}, u32[]{:S(2)}, u32[]{:S(2)}) %all-to-all-start.2) | async-done | bytes 32800 | tf_op jit(solution)/shard_map/all_to_all | solution.py:535
  167.4 3.8 %collective-permute-start.17 = (bf16[8,3,128,128]{3,2,1,0:T(8,128)(2,1)}, bf16[8,3,128,128]{3,2,1,0:T(8,128)(2,1)S(1)}, u32[]{:S(2)}, u32[]{:S(2)}) collective-permute-start(bf16[8,3,128,128]{3,2,1,0:T(8,128)(2,1)} %get-tuple-element.119), channel_id=1, source_target_pairs={{0,64},{8,72},{16,80},{24,88},{32,96},{40,104},{48,112},{56,120},{... | collective-permute-start | bytes 2359304 | tf_op jit(solution)/shard_map/ppermute | solution.py:601
  171.1 5.5 %collective-permute-start.18 = (bf16[8,3,128,128]{3,2,1,0:T(8,128)(2,1)}, bf16[8,3,128,128]{3,2,1,0:T(8,128)(2,1)S(1)}, u32[]{:S(2)}, u32[]{:S(2)}) collective-permute-start(bf16[8,3,128,128]{3,2,1,0:T(8,128)(2,1)} %get-tuple-element.120), channel_id=1, source_target_pairs={{0,16},{8,24},{16,0},{24,8},{32,48},{40,56},{48,32},{56,40},{64,80... | collective-permute-start | bytes 2359304 | tf_op jit(solution)/shard_map/ppermute | solution.py:601
  179.0 7.4 %even_blocks.1.own = bf16[64,128,384]{2,1,0:T(8,128)(2,1)} custom-call(s32[64]{0:T(128)S(1)} %convert_reduce_fusion.1.places, bf16[64,2,128,128]{3,2,1,0:T(8,128)(2,1)S(1)} %bitcast.39, bf16[64,2,128,128]{3,2,1,0:T(8,128)(2,1)} %bitcast.42, bf16[64,2,128,128]{3,2,1,0:T(8,128)(2,1)} %bitcast.50), custom_call_target="tpu_custom_call" | custom-call | tf_op jit(solution)/shard_map/even_blocks/pallas_call | solution.py:271
  186.8 11.0 %coarse_early.1 = (bf16[64,128,128]{2,1,0:T(8,128)(2,1)}, bf16[16,3,128,128]{3,2,1,0:T(8,128)(2,1)}, f32[64,128]{1,0:T(8,128)S(1)}, f32[128,128]{1,0:T(8,128)S(1)}, f32[64,128]{1,0:T(8,128)S(1)}) custom-call(s32[64]{0:T(128)S(1)} %select_reduce_fusion.items, s32[64]{0:T(128)S(1)} %get-tuple-element.136.recvs, s32[15]{0:T(128)S(1)} %broadcast_select_fusion.1.starts, ...), custom_call_target="tpu_custom_call" | custom-call | tf_op jit(solution)/shard_map/coarse_early/pallas_call | solution.py:393
  199.3 5.0 %coarse_late.1 = (bf16[64,128,128]{2,1,0:T(8,128)(2,1)}, f32[64,128]{1,0:T(8,128)}, bf16[128,128]{1,0:T(8,128)(2,1)S(1)}, f32[64,128]{1,0:T(8,128)S(1)}) custom-call(s32[64]{0:T(128)S(1)} %select_reduce_fusion.items, s32[64]{0:T(128)S(1)} %get-tuple-element.136.recvs, s32[15]{0:T(128)S(1)} %broadcast_select_fusion.1.starts, ...), custom_call_target="tpu_custom_call", output_to_operand_aliasing={{0}: (9, {})} | custom-call | tf_op jit(solution)/shard_map/coarse_late/pallas_call | solution.py:436
  204.3 15.6 %all_to_all.21 = bf16[16,8,128]{2,1,0:T(8,128)(2,1)S(1)} all-to-all(bf16[16,8,128]{2,1,0:T(8,128)(2,1)S(1)} %bitcast.48), channel_id=1, replica_groups=mesh['rx'=16,'ry'=8] {'rx'}, dimensions={0} | all-to-all | bytes 65536 | tf_op jit(solution)/shard_map/all_to_all | solution.py:535
  219.9 2.7 %finish.1 = f32[128,128]{1,0:T(8,128)} custom-call(s32[64]{0:T(128)S(1)} %get-tuple-element.135.sends, bf16[128,128]{1,0:T(8,128)(2,1)S(1)} %bitcast.47, f32[64,128]{1,0:T(8,128)S(1)} %get-tuple-element.122.lift, f32[128,128]{1,0:T(8,128)S(1)} %get-tuple-element.96.x_group.x, bf16[64,2,128,128]{3,2,1,0:T(8,128)(2,1)S(1)} %bitcast.40), custom_call_target="tpu_custom_call" | custom-call | tf_op jit(solution)/shard_map/finish/pallas_call | solution.py:490
  (91 shorter events, 25.1 us)
Async XLA Ops:
  11.7 49.0 %collective-permute-start = (bf16[8,3,128,128]{3,2,1,0:T(8,128)(2,1)}, bf16[8,3,128,128]{3,2,1,0:T(8,128)(2,1)S(1)}, u32[]{:S(2)}, u32[]{:S(2)}) collective-permute-start(bf16[8,3,128,128]{3,2,1,0:T(8,128)(2,1)} %get-tuple-element.79), channel_id=1, source_target_pairs={{0,40},{8,48},{16,56},{24,32},{32,72},{40,80},{48,88},{56,64},{64,... | collective-permute-start | bytes 2359304 | tf_op jit(solution)/shard_map/ppermute | solution.py:601
  14.3 46.3 %collective-permute-start.1 = (bf16[8,3,128,128]{3,2,1,0:T(8,128)(2,1)}, bf16[8,3,128,128]{3,2,1,0:T(8,128)(2,1)S(1)}, u32[]{:S(2)}, u32[]{:S(2)}) collective-permute-start(bf16[8,3,128,128]{3,2,1,0:T(8,128)(2,1)} %get-tuple-element.80), channel_id=1, source_target_pairs={{0,120},{8,96},{16,104},{24,112},{32,24},{40,0},{48,8},{56,16},{64... | collective-permute-start | bytes 2359304 | tf_op jit(solution)/shard_map/ppermute | solution.py:601
  17.5 43.2 %collective-permute-start.2 = (bf16[8,3,128,128]{3,2,1,0:T(8,128)(2,1)}, bf16[8,3,128,128]{3,2,1,0:T(8,128)(2,1)S(1)}, u32[]{:S(2)}, u32[]{:S(2)}) collective-permute-start(bf16[8,3,128,128]{3,2,1,0:T(8,128)(2,1)} %get-tuple-element.81), channel_id=1, source_target_pairs={{0,56},{8,32},{16,40},{24,48},{32,88},{40,64},{48,72},{56,80},{64,... | collective-permute-start | bytes 2359304 | tf_op jit(solution)/shard_map/ppermute | solution.py:601
  19.1 41.6 %collective-permute-start.3 = (bf16[8,3,128,128]{3,2,1,0:T(8,128)(2,1)}, bf16[8,3,128,128]{3,2,1,0:T(8,128)(2,1)}, u32[]{:S(2)}, u32[]{:S(2)}) collective-permute-start(bf16[8,3,128,128]{3,2,1,0:T(8,128)(2,1)} %get-tuple-element.82), channel_id=1, source_target_pairs={{0,104},{8,112},{16,120},{24,96},{32,8},{40,16},{48,24},{56,0},{64... | collective-permute-start | bytes 2359304 | tf_op jit(solution)/shard_map/ppermute | solution.py:601
  25.2 35.5 %all-to-all-start = ((bf16[16,128,128]{2,1,0:T(8,128)(2,1)}), bf16[16,128,128]{2,1,0:T(8,128)(2,1)S(1)}, u32[]{:S(2)}, u32[]{:S(2)}) async-start(bf16[16,128,128]{2,1,0:T(8,128)(2,1)} %broadcast_in_dim.83), calls=%async_computation | async-start | bytes 1048576 | tf_op jit(solution)/shard_map/all_to_all | solution.py:521
  29.7 39.9 %collective-permute-start.9 = (bf16[128,128]{1,0:T(8,128)(2,1)S(1)}, bf16[128,128]{1,0:T(8,128)(2,1)S(1)}, u32[]{:S(2)}, u32[]{:S(2)}) collective-permute-start(bf16[128,128]{1,0:T(8,128)(2,1)S(1)} %get-tuple-element.84), channel_id=1, source_target_pairs={{1,0},{2,1},{3,2},{4,3},{5,4},{6,5},{7,6},{0,7},{9,8},{10,9},{11,1... | collective-permute-start | bytes 98312 | tf_op jit(solution)/shard_map/ppermute | solution.py:529
  60.7 46.0 %collective-permute-start.4 = (bf16[8,3,128,128]{3,2,1,0:T(8,128)(2,1)}, bf16[8,3,128,128]{3,2,1,0:T(8,128)(2,1)S(1)}, u32[]{:S(2)}, u32[]{:S(2)}) collective-permute-start(bf16[8,3,128,128]{3,2,1,0:T(8,128)(2,1)} %copy-done.15), channel_id=1, source_target_pairs={{0,72},{8,80},{16,88},{24,64},{32,104},{40,112},{48,120},{56,96},{... | collective-permute-start | bytes 2359304 | tf_op jit(solution)/shard_map/ppermute | solution.py:601
  62.2 44.6 %collective-permute-start.5 = (bf16[8,3,128,128]{3,2,1,0:T(8,128)(2,1)}, bf16[8,3,128,128]{3,2,1,0:T(8,128)(2,1)S(1)}, u32[]{:S(2)}, u32[]{:S(2)}) collective-permute-start(bf16[8,3,128,128]{3,2,1,0:T(8,128)(2,1)} %copy-done.14), channel_id=1, source_target_pairs={{0,88},{8,64},{16,72},{24,80},{32,120},{40,96},{48,104},{56,112},{... | collective-permute-start | bytes 2359304 | tf_op jit(solution)/shard_map/ppermute | solution.py:601
  66.4 40.3 %collective-permute-start.6 = (bf16[8,3,128,128]{3,2,1,0:T(8,128)(2,1)}, bf16[8,3,128,128]{3,2,1,0:T(8,128)(2,1)S(1)}, u32[]{:S(2)}, u32[]{:S(2)}) collective-permute-start(bf16[8,3,128,128]{3,2,1,0:T(8,128)(2,1)} %copy-done.13), channel_id=1, source_target_pairs={{0,8},{8,16},{16,24},{24,0},{32,40},{40,48},{48,56},{56,32},{64,72... | collective-permute-start | bytes 2359304 | tf_op jit(solution)/shard_map/ppermute | solution.py:601
  66.4 40.4 %collective-permute-start.7 = (bf16[8,3,128,128]{3,2,1,0:T(8,128)(2,1)}, bf16[8,3,128,128]{3,2,1,0:T(8,128)(2,1)S(1)}, u32[]{:S(2)}, u32[]{:S(2)}) collective-permute-start(bf16[8,3,128,128]{3,2,1,0:T(8,128)(2,1)} %get-tuple-element.88), channel_id=1, source_target_pairs={{0,24},{8,0},{16,8},{24,16},{32,56},{40,32},{48,40},{56,48},{64,88... | collective-permute-start | bytes 2359304 | tf_op jit(solution)/shard_map/ppermute | solution.py:601
  69.7 4.6 %collective-permute-start.8 = (bf16[128,128]{1,0:T(8,128)(2,1)S(1)}, bf16[128,128]{1,0:T(8,128)(2,1)S(1)}, u32[]{:S(2)}, u32[]{:S(2)}) collective-permute-start(bf16[128,128]{1,0:T(8,128)(2,1)S(1)} %get-tuple-element.84), channel_id=1, source_target_pairs={{0,1},{1,2},{2,3},{3,4},{4,5},{5,6},{6,7},{7,0},{8,9},{9,10},{10,1... | collective-permute-start | bytes 98312 | tf_op jit(solution)/shard_map/ppermute | solution.py:529
  76.4 44.3 %copy-start.3 = (bf16[128,128,128]{2,1,0:T(8,128)(2,1)S(1)}, bf16[128,128,128]{2,1,0:T(8,128)(2,1)}, u32[]{:S(2)}) copy-start(bf16[128,128,128]{2,1,0:T(8,128)(2,1)} %diag.3) | copy-start | bytes 12582916
  106.7 28.6 %copy-start.6 = (bf16[8,3,128,128]{3,2,1,0:T(8,128)(2,1)}, bf16[8,3,128,128]{3,2,1,0:T(8,128)(2,1)S(1)}, u32[]{:S(2)}) copy-start(bf16[8,3,128,128]{3,2,1,0:T(8,128)(2,1)S(1)} %collective-permute-done.4.rest_4_) | copy-start | bytes 2359300
  106.7 28.6 %copy-start.8 = (bf16[8,3,128,128]{3,2,1,0:T(8,128)(2,1)}, bf16[8,3,128,128]{3,2,1,0:T(8,128)(2,1)S(1)}, u32[]{:S(2)}) copy-start(bf16[8,3,128,128]{3,2,1,0:T(8,128)(2,1)S(1)} %collective-permute-done.5.rest_5_) | copy-start | bytes 2359300
  106.8 60.5 %collective-permute-start.10 = (bf16[8,3,128,128]{3,2,1,0:T(8,128)(2,1)}, bf16[8,3,128,128]{3,2,1,0:T(8,128)(2,1)S(1)}, u32[]{:S(2)}, u32[]{:S(2)}) collective-permute-start(bf16[8,3,128,128]{3,2,1,0:T(8,128)(2,1)} %get-tuple-element.92), channel_id=1, source_target_pairs={{0,112},{8,120},{16,96},{24,104},{32,16},{40,24},{48,0},{56,8},{64... | collective-permute-start | bytes 2359304 | tf_op jit(solution)/shard_map/ppermute | solution.py:601
  110.6 56.8 %collective-permute-start.11 = (bf16[8,3,128,128]{3,2,1,0:T(8,128)(2,1)}, bf16[8,3,128,128]{3,2,1,0:T(8,128)(2,1)}, u32[]{:S(2)}, u32[]{:S(2)}) collective-permute-start(bf16[8,3,128,128]{3,2,1,0:T(8,128)(2,1)} %get-tuple-element.93), channel_id=1, source_target_pairs={{0,32},{8,40},{16,48},{24,56},{32,64},{40,72},{48,80},{56,88},{64,... | collective-permute-start | bytes 2359304 | tf_op jit(solution)/shard_map/ppermute | solution.py:601
  110.9 56.5 %collective-permute-start.12 = (bf16[8,3,128,128]{3,2,1,0:T(8,128)(2,1)}, bf16[8,3,128,128]{3,2,1,0:T(8,128)(2,1)}, u32[]{:S(2)}, u32[]{:S(2)}) collective-permute-start(bf16[8,3,128,128]{3,2,1,0:T(8,128)(2,1)} %get-tuple-element.94), channel_id=1, source_target_pairs={{0,96},{8,104},{16,112},{24,120},{32,0},{40,8},{48,16},{56,24},{64... | collective-permute-start | bytes 2359304 | tf_op jit(solution)/shard_map/ppermute | solution.py:601
  113.8 53.5 %collective-permute-start.13 = (bf16[8,3,128,128]{3,2,1,0:T(8,128)(2,1)}, bf16[8,3,128,128]{3,2,1,0:T(8,128)(2,1)}, u32[]{:S(2)}, u32[]{:S(2)}) collective-permute-start(bf16[8,3,128,128]{3,2,1,0:T(8,128)(2,1)} %get-tuple-element.95), channel_id=1, source_target_pairs={{0,80},{8,88},{16,64},{24,72},{32,112},{40,120},{48,96},{56,104},{... | collective-permute-start | bytes 2359304 | tf_op jit(solution)/shard_map/ppermute | solution.py:601
  113.8 1.9 collective-permute-start.15
  115.8 4.9 %collective-permute-start.14 = (bf16[128,128]{1,0:T(8,128)(2,1)S(1)}, bf16[128,128]{1,0:T(8,128)(2,1)S(1)}, u32[]{:S(2)}, u32[]{:S(2)}) collective-permute-start(bf16[128,128]{1,0:T(8,128)(2,1)S(1)} %get-tuple-element.91), channel_id=1, source_target_pairs={{0,1},{1,2},{2,3},{3,4},{4,5},{5,6},{6,7},{7,0},{8,9},{9,10},{10,1... | collective-permute-start | bytes 98312 | tf_op jit(solution)/shard_map/ppermute | solution.py:529
  135.4 31.9 %all-to-all-start.2 = ((bf16[16,8,128]{2,1,0:T(8,128)(2,1)}), bf16[16,8,128]{2,1,0:T(8,128)(2,1)S(1)}, u32[]{:S(2)}, u32[]{:S(2)}) async-start(bf16[16,8,128]{2,1,0:T(8,128)(2,1)} %bitcast.9), calls=%async_computation.2 | async-start | bytes 65536 | tf_op jit(solution)/shard_map/all_to_all | solution.py:535
  144.0 42.8 %collective-permute-start.16 = (bf16[8,3,128,128]{3,2,1,0:T(8,128)(2,1)}, bf16[8,3,128,128]{3,2,1,0:T(8,128)(2,1)}, u32[]{:S(2)}, u32[]{:S(2)}) collective-permute-start(bf16[8,3,128,128]{3,2,1,0:T(8,128)(2,1)} %get-tuple-element.109), channel_id=1, source_target_pairs={{0,48},{8,56},{16,32},{24,40},{32,80},{40,88},{48,64},{56,72},{64,... | collective-permute-start | bytes 2359304 | tf_op jit(solution)/shard_map/ppermute | solution.py:601
  167.4 30.5 %collective-permute-start.17 = (bf16[8,3,128,128]{3,2,1,0:T(8,128)(2,1)}, bf16[8,3,128,128]{3,2,1,0:T(8,128)(2,1)S(1)}, u32[]{:S(2)}, u32[]{:S(2)}) collective-permute-start(bf16[8,3,128,128]{3,2,1,0:T(8,128)(2,1)} %get-tuple-element.119), channel_id=1, source_target_pairs={{0,64},{8,72},{16,80},{24,88},{32,96},{40,104},{48,112},{56,120},{... | collective-permute-start | bytes 2359304 | tf_op jit(solution)/shard_map/ppermute | solution.py:601
  171.1 26.7 %collective-permute-start.18 = (bf16[8,3,128,128]{3,2,1,0:T(8,128)(2,1)}, bf16[8,3,128,128]{3,2,1,0:T(8,128)(2,1)S(1)}, u32[]{:S(2)}, u32[]{:S(2)}) collective-permute-start(bf16[8,3,128,128]{3,2,1,0:T(8,128)(2,1)} %get-tuple-element.120), channel_id=1, source_target_pairs={{0,16},{8,24},{16,0},{24,8},{32,48},{40,56},{48,32},{56,40},{64,80... | collective-permute-start | bytes 2359304 | tf_op jit(solution)/shard_map/ppermute | solution.py:601
  (17 other events, 240.1 us)
